TPU v7x, 16 devices: a whole 2x2x2 slice. The times are simulated.
16 devices in a mesh: data: 16 (over z, y, x, core).
Axes of the slice: x: 2, y: 2, z: 2, core: 2. Of those that a mesh axis runs over, the one named last changes fastest.
Arguments:
- x_init: bfloat16 [128, 128, 1280], P('data')
- cot_out: bfloat16 [128, 128, 1280], P('data')
- w_query: bfloat16 [2, 1280, 1280], replicated
- w_key: bfloat16 [2, 1280, 1280], replicated
- w_value: bfloat16 [2, 1280, 1280], replicated
- w_proj: bfloat16 [2, 1280, 1280], replicated
- w_up: bfloat16 [1280, 5120], replicated
- w_down: bfloat16 [5120, 1280], replicated
Outputs:
- output 1: float32 [2, 1280, 1280], replicated
- output 2: float32 [2, 1280, 1280], replicated
- output 3: float32 [2, 1280, 1280], replicated
- output 4: float32 [2, 1280, 1280], replicated
- output 5: float32 [1280, 5120], replicated
- output 6: float32 [5120, 1280], replicated
- output 7: bfloat16 [128, 128, 1280], P('data')
All inputs are finite; a program needn't handle non-finite values.
Results may differ from a plain program's by a relative error of at most 0.02.
Values are sent between devices in bfloat16 or wider.
A program may use at most 1 GiB of HBM per device.

v0:
```python
import jax
import jax.numpy as jnp
from jax import lax
from jax.sharding import PartitionSpec as P

EPS = 1e-6
HEAD_DIM = 64


def rms_norm(x_f32):
    return x_f32 * lax.rsqrt(jnp.mean(x_f32 * x_f32, axis=-1, keepdims=True) + EPS)


def gelu_tanh(pre_f32):
    return jax.nn.gelu(pre_f32, approximate=True)


def product(subscripts, lhs, rhs):
    return jnp.einsum(subscripts, lhs, rhs, preferred_element_type=jnp.float32)


def layer_forward(x_act, w_query, w_key, w_value, w_proj, w_up, w_down, heads):
    batch, seq_len, width = x_act.shape
    head_dim = width // heads
    x_f32 = x_act.astype(jnp.float32)
    normed = rms_norm(x_f32).astype(jnp.bfloat16)
    query = product("bsd,de->bse", normed, w_query).astype(jnp.bfloat16).reshape(batch, seq_len, heads, head_dim)
    key_act = product("bsd,de->bse", normed, w_key).astype(jnp.bfloat16).reshape(batch, seq_len, heads, head_dim)
    value = product("bsd,de->bse", normed, w_value).astype(jnp.bfloat16).reshape(batch, seq_len, heads, head_dim)
    scores = product("bqhd,bkhd->bhqk", query, key_act) * head_dim ** -0.5
    probs = jax.nn.softmax(scores, axis=-1).astype(jnp.bfloat16)
    mixed = product("bhqk,bkhd->bqhd", probs, value).astype(jnp.bfloat16).reshape(batch, seq_len, width)
    attn_out = product("bsd,de->bse", mixed, w_proj).astype(jnp.bfloat16)
    hidden = (x_f32 + attn_out.astype(jnp.float32)).astype(jnp.bfloat16)
    normed2 = rms_norm(hidden.astype(jnp.float32)).astype(jnp.bfloat16)
    pre_act = product("bsd,df->bsf", normed2, w_up).astype(jnp.bfloat16)
    activated = gelu_tanh(pre_act.astype(jnp.float32)).astype(jnp.bfloat16)
    mlp_out = product("bsf,fd->bsd", activated, w_down).astype(jnp.bfloat16)
    x_next = (hidden.astype(jnp.float32) + mlp_out.astype(jnp.float32)).astype(jnp.bfloat16)
    kept = (x_act, normed, query, key_act, value, probs, mixed, hidden, normed2, pre_act, activated)
    return x_next, kept


def layer_backward(d_next, kept, w_query, w_key, w_value, w_proj, w_up, w_down):
    x_act, normed, query, key_act, value, probs, mixed, hidden, normed2, pre_act, activated = kept
    batch, seq_len, heads, head_dim = query.shape
    width = heads * head_dim
    g_down = product("bsf,bsd->fd", activated, d_next)
    d_activated = product("bsd,fd->bsf", d_next, w_down).astype(jnp.bfloat16)
    gelu_pull = jax.vjp(gelu_tanh, pre_act.astype(jnp.float32))[1]
    d_pre = gelu_pull(d_activated.astype(jnp.float32))[0].astype(jnp.bfloat16)
    g_up = product("bsd,bsf->df", normed2, d_pre)
    d_normed2 = product("bsf,df->bsd", d_pre, w_up).astype(jnp.bfloat16)
    hidden_pull = jax.vjp(rms_norm, hidden.astype(jnp.float32))[1]
    d_hidden = (d_next.astype(jnp.float32) + hidden_pull(d_normed2.astype(jnp.float32))[0]).astype(jnp.bfloat16)
    g_proj = product("bsd,bse->de", mixed, d_hidden)
    d_mixed = product("bse,de->bsd", d_hidden, w_proj).astype(jnp.bfloat16).reshape(batch, seq_len, heads, head_dim)
    d_probs = product("bqhd,bkhd->bhqk", d_mixed, value).astype(jnp.bfloat16).astype(jnp.float32)
    d_value = product("bhqk,bqhd->bkhd", probs, d_mixed).astype(jnp.bfloat16).reshape(batch, seq_len, width)
    probs_f32 = probs.astype(jnp.float32)
    row_dot = jnp.sum(d_probs * probs_f32, axis=-1, keepdims=True)
    d_scores = (probs_f32 * (d_probs - row_dot) * head_dim ** -0.5).astype(jnp.bfloat16)
    d_query = product("bhqk,bkhd->bqhd", d_scores, key_act).astype(jnp.bfloat16).reshape(batch, seq_len, width)
    d_key = product("bhqk,bqhd->bkhd", d_scores, query).astype(jnp.bfloat16).reshape(batch, seq_len, width)
    g_query = product("bsd,bse->de", normed, d_query)
    g_key = product("bsd,bse->de", normed, d_key)
    g_value = product("bsd,bse->de", normed, d_value)
    d_normed = (product("bse,de->bsd", d_query, w_query) + product("bse,de->bsd", d_key, w_key)
                + product("bse,de->bsd", d_value, w_value)).astype(jnp.bfloat16)
    input_pull = jax.vjp(rms_norm, x_act.astype(jnp.float32))[1]
    d_input = (d_hidden.astype(jnp.float32) + input_pull(d_normed.astype(jnp.float32))[0]).astype(jnp.bfloat16)
    return d_input, (g_query, g_key, g_value, g_proj), g_up, g_down


def solution(mesh):
    def local_step(x_init, cot_out, w_query, w_key, w_value, w_proj, w_up, w_down):
        heads = x_init.shape[-1] // HEAD_DIM
        layers = w_query.shape[0]
        x_act = x_init
        kept_all = []
        for layer in range(layers):
            x_act, kept = layer_forward(x_act, w_query[layer], w_key[layer], w_value[layer], w_proj[layer], w_up, w_down, heads)
            kept_all.append(kept)
        d_act = cot_out
        g_up = jnp.zeros(w_up.shape, jnp.float32)
        g_down = jnp.zeros(w_down.shape, jnp.float32)
        attn_grads = []
        for layer in reversed(range(layers)):
            d_act, attn_part, up_part, down_part = layer_backward(
                d_act, kept_all[layer], w_query[layer], w_key[layer], w_value[layer], w_proj[layer], w_up, w_down)
            attn_part, up_part, down_part = lax.psum((attn_part, up_part, down_part), "data")
            attn_grads.append(attn_part)
            g_up = g_up + up_part
            g_down = g_down + down_part
        attn_grads = attn_grads[::-1]
        g_query = jnp.stack([part[0] for part in attn_grads])
        g_key = jnp.stack([part[1] for part in attn_grads])
        g_value = jnp.stack([part[2] for part in attn_grads])
        g_proj = jnp.stack([part[3] for part in attn_grads])
        return g_query, g_key, g_value, g_proj, g_up, g_down, d_act

    data_spec = P("data")
    full_spec = P()
    in_specs = (data_spec, data_spec, full_spec, full_spec, full_spec, full_spec, full_spec, full_spec)
    out_specs = (full_spec, full_spec, full_spec, full_spec, full_spec, full_spec, data_spec)
    return jax.shard_map(local_step, mesh=mesh, in_specs=in_specs, out_specs=out_specs, check_vma=False)
```

profile of v0, /device:TPU:0, one launch (start us, length us, event | category | flops | bytes accessed | tf_op | source)
XLA Modules:
  0.0 1573.5 jit_solution(12908353441946530433)
XLA Ops:
  10.1 7.8 convolution_convert_fusion.7
  18.0 3.7 copy.65
  21.7 8.8 convolution_convert_fusion.8
  30.5 4.4 copy.64
  34.9 7.8 convolution_convert_fusion.9
  42.7 4.5 copy.63
  47.2 10.6 fusion.193
  57.7 5.7 divide_convert_fusion.1
  67.1 6.4 fusion.83
  74.2 21.1 %fusion.52 = bf16[8,128,5120]{2,1,0:T(8,128)(2,1)} fusion(bf16[1280,5120]{1,0:T(8,128)(2,1)} %param.14, bf16[8,128,1280]{2,1,0:T(8,128)(2,1)S(1)} %get-tuple-element.20, f32[8,128]{1,0:T(8,128)S(1)} %fusion.174), kind=kOutput, calls=%fused_computation.94 | convolution fusion | flops 13430947840 | bytes 26218496 | tf_op jit(solution)/shard_map/bsd,df->bsf/dot_general | solution.py:19
  95.4 24.4 %fusion.87 = (f32[8,128]{1,0:T(8,128)S(1)}, bf16[8,128,1280]{2,1,0:T(8,128)(2,1)S(1)}) fusion(bf16[5120,1280]{1,0:T(8,128)(2,1)} %param.15, bf16[8,128,5120]{2,1,0:T(8,128)(2,1)} %fusion.52, bf16[8,128,1280]{2,1,0:T(8,128)(2,1)S(1)} %get-tuple-element.20), kind=kOutput, calls=%fused_computation.139 | convolution fusion | flops 13484686336 | bytes 28839936 | tf_op jit(solution)/shard_map/bsf,fd->bsd/dot_general | solution.py:19
  119.9 4.9 convolution_convert_fusion.3
  124.9 5.9 convolution_convert_fusion.4
  130.8 5.2 convolution_convert_fusion.5
  136.0 4.4 copy.70
  140.4 2.5 copy.69
  143.0 3.2 copy.68
  146.2 11.5 fusion.194
  157.7 5.7 divide_convert_fusion
  167.1 6.2 fusion.76
  174.9 21.5 %fusion.55 = bf16[8,128,5120]{2,1,0:T(8,128)(2,1)} fusion(bf16[1280,5120]{1,0:T(8,128)(2,1)} %param.14, bf16[8,128,1280]{2,1,0:T(8,128)(2,1)S(1)} %get-tuple-element.26, f32[8,128]{1,0:T(8,128)S(1)} %fusion.176), kind=kOutput, calls=%fused_computation.95 | convolution fusion | flops 13430947840 | bytes 26218496 | tf_op jit(solution)/shard_map/bsd,df->bsf/dot_general | solution.py:19
  196.4 29.7 %fusion.8 = bf16[8,128,5120]{2,1,0:T(8,128)(2,1)} fusion(bf16[8,128,5120]{2,1,0:T(8,128)(2,1)} %fusion.55, bf16[8,128,1280]{2,1,0:T(8,128)(2,1)S(1)} %copy-done.23, bf16[5120,1280]{1,0:T(8,128)(2,1)} %param.15), kind=kOutput, calls=%fused_computation.22 | convolution fusion | flops 13542359040 | bytes 36700160 | tf_op jit(solution)/shard_map/bsd,fd->bsf/dot_general | solution.py:19
  226.1 21.3 %fusion.78 = (f32[8,128]{1,0:T(8,128)S(1)}, bf16[8,128,1280]{2,1,0:T(8,128)(2,1)}) fusion(bf16[8,128,1280]{2,1,0:T(8,128)(2,1)} %copy-done.25, bf16[8,128,5120]{2,1,0:T(8,128)(2,1)} %fusion.8, bf16[1280,5120]{1,0:T(8,128)(2,1)} %param.14), kind=kOutput, calls=%fused_computation.130 | convolution fusion | flops 13428325376 | bytes 28839936 | tf_op jit(solution)/shard_map/bsf,df->bsd/dot_general | solution.py:19
  247.5 3.3 fusion.69
  252.3 4.9 convolution_convert_fusion.1
  257.1 4.5 copy.73
  261.7 6.6 convolution_convert_fusion.11
  268.3 4.9 convolution_convert_fusion.13
  273.3 14.3 fusion.155
  287.6 13.7 fusion.156
  301.3 6.9 convolution_bitcast_fusion
  308.2 7.5 fusion.111
  315.7 6.4 convolution_bitcast_fusion.6
  322.2 5.4 fusion.108
  327.6 6.1 convolution_bitcast_fusion.4
  333.7 6.0 convolution_bitcast_fusion.2
  339.8 6.9 fusion.90
  346.7 2.7 fusion.71
  349.4 32.2 %fusion.11 = bf16[8,128,5120]{2,1,0:T(8,128)(2,1)} fusion(bf16[8,128,5120]{2,1,0:T(8,128)(2,1)} %fusion.52, bf16[8,128,1280]{2,1,0:T(8,128)(2,1)} %fusion.71, bf16[5120,1280]{1,0:T(8,128)(2,1)} %param.15), kind=kOutput, calls=%fused_computation.25 | convolution fusion | flops 13542359040 | bytes 36700160 | tf_op jit(solution)/shard_map/bsd,fd->bsf/dot_general | solution.py:19
  381.6 21.3 %fusion.86 = (f32[8,128]{1,0:T(8,128)S(1)}, bf16[8,128,1280]{2,1,0:T(8,128)(2,1)}) fusion(bf16[8,128,1280]{2,1,0:T(8,128)(2,1)S(1)} %copy-done.7, bf16[8,128,5120]{2,1,0:T(8,128)(2,1)} %fusion.11, bf16[1280,5120]{1,0:T(8,128)(2,1)} %param.14), kind=kOutput, calls=%fused_computation.138 | convolution fusion | flops 13428325376 | bytes 28839936 | tf_op jit(solution)/shard_map/bsf,df->bsd/dot_general | solution.py:19
  402.9 3.0 fusion.73
  407.5 6.8 convolution_convert_fusion
  414.3 4.4 copy.80
  418.7 6.6 convolution_convert_fusion.10
  425.4 5.2 convolution_convert_fusion.12
  430.6 13.5 fusion.153
  444.1 13.2 fusion.154
  457.3 6.9 convolution_bitcast_fusion.1
  464.2 22.5 %fusion.150 = f32[1280,5120,1]{1,0,2:T(8,128)} fusion(bf16[8,128,5120]{2,1,0:T(8,128)(2,1)} %fusion.8, bf16[8,128,1280]{2,1,0:T(8,128)(2,1)S(1)} %copy-done.27, f32[8,128]{1,0:T(8,128)S(1)} %copy-done.38), kind=kOutput, calls=%fused_computation.202 | convolution fusion | flops 13425704960 | bytes 39325696 | tf_op jit(solution)/shard_map/bsd,bsf->df/dot_general | solution.py:19
  486.7 25.7 %fusion.40 = f32[5120,1280,1]{1,0,2:T(8,128)} fusion(bf16[8,128,1280]{2,1,0:T(8,128)(2,1)S(1)} %copy-done.24, bf16[8,128,5120]{2,1,0:T(8,128)(2,1)} %fusion.55), kind=kOutput, calls=%fused_computation.64 | convolution fusion | flops 13474201600 | bytes 39321600 | tf_op jit(solution)/shard_map/bsf,bsd->fd/dot_general | solution.py:19
  512.5 6.1 convolution_bitcast_fusion.7
  518.6 6.2 convolution_bitcast_fusion.3
  524.8 6.0 convolution_bitcast_fusion.5
  530.8 27.7 %bitcast_add_fusion.1 = f32[1280,5120]{1,0:T(8,128)} fusion(f32[1280,5120,1]{1,0,2:T(8,128)} %fusion.150, bf16[8,128,5120]{2,1,0:T(8,128)(2,1)} %fusion.11, bf16[8,128,1280]{2,1,0:T(8,128)(2,1)S(1)} %copy-done.8, f32[8,128]{1,0:T(8,128)S(1)} %copy-done.32), kind=kOutput, calls=%fused_computation.17 | convolution fusion | flops 13432258560 | bytes 65540096 | tf_op jit(solution)/shard_map/bsd,bsf->df/dot_general | solution.py:19
  558.6 29.5 %bitcast_add_fusion = f32[5120,1280]{1,0:T(8,128)} fusion(f32[5120,1280,1]{1,0,2:T(8,128)} %fusion.40, bf16[8,128,1280]{2,1,0:T(8,128)(2,1)} %fusion.71, bf16[8,128,5120]{2,1,0:T(8,128)(2,1)} %fusion.52), kind=kOutput, calls=%fused_computation.16 | convolution fusion | flops 13480755200 | bytes 65536000 | tf_op jit(solution)/shard_map/bsf,bsd->fd/dot_general | solution.py:19
  588.1 8.8 fusion.120
  597.0 7.5 fusion.123
  604.5 7.3 fusion.82
  611.8 2.7 fusion.75
  614.5 883.8 %all-reduce.3.cloned.1.call-done = (f32[1,1280,1280]{2,1,0:T(8,128)}, f32[1,1280,1280]{2,1,0:T(8,128)}, f32[1,1280,1280]{2,1,0:T(8,128)}, f32[1,1280,1280]{2,1,0...) async-done(((f32[1,1280,1280]{2,1,0:T(8,128)}, ...) | async-done | bytes 104857616 | tf_op jit(solution)/shard_map/psum | solution.py:91
  1498.3 18.5 %pad_maximum_fusion = (f32[2,1280,1280]{2,1,0:T(8,128)}, f32[2,1280,1280]{2,1,0:T(8,128)}) fusion(f32[1,1280,1280]{2,1,0:T(8,128)} %get-tuple-element.7, f32[1,1280,1280]{2,1,0:T(8,128)} %get-tuple-element.8, f32[1,1280,1280]{2,1,0:T(8,128)} %get-tuple-element.9, f32[1,1280,1280]{2,1,0:T(8,128)} %get-tuple-element.10), kind=kLoop, calls=%fused_computation.40 | loop fusion | flops 6553600 | bytes 52428800 | tf_op jit(solution)/shard_map/stack | solution.py:96
  1517.6 18.2 %pad_maximum_fusion.2 = (f32[2,1280,1280]{2,1,0:T(8,128)}, f32[2,1280,1280]{2,1,0:T(8,128)}) fusion(f32[1,1280,1280]{2,1,0:T(8,128)S(1)} %copy-done.19, f32[1,1280,1280]{2,1,0:T(8,128)} %get-tuple-element.12, f32[1,1280,1280]{2,1,0:T(8,128)} %get-tuple-element.13, f32[1,1280,1280]{2,1,0:T(8,128)} %get-tuple-element.14), kind=kLoop, calls=%fused_computation.42 | loop fusion | flops 6553600 | bytes 52428800 | tf_op jit(solution)/shard_map/stack | solution.py:98
  1535.8 20.6 %copy.145 = f32[1280,5120]{1,0:T(8,128)} copy(f32[1280,5120]{1,0:T(8,128)} %get-tuple-element.43) | data formatting | bytes 52428800
  1556.9 9.3 copy.146
  (169 shorter events, 17.0 us)
Async XLA Ops:
  7.2 1491.1 %all-reduce.3.cloned.1.call-start = ((), (), s32[]{:S(2)}) async-start(), calls=%async_computation | async-start | bytes 209715200 | tf_op jit(solution)/shard_map/psum | solution.py:91
  10.1 24.7 %copy-start.35 = (f32[8,128]{1,0:T(8,128)}, f32[8,128]{1,0:T(8,128)S(1)}, u32[]{:S(2)}) copy-start(f32[8,128]{1,0:T(8,128)S(1)} %fusion.173) | copy-start | bytes 12292
  21.7 41.8 %copy-start.2 = (bf16[8,128,1280]{1,2,0:T(8,128)(2,1)}, bf16[8,128,1280]{1,2,0:T(8,128)(2,1)S(1)}, u32[]{:S(2)}) copy-start(bf16[8,128,1280]{1,2,0:T(8,128)(2,1)S(1)} %copy.65) | copy-start | bytes 7864324
  66.1 7.5 copy-start.17
  67.1 52.7 %slice-start.11 = ((s8[6553600]{0:T(1024)(128)(4,1)}), s8[2359296]{0:T(1024)(128)(4,1)S(1)}, s32[]{:S(2)}) async-start(s8[6553600]{0:T(1024)(128)(4,1)} %bitcast.244), calls=%async_computation.12 | async-start | bytes 4718592
  73.6 21.8 %copy-start.6 = (bf16[8,128,1280]{2,1,0:T(8,128)(2,1)}, bf16[8,128,1280]{2,1,0:T(8,128)(2,1)S(1)}, u32[]{:S(2)}) copy-start(bf16[8,128,1280]{2,1,0:T(8,128)(2,1)S(1)} %get-tuple-element.20) | copy-start | bytes 7864324
  74.2 45.6 %slice-start.12 = ((s8[6553600]{0:T(1024)(128)(4,1)}), s8[4194304]{0:T(1024)(128)(4,1)S(1)}, s32[]{:S(2)}) async-start(s8[6553600]{0:T(1024)(128)(4,1)} %bitcast.244), calls=%async_computation.13 | async-start | bytes 8388608
  119.8 5.0 copy-start.43
  119.8 10.9 copy-start.28
  119.9 10.9 copy-start.39
  119.9 10.9 slice-start.15
  124.8 6.0 slice-start.16
  146.2 17.2 %copy-start.3 = (bf16[8,128,1280]{1,2,0:T(8,128)(2,1)}, bf16[8,128,1280]{1,2,0:T(8,128)(2,1)S(1)}, u32[]{:S(2)}) copy-start(bf16[8,128,1280]{1,2,0:T(8,128)(2,1)S(1)} %copy.68) | copy-start | bytes 7864324
  166.1 7.2 copy-start.18
  173.9 73.5 %copy-start.37 = (f32[8,128]{1,0:T(8,128)}, f32[8,128]{1,0:T(8,128)S(1)}, u32[]{:S(2)}) copy-start(f32[8,128]{1,0:T(8,128)S(1)} %fusion.176) | copy-start | bytes 12292
  174.9 21.5 %copy-start.23 = (bf16[8,128,1280]{2,1,0:T(8,128)(2,1)S(1)}, bf16[8,128,1280]{2,1,0:T(8,128)(2,1)}, u32[]{:S(2)}) copy-start(bf16[8,128,1280]{2,1,0:T(8,128)(2,1)} %param.9) | copy-start | bytes 7864324
  226.1 21.3 %copy-start.46 = (f32[8,128]{1,0:T(8,128)S(1)}, f32[8,128]{1,0:T(8,128)}, u32[]{:S(2)}) copy-start(f32[8,128]{1,0:T(8,128)} %copy-done.45) | copy-start | bytes 12292
  226.1 21.3 %copy-start.26 = (bf16[8,128,1280]{2,1,0:T(8,128)(2,1)S(1)}, bf16[8,128,1280]{2,1,0:T(8,128)(2,1)}, u32[]{:S(2)}) copy-start(bf16[8,128,1280]{2,1,0:T(8,128)(2,1)} %copy-done.25) | copy-start | bytes 7864324
  247.5 4.8 copy-start.47
  257.1 11.2 slice-start.2
  261.7 6.7 slice-start.3
  261.7 6.7 copy-start.4
  287.6 13.7 copy-start.16
  301.3 6.9 copy-start.52
  301.3 20.9 %slice-start.13 = ((s8[6553600]{0:T(1024)(128)(4,1)}), s8[4194304]{0:T(1024)(128)(4,1)S(1)}, s32[]{:S(2)}) async-start(s8[6553600]{0:T(1024)(128)(4,1)} %bitcast.246), calls=%async_computation.14 | async-start | bytes 8388608
  308.2 7.5 copy-start.30
  308.2 7.5 copy-start.40
  308.2 14.0 slice-start.14
  315.7 6.5 copy-start.51
  327.6 6.1 copy-start.22
  327.6 12.1 slice-start.17
  333.7 6.0 slice-start.18
  339.8 6.9 copy-start.44
  349.4 32.2 %copy-start.7 = (bf16[8,128,1280]{2,1,0:T(8,128)(2,1)S(1)}, bf16[8,128,1280]{2,1,0:T(8,128)(2,1)}, u32[]{:S(2)}) copy-start(bf16[8,128,1280]{2,1,0:T(8,128)(2,1)} %copy-done.6) | copy-start | bytes 7864324
  381.6 21.3 %copy-start.42 = (f32[8,128]{1,0:T(8,128)S(1)}, f32[8,128]{1,0:T(8,128)}, u32[]{:S(2)}) copy-start(f32[8,128]{1,0:T(8,128)} %copy-done.41) | copy-start | bytes 12292
  381.6 21.3 %copy-start.14 = (bf16[8,128,1280]{2,1,0:T(8,128)(2,1)S(1)}, bf16[8,128,1280]{2,1,0:T(8,128)(2,1)}, u32[]{:S(2)}) copy-start(bf16[8,128,1280]{2,1,0:T(8,128)(2,1)} %fusion.71) | copy-start | bytes 7864324
  381.6 21.3 %copy-start.32 = (f32[8,128]{1,0:T(8,128)S(1)}, f32[8,128]{1,0:T(8,128)}, u32[]{:S(2)}) copy-start(f32[8,128]{1,0:T(8,128)} %copy-done.31) | copy-start | bytes 12292
  414.2 11.1 slice-start
  418.7 6.7 slice-start.1
  418.7 6.7 copy-start.5
  444.1 13.2 copy-start.12
  457.3 6.9 copy-start.27
  457.3 6.9 copy-start.38
  464.2 22.5 %copy-start.24 = (bf16[8,128,1280]{2,1,0:T(8,128)(2,1)S(1)}, bf16[8,128,1280]{2,1,0:T(8,128)(2,1)}, u32[]{:S(2)}) copy-start(bf16[8,128,1280]{2,1,0:T(8,128)(2,1)} %param.9) | copy-start | bytes 7864324
  486.7 25.8 %copy-start.10 = (bf16[8,128,1280]{2,1,0:T(8,128)(2,1)S(1)}, bf16[8,128,1280]{2,1,0:T(8,128)(2,1)}, u32[]{:S(2)}) copy-start(bf16[8,128,1280]{2,1,0:T(8,128)(2,1)} %param.8) | copy-start | bytes 7864324
  486.7 25.8 %copy-start.36 = (f32[8,128]{1,0:T(8,128)S(1)}, f32[8,128]{1,0:T(8,128)}, u32[]{:S(2)}) copy-start(f32[8,128]{1,0:T(8,128)} %copy-done.35) | copy-start | bytes 12292
  486.7 25.8 %copy-start.48 = (bf16[8,20,64,128]{3,2,1,0:T(8,128)(2,1)S(1)}, bf16[8,20,64,128]{3,2,1,0:T(8,128)(2,1)}, u32[]{:S(2)}) copy-start(bf16[8,20,64,128]{3,2,1,0:T(8,128)(2,1)} %fusion.153) | copy-start | bytes 7864324
  512.5 6.1 copy-start.20
  518.6 6.2 copy-start.49
  524.8 6.0 copy-start.8
  588.1 8.8 copy-start.50
  588.1 16.3 %slice-start.19 = ((s8[6553600]{0:T(1024)(128)(4,1)}), s8[4194304]{0:T(1024)(128)(4,1)S(1)}, s32[]{:S(2)}) async-start(s8[6553600]{0:T(1024)(128)(4,1)} %bitcast.252), calls=%async_computation.20 | async-start | bytes 8388608
  597.0 7.5 copy-start.21
  597.0 7.5 slice-start.20
  604.5 7.3 copy-start.34
  604.5 7.3 copy-start.13
  1498.3 19.3 %copy-start.19 = (f32[1,1280,1280]{2,1,0:T(8,128)S(1)}, f32[1,1280,1280]{2,1,0:T(8,128)}, u32[]{:S(2)}) copy-start(f32[1,1280,1280]{2,1,0:T(8,128)} %get-tuple-element.11) | copy-start | bytes 19660804
  1517.6 38.9 %slice-start.4 = ((s8[26214400]{0:T(1024)(128)(4,1)}), s8[1048576]{0:T(1024)(128)(4,1)S(1)}, s32[]{:S(2)}) async-start(s8[26214400]{0:T(1024)(128)(4,1)} %bitcast.222), calls=%async_computation.5 | async-start | bytes 2097152
  1517.6 38.9 %slice-start.5 = ((s8[26214400]{0:T(1024)(128)(4,1)}), s8[4194304]{0:T(1024)(128)(4,1)S(1)}, s32[]{:S(2)}) async-start(s8[26214400]{0:T(1024)(128)(4,1)} %bitcast.222), calls=%async_computation.6 | async-start | bytes 8388608
  1517.6 38.9 %slice-start.6 = ((s8[26214400]{0:T(1024)(128)(4,1)}), s8[4194304]{0:T(1024)(128)(4,1)S(1)}, s32[]{:S(2)}) async-start(s8[26214400]{0:T(1024)(128)(4,1)} %bitcast.222), calls=%async_computation.7 | async-start | bytes 8388608
  1517.6 38.9 %slice-start.7 = ((s8[26214400]{0:T(1024)(128)(4,1)}), s8[4194304]{0:T(1024)(128)(4,1)S(1)}, s32[]{:S(2)}) async-start(s8[26214400]{0:T(1024)(128)(4,1)} %bitcast.222), calls=%async_computation.8 | async-start | bytes 8388608
  1535.8 20.7 %slice-start.8 = ((s8[26214400]{0:T(1024)(128)(4,1)}), s8[4194304]{0:T(1024)(128)(4,1)S(1)}, s32[]{:S(2)}) async-start(s8[26214400]{0:T(1024)(128)(4,1)} %bitcast.222), calls=%async_computation.9 | async-start | bytes 8388608
  1535.8 20.7 %slice-start.9 = ((s8[26214400]{0:T(1024)(128)(4,1)}), s8[4194304]{0:T(1024)(128)(4,1)S(1)}, s32[]{:S(2)}) async-start(s8[26214400]{0:T(1024)(128)(4,1)} %bitcast.222), calls=%async_computation.10 | async-start | bytes 8388608
  1535.8 21.1 %slice-start.10 = ((s8[26214400]{0:T(1024)(128)(4,1)}), s8[4194304]{0:T(1024)(128)(4,1)S(1)}, s32[]{:S(2)}) async-start(s8[26214400]{0:T(1024)(128)(4,1)} %bitcast.222), calls=%async_computation.11 | async-start | bytes 8388608
  (11 other events, 19.7 us)
Sparse Core Ops, SparseCore 0:
  588.2 910.0 all-reduce.2
where the time goes:
time: 1580 us; the launch traced here: 1570 us
  waiting for transfers between devices  884 us (56%)
  matrix products  539 us (34%)
  local copies, waits for them, and re-layouts  72.9 us (5%)
  other arithmetic  62.1 us (4%)
    psum x1, waiting for transfers between devices, local_step(): lax.psum((attn_part, up_part, down_part), 'data')  884 us
    dot_general x45, matrix products, product(): return jnp.einsum(subscripts, lhs, rhs, preferred_element_type=jnp.float32)  517 us
    unnamed x150, local copies, waits for them, and re-layouts  41.1 us
  transfers between devices with their start and end apart: 1, of which 1 were waited for; matrix products, arithmetic and copies ran while one was open for 2% of the time, Pallas kernels for 0%

commit v1 on v0

--- a/solution.py
+++ b/solution.py
@@ -1,10 +1,18 @@
+import functools
+
 import jax
 import jax.numpy as jnp
 from jax import lax
+from jax.experimental import pallas as pl
+from jax.experimental.pallas import tpu as pltpu
 from jax.sharding import PartitionSpec as P
 
 EPS = 1e-6
 HEAD_DIM = 64
+MESH = pl.DeviceIdType.MESH
+ROWS, LANES = 40, 128
+LAG = 2
+ORDERS = ("xyz", "yzx", "zxy")
 
 
 def rms_norm(x_f32):
@@ -17,6 +25,144 @@
 
 def product(subscripts, lhs, rhs):
     return jnp.einsum(subscripts, lhs, rhs, preferred_element_type=jnp.float32)
+
+
+def scatter_kernel(segments, n_chunks, *refs):
+    n_in_refs = len(segments)
+    g_refs, out_refs = refs[:n_in_refs], refs[n_in_refs:2 * n_in_refs]
+    own, rc, r1, r2, r3, load_sem, out_sem, send_sem, recv_sem = refs[2 * n_in_refs:]
+    me = lax.axis_index("data")
+    bit = {"c": lax.rem(me, 2), "x": lax.rem(me // 2, 2), "y": lax.rem(me // 4, 2), "z": me // 8}
+    step = {"c": 1, "x": 2, "y": 4, "z": 8}
+    peer = {d: me + step[d] * (1 - 2 * bit[d]) for d in step}
+    barrier = pltpu.get_barrier_semaphore()
+    for d in "cxyz":
+        pl.semaphore_signal(barrier, inc=1, device_id=(peer[d],), device_id_type=MESH)
+    pl.semaphore_wait(barrier, 4)
+    n_own, n_in = own.shape[1], rc.shape[1]
+    bufs = (rc, r1, r2, r3)
+
+    def pick(color, stage, other):
+        idx = {"z": slice(None), "y": slice(None), "x": slice(None)}
+        for s in range(stage):
+            d = ORDERS[color][s]
+            idx[d] = 1 - bit[d] if (other and s == stage - 1) else bit[d]
+        return tuple(idx[d] for d in "zyx")
+
+    def place(seg, k):
+        per, first = segments[seg]
+        blocks = per // ROWS
+        k = k - first
+        return pl.multiple_of(lax.rem(k, blocks) * ROWS, 8), pl.multiple_of((k // blocks) * LANES, LANES)
+
+    def each(k, fn):
+        for seg in range(n_in_refs):
+            first = segments[seg][1]
+            last = segments[seg + 1][1] if seg + 1 < n_in_refs else n_chunks
+            if n_in_refs == 1:
+                fn(seg, k)
+            else:
+                @pl.when(jnp.logical_and(k >= first, k < last))
+                def _():
+                    fn(seg, k)
+
+    def first_send(color, j, seg, k):
+        row, col = place(seg, k)
+        slot = lax.rem(j, n_in)
+        return pltpu.make_async_remote_copy(
+            g_refs[seg].at[:, :, :, 1 - bit["c"], pl.ds(row, ROWS), pl.ds(col, LANES)], rc.at[color, slot],
+            send_sem.at[color, 0, slot], recv_sem.at[color, 0, slot], device_id=(peer["c"],), device_id_type=MESH)
+
+    def next_send(color, stage, j):
+        slot, so = lax.rem(j, n_in), lax.rem(j, n_own)
+        return pltpu.make_async_remote_copy(
+            own.at[(color, so) + pick(color, stage, True)], bufs[stage].at[color, slot],
+            send_sem.at[color, stage, slot], recv_sem.at[color, stage, slot],
+            device_id=(peer[ORDERS[color][stage - 1]],), device_id_type=MESH)
+
+    def load(color, j, seg, k):
+        so = lax.rem(j, n_own)
+        row, col = place(seg, k)
+        return pltpu.make_async_copy(g_refs[seg].at[:, :, :, bit["c"], pl.ds(row, ROWS), pl.ds(col, LANES)],
+                                     own.at[color, so], load_sem.at[color, so])
+
+    def store(color, j, seg, k):
+        so = lax.rem(j, n_own)
+        row, col = place(seg, k)
+        return pltpu.make_async_copy(own.at[(color, so) + pick(color, 3, False)],
+                                     out_refs[seg].at[pl.ds(row, ROWS), pl.ds(col, LANES)], out_sem.at[color, so])
+
+    def live(j, color):
+        return jnp.logical_and(j >= 0, 3 * j + color < n_chunks)
+
+    def tick(t, carry):
+        for color in range(3):
+            j = t - 4 * LAG - 1
+
+            @pl.when(live(j, color))
+            def _():
+                store(color, j, 0, segments[0][1]).wait()
+        for stage in (3, 2, 1, 0):
+            j = t - (stage + 1) * LAG
+            for color in range(3):
+                @pl.when(live(j, color))
+                def _():
+                    slot, so = lax.rem(j, n_in), lax.rem(j, n_own)
+                    if stage == 0:
+                        load(color, j, 0, segments[0][1]).wait()
+                        copy = first_send(color, j, 0, segments[0][1])
+                    else:
+                        copy = next_send(color, stage, j)
+                    copy.wait_send()
+                    copy.wait_recv()
+                    keep = (color, so) + pick(color, stage, False)
+                    own[keep] = own[keep] + bufs[stage][color, slot]
+                    if stage < 3:
+                        next_send(color, stage + 1, j).start()
+                    else:
+                        each(3 * j + color, lambda seg, k: store(color, j, seg, k).start())
+        for color in range(3):
+            @pl.when(live(t, color))
+            def _():
+                def go(seg, k):
+                    first_send(color, t, seg, k).start()
+                    load(color, t, seg, k).start()
+                each(3 * t + color, go)
+        return carry
+
+    lax.fori_loop(0, pl.cdiv(n_chunks, 3) + 4 * LAG + 1, tick, 0)
+
+
+def scatter_sum(grads, collective_id):
+    segments, first, views, outs = [], 0, [], []
+    for grad in grads:
+        rows, cols = grad.shape
+        per = rows // 16
+        segments.append((per, first))
+        first += (per // ROWS) * (cols // LANES)
+        views.append(grad.reshape(2, 2, 2, 2, per, cols))
+        outs.append(jax.ShapeDtypeStruct((per, cols), jnp.float32))
+    n_own, n_in, blk = 4 * LAG + 2, 2 * LAG, (ROWS, LANES)
+    size = sum(g.size for g in grads) * 4
+    return pl.pallas_call(
+        functools.partial(scatter_kernel, tuple(segments), first),
+        out_shape=outs,
+        in_specs=[pl.BlockSpec(memory_space=pl.ANY)] * len(grads),
+        out_specs=[pl.BlockSpec(memory_space=pl.ANY)] * len(grads),
+        scratch_shapes=[
+            pltpu.VMEM((3, n_own, 2, 2, 2) + blk, jnp.float32), pltpu.VMEM((3, n_in, 2, 2, 2) + blk, jnp.float32),
+            pltpu.VMEM((3, n_in, 2, 2) + blk, jnp.float32), pltpu.VMEM((3, n_in, 2) + blk, jnp.float32),
+            pltpu.VMEM((3, n_in) + blk, jnp.float32),
+            pltpu.SemaphoreType.DMA((3, n_own)), pltpu.SemaphoreType.DMA((3, n_own)),
+            pltpu.SemaphoreType.DMA((3, 4, n_in)), pltpu.SemaphoreType.DMA((3, 4, n_in))],
+        compiler_params=pltpu.CompilerParams(collective_id=collective_id, has_side_effects=True),
+        cost_estimate=pl.CostEstimate(flops=size * 8000, bytes_accessed=2 * size, transcendentals=0),
+        name=f"scatter_sum_{collective_id}",
+    )(*views)
+
+
+def gather(shard):
+    return lax.all_gather(shard, "data", axis=0, tiled=True)
 
 
 def layer_forward(x_act, w_query, w_key, w_value, w_proj, w_up, w_down, heads):
@@ -41,18 +187,21 @@
     return x_next, kept
 
 
-def layer_backward(d_next, kept, w_query, w_key, w_value, w_proj, w_up, w_down):
-    x_act, normed, query, key_act, value, probs, mixed, hidden, normed2, pre_act, activated = kept
-    batch, seq_len, heads, head_dim = query.shape
-    width = heads * head_dim
-    g_down = product("bsf,bsd->fd", activated, d_next)
+def mlp_backward(d_next, kept, w_up, w_down):
+    hidden, normed2, pre_act = kept[7], kept[8], kept[9]
     d_activated = product("bsd,fd->bsf", d_next, w_down).astype(jnp.bfloat16)
     gelu_pull = jax.vjp(gelu_tanh, pre_act.astype(jnp.float32))[1]
     d_pre = gelu_pull(d_activated.astype(jnp.float32))[0].astype(jnp.bfloat16)
-    g_up = product("bsd,bsf->df", normed2, d_pre)
     d_normed2 = product("bsf,df->bsd", d_pre, w_up).astype(jnp.bfloat16)
     hidden_pull = jax.vjp(rms_norm, hidden.astype(jnp.float32))[1]
     d_hidden = (d_next.astype(jnp.float32) + hidden_pull(d_normed2.astype(jnp.float32))[0]).astype(jnp.bfloat16)
+    return d_pre, d_hidden
+
+
+def attention_backward(d_hidden, kept, w_query, w_key, w_value, w_proj):
+    x_act, normed, query, key_act, value, probs, mixed = kept[:7]
+    batch, seq_len, heads, head_dim = query.shape
+    width = heads * head_dim
     g_proj = product("bsd,bse->de", mixed, d_hidden)
     d_mixed = product("bse,de->bsd", d_hidden, w_proj).astype(jnp.bfloat16).reshape(batch, seq_len, heads, head_dim)
     d_probs = product("bqhd,bkhd->bhqk", d_mixed, value).astype(jnp.bfloat16).astype(jnp.float32)
@@ -69,35 +218,49 @@
                 + product("bse,de->bsd", d_value, w_value)).astype(jnp.bfloat16)
     input_pull = jax.vjp(rms_norm, x_act.astype(jnp.float32))[1]
     d_input = (d_hidden.astype(jnp.float32) + input_pull(d_normed.astype(jnp.float32))[0]).astype(jnp.bfloat16)
-    return d_input, (g_query, g_key, g_value, g_proj), g_up, g_down
+    return d_input, (g_query, g_key, g_value, g_proj)
+
+
+def place_rows(dst, shard_sum, layer):
+    rows, cols = shard_sum.shape
+    blk = 256
+
+    def kernel(*refs):
+        refs[-1][0] = refs[0][...]
+
+    args = (shard_sum,) if dst is None else (shard_sum, dst)
+    return pl.pallas_call(
+        kernel,
+        grid=(rows // blk,),
+        out_shape=jax.ShapeDtypeStruct((2, rows, cols), jnp.float32),
+        in_specs=[pl.BlockSpec((blk, cols), lambda i: (i, 0))] + [pl.BlockSpec(memory_space=pl.ANY)] * (len(args) - 1),
+        out_specs=pl.BlockSpec((1, blk, cols), lambda i: (layer, i, 0)),
+        input_output_aliases={} if dst is None else {1: 0},
+        cost_estimate=pl.CostEstimate(flops=rows * cols, bytes_accessed=8 * rows * cols, transcendentals=0),
+        name=f"place_rows_{layer}",
+    )(*args)
 
 
 def solution(mesh):
     def local_step(x_init, cot_out, w_query, w_key, w_value, w_proj, w_up, w_down):
         heads = x_init.shape[-1] // HEAD_DIM
-        layers = w_query.shape[0]
-        x_act = x_init
-        kept_all = []
-        for layer in range(layers):
-            x_act, kept = layer_forward(x_act, w_query[layer], w_key[layer], w_value[layer], w_proj[layer], w_up, w_down, heads)
-            kept_all.append(kept)
-        d_act = cot_out
-        g_up = jnp.zeros(w_up.shape, jnp.float32)
-        g_down = jnp.zeros(w_down.shape, jnp.float32)
-        attn_grads = []
-        for layer in reversed(range(layers)):
-            d_act, attn_part, up_part, down_part = layer_backward(
-                d_act, kept_all[layer], w_query[layer], w_key[layer], w_value[layer], w_proj[layer], w_up, w_down)
-            attn_part, up_part, down_part = lax.psum((attn_part, up_part, down_part), "data")
-            attn_grads.append(attn_part)
-            g_up = g_up + up_part
-            g_down = g_down + down_part
-        attn_grads = attn_grads[::-1]
-        g_query = jnp.stack([part[0] for part in attn_grads])
-        g_key = jnp.stack([part[1] for part in attn_grads])
-        g_value = jnp.stack([part[2] for part in attn_grads])
-        g_proj = jnp.stack([part[3] for part in attn_grads])
-        return g_query, g_key, g_value, g_proj, g_up, g_down, d_act
+        weights = [(w_query[i], w_key[i], w_value[i], w_proj[i]) for i in range(2)]
+        x_mid, kept0 = layer_forward(x_init, *weights[0], w_up, w_down, heads)
+        _, kept1 = layer_forward(x_mid, *weights[1], w_up, w_down, heads)
+        d_pre1, d_hidden1 = mlp_backward(cot_out, kept1, w_up, w_down)
+        d_mid, attn1 = attention_backward(d_hidden1, kept1, *weights[1])
+        shards1 = scatter_sum(list(attn1), 1)
+        full1 = [gather(s) for s in shards1]
+        d_pre0, d_hidden0 = mlp_backward(d_mid, kept0, w_up, w_down)
+        g_up = product("bsd,bsf->df", kept1[8], d_pre1) + product("bsd,bsf->df", kept0[8], d_pre0)
+        g_down = product("bsf,bsd->fd", kept1[10], cot_out) + product("bsf,bsd->fd", kept0[10], d_mid)
+        s_up, s_down = scatter_sum([g_up, g_down], 2)
+        f_up, f_down = gather(s_up), gather(s_down)
+        dx, attn0 = attention_backward(d_hidden0, kept0, *weights[0])
+        shards0 = scatter_sum(list(attn0), 3)
+        full0 = [gather(s) for s in shards0]
+        attn = [place_rows(place_rows(None, a, 1), b, 0) for a, b in zip(full1, full0)]
+        return (*attn, f_up, f_down, dx)
 
     data_spec = P("data")
     full_spec = P()

time: 1580 us -> 1290 us (0.82)
  waiting for transfers between devices: 884 us -> 161 us
  Pallas kernels: 0 us -> 466 us
  other arithmetic: 62.1 us -> 26 us
    psum x1 -> x0, waiting for transfers between devices: 884 us -> none  [local_step(): lax.psum((attn_part, up_part, down_part), 'data')]
    pallas_call x0 -> x11, Pallas kernels: none -> 466 us  [the longest x3 408 us: scatter_sum(): pl.pallas_call(functools.partial(scatter_kernel, tuple(segments), first),...]
    all_gather x0 -> x10, waiting for transfers between devices: none -> 157 us  [gather(): return lax.all_gather(shard, 'data', axis=0, tiled=True)]
    another operation x2 -> x0, other arithmetic: 36.7 us -> none  [the longest x1 18.5 us: local_step(): g_query = jnp.stack([part[0] for part in attn_grads])]
    unnamed x150 -> x156, local copies, waits for them, and re-layouts: 41.1 us -> 44.3 us
  transfers between devices with their start and end apart: 1 -> 10, of which waited for: 1 -> 2; matrix products, arithmetic and copies ran while one was open for 2% -> 20% of each run, Pallas kernels for 0% -> 29%
where the time goes in v1:
time: 1290 us; the launch traced here: 1280 us
  matrix products  532 us (41%)
  Pallas kernels  466 us (36%)
  waiting for transfers between devices  161 us (12%)
  local copies, waits for them, and re-layouts  83.2 us (6%)
  other arithmetic  26 us (2%)
  between operations  15.3 us (1%)
    dot_general x45, matrix products, product(): return jnp.einsum(subscripts, lhs, rhs, preferred_element_type=jnp.float32)  509 us
    pallas_call x3, Pallas kernels, scatter_sum(): pl.pallas_call(functools.partial(scatter_kernel, tuple(segments), first),...  408 us
    all_gather x10, waiting for transfers between devices, gather(): return lax.all_gather(shard, 'data', axis=0, tiled=True)  157 us
    pallas_call x8, Pallas kernels, place_rows(): pl.pallas_call(kernel, grid=(rows // blk,), out_shape=jax.ShapeDtypeStruc...  58.4 us
    unnamed x156, local copies, waits for them, and re-layouts  44.3 us
  transfers between devices with their start and end apart: 10, of which 2 were waited for; matrix products, arithmetic and copies ran while one was open for 20% of the time, Pallas kernels for 29%

profile of v1, /device:TPU:0, one launch (start us, length us, event | category | flops | bytes accessed | tf_op | source)
XLA Modules:
  0.0 1284.4 jit_solution(3873513035578281928)
XLA Ops:
  10.1 7.8 convolution_convert_fusion.9
  22.7 6.8 convolution_convert_fusion.8
  34.0 6.8 convolution_convert_fusion.7
  44.1 11.5 fusion.197
  55.6 5.7 divide_convert_fusion.1
  65.0 6.3 fusion.83
  71.9 21.4 %fusion.52 = bf16[8,128,5120]{2,1,0:T(8,128)(2,1)} fusion(bf16[1280,5120]{1,0:T(8,128)(2,1)} %param.14, bf16[8,128,1280]{2,1,0:T(8,128)(2,1)S(1)} %get-tuple-element.34, f32[8,128]{1,0:T(8,128)S(1)} %fusion.178), kind=kOutput, calls=%fused_computation.90 | convolution fusion | flops 13430947840 | bytes 26218496 | tf_op jit(solution)/shard_map/bsd,df->bsf/dot_general | solution.py:27
  93.4 24.4 %fusion.87 = (f32[8,128]{1,0:T(8,128)S(1)}, bf16[8,128,1280]{2,1,0:T(8,128)(2,1)S(1)}) fusion(bf16[5120,1280]{1,0:T(8,128)(2,1)} %param.15, bf16[8,128,5120]{2,1,0:T(8,128)(2,1)} %fusion.52, bf16[8,128,1280]{2,1,0:T(8,128)(2,1)S(1)} %get-tuple-element.34), kind=kOutput, calls=%fused_computation.127 | convolution fusion | flops 13484686336 | bytes 28839936 | tf_op jit(solution)/shard_map/bsf,fd->bsd/dot_general | solution.py:27
  117.9 4.9 convolution_convert_fusion.3
  122.8 5.9 convolution_convert_fusion.4
  128.8 5.0 convolution_convert_fusion.5
  144.5 11.5 fusion.198
  156.0 5.7 divide_convert_fusion
  165.4 6.2 fusion.76
  173.1 21.0 %fusion.55 = bf16[8,128,5120]{2,1,0:T(8,128)(2,1)} fusion(bf16[1280,5120]{1,0:T(8,128)(2,1)} %param.14, bf16[8,128,1280]{2,1,0:T(8,128)(2,1)S(1)} %get-tuple-element.40, f32[8,128]{1,0:T(8,128)S(1)} %fusion.180), kind=kOutput, calls=%fused_computation.91 | convolution fusion | flops 13430947840 | bytes 26218496 | tf_op jit(solution)/shard_map/bsd,df->bsf/dot_general | solution.py:27
  194.1 29.9 %fusion.8 = bf16[8,128,5120]{2,1,0:T(8,128)(2,1)} fusion(bf16[8,128,5120]{2,1,0:T(8,128)(2,1)} %fusion.55, bf16[8,128,1280]{2,1,0:T(8,128)(2,1)S(1)} %copy-done.31, bf16[5120,1280]{1,0:T(8,128)(2,1)} %param.15), kind=kOutput, calls=%fused_computation.22 | convolution fusion | flops 13542359040 | bytes 36700160 | tf_op jit(solution)/shard_map/bsd,fd->bsf/dot_general | solution.py:27
  224.0 21.3 %fusion.78 = (f32[8,128]{1,0:T(8,128)S(1)}, bf16[8,128,1280]{2,1,0:T(8,128)(2,1)}) fusion(bf16[8,128,1280]{2,1,0:T(8,128)(2,1)} %copy-done.33, bf16[8,128,5120]{2,1,0:T(8,128)(2,1)} %fusion.8, bf16[1280,5120]{1,0:T(8,128)(2,1)} %param.14), kind=kOutput, calls=%fused_computation.118 | convolution fusion | flops 13428325376 | bytes 28839936 | tf_op jit(solution)/shard_map/bsf,df->bsd/dot_general | solution.py:27
  249.9 4.9 convolution_convert_fusion.1
  254.8 4.8 copy.78
  259.6 5.7 convolution_convert_fusion.11
  265.3 13.5 %fusion.158 = bf16[8,20,64,128]{3,2,1,0:T(8,128)(2,1)} fusion(bf16[8,128,20,64]{1,3,2,0:T(8,128)(2,1)} %bitcast.282, bf16[8,20,128,128]{2,3,1,0:T(8,128)(2,1)} %copy-done.1, bf16[8,20,128,128]{2,3,1,0:T(8,128)(2,1)} %convolution_convert_fusion.11), kind=kOutput, calls=%fused_computation.204 | convolution fusion | flops 360468608 | bytes 15728640 | tf_op jit(solution)/shard_map/bhqk,bqhd->bkhd/dot_general | solution.py:27
  278.8 14.0 %fusion.157 = bf16[8,20,64,128]{3,2,1,0:T(8,128)(2,1)} fusion(bf16[8,128,20,64]{1,3,2,0:T(8,128)(2,1)} %bitcast.280, bf16[8,20,128,128]{2,3,1,0:T(8,128)(2,1)} %copy-done.1, bf16[8,20,128,128]{2,3,1,0:T(8,128)(2,1)} %convolution_convert_fusion.11), kind=kOutput, calls=%fused_computation.203 | convolution fusion | flops 360468608 | bytes 15728640 | tf_op jit(solution)/shard_map/bhqk,bkhd->bqhd/dot_general | solution.py:27
  292.8 6.3 convolution_convert_fusion.13
  299.2 7.0 fusion.108
  306.3 5.4 fusion.111
  311.7 6.5 fusion.90
  324.6 9.1 convolution_bitcast_fusion.2.refs_2_
  333.7 5.7 convolution_bitcast_fusion.3.refs_1_
  339.4 5.5 convolution_bitcast_fusion.4.refs_0_
  344.9 6.2 convolution_bitcast_fusion.refs_3_
  351.1 96.1 %scatter_sum_1.1 = (f32[80,1280]{1,0:T(8,128)}, f32[80,1280]{1,0:T(8,128)}, f32[80,1280]{1,0:T(8,128)}, f32[80,1280]{1,0:T(8,128)}) custom-call(f32[2,2,2,2,80,1280]{5,4,3,2,1,0:T(8,128)} %convolution_bitcast_fusion.4.refs_0_, f32[2,2,2,2,80,1280]{5,4,3,2,1,0:T(8,128)} %convolution_bitcast_fusion.3.refs_1_, ...), custom_call_target="tpu_custom_call" | custom-call | flops 209715200000 | bytes 52428800 | tf_op jit(solution)/shard_map/scatter_sum_1/pallas_call | solution.py:147
  449.4 32.0 %fusion.11 = bf16[8,128,5120]{2,1,0:T(8,128)(2,1)} fusion(bf16[8,128,5120]{2,1,0:T(8,128)(2,1)} %fusion.52, bf16[8,128,1280]{2,1,0:T(8,128)(2,1)} %get-tuple-element.30, bf16[5120,1280]{1,0:T(8,128)(2,1)} %param.15), kind=kOutput, calls=%fused_computation.25 | convolution fusion | flops 13542359040 | bytes 36700160 | tf_op jit(solution)/shard_map/bsd,fd->bsf/dot_general | solution.py:27
  481.4 21.6 %fusion.86 = (f32[8,128]{1,0:T(8,128)S(1)}, bf16[8,128,1280]{2,1,0:T(8,128)(2,1)}) fusion(bf16[8,128,1280]{2,1,0:T(8,128)(2,1)S(1)} %copy-done.10, bf16[8,128,5120]{2,1,0:T(8,128)(2,1)} %fusion.11, bf16[1280,5120]{1,0:T(8,128)(2,1)} %param.14), kind=kOutput, calls=%fused_computation.126 | convolution fusion | flops 13428325376 | bytes 28839936 | tf_op jit(solution)/shard_map/bsf,df->bsd/dot_general | solution.py:27
  507.6 4.8 convolution_convert_fusion
  517.0 5.7 convolution_convert_fusion.10
  522.7 13.3 %fusion.156 = bf16[8,20,64,128]{3,2,1,0:T(8,128)(2,1)} fusion(bf16[8,128,20,64]{1,3,2,0:T(8,128)(2,1)} %bitcast.278, bf16[8,20,128,128]{2,3,1,0:T(8,128)(2,1)} %copy-done, bf16[8,20,128,128]{2,3,1,0:T(8,128)(2,1)} %convolution_convert_fusion.10), kind=kOutput, calls=%fused_computation.202 | convolution fusion | flops 360468608 | bytes 15728640 | tf_op jit(solution)/shard_map/bhqk,bqhd->bkhd/dot_general | solution.py:27
  536.0 13.9 %fusion.155 = bf16[8,20,64,128]{3,2,1,0:T(8,128)(2,1)} fusion(bf16[8,128,20,64]{1,3,2,0:T(8,128)(2,1)} %bitcast.276, bf16[8,20,128,128]{2,3,1,0:T(8,128)(2,1)} %copy-done, bf16[8,20,128,128]{2,3,1,0:T(8,128)(2,1)} %convolution_convert_fusion.10), kind=kOutput, calls=%fused_computation.201 | convolution fusion | flops 360468608 | bytes 15728640 | tf_op jit(solution)/shard_map/bhqk,bkhd->bqhd/dot_general | solution.py:27
  549.9 6.3 convolution_convert_fusion.12
  556.3 6.7 fusion.123
  563.1 5.4 fusion.120
  568.5 6.5 fusion.82
  581.4 9.0 convolution_bitcast_fusion.5.refs_2_
  590.3 5.7 convolution_bitcast_fusion.6.refs_1_
  596.1 5.5 convolution_bitcast_fusion.7.refs_0_
  601.6 6.2 convolution_bitcast_fusion.1.refs_3_
  607.8 102.8 %scatter_sum_3.1 = (f32[80,1280]{1,0:T(8,128)}, f32[80,1280]{1,0:T(8,128)}, f32[80,1280]{1,0:T(8,128)}, f32[80,1280]{1,0:T(8,128)}) custom-call(f32[2,2,2,2,80,1280]{5,4,3,2,1,0:T(8,128)} %convolution_bitcast_fusion.7.refs_0_, f32[2,2,2,2,80,1280]{5,4,3,2,1,0:T(8,128)} %convolution_bitcast_fusion.6.refs_1_, ...), custom_call_target="tpu_custom_call" | custom-call | flops 209715200000 | bytes 52428800 | tf_op jit(solution)/shard_map/scatter_sum_3/pallas_call | solution.py:147
  712.8 22.7 %fusion.152 = f32[1280,5120,1]{1,0,2:T(8,128)} fusion(bf16[8,128,5120]{2,1,0:T(8,128)(2,1)} %fusion.8, bf16[8,128,1280]{2,1,0:T(8,128)(2,1)} %copy-done.33, f32[8,128]{1,0:T(8,128)S(1)} %copy-done.44), kind=kOutput, calls=%fused_computation.200 | convolution fusion | flops 13425704960 | bytes 39325696 | tf_op jit(solution)/shard_map/bsd,bsf->df/dot_general | solution.py:27
  735.5 25.9 %fusion.40 = f32[5120,1280,1]{1,0,2:T(8,128)} fusion(bf16[8,128,1280]{2,1,0:T(8,128)(2,1)S(1)} %copy-done.32, bf16[8,128,5120]{2,1,0:T(8,128)(2,1)} %fusion.55), kind=kOutput, calls=%fused_computation.60 | convolution fusion | flops 13474201600 | bytes 39321600 | tf_op jit(solution)/shard_map/bsf,bsd->fd/dot_general | solution.py:27
  761.4 27.9 %bitcast_add_fusion.1 = f32[1280,5120]{1,0:T(8,128)} fusion(f32[1280,5120,1]{1,0,2:T(8,128)} %fusion.152, bf16[8,128,5120]{2,1,0:T(8,128)(2,1)} %fusion.11, bf16[8,128,1280]{2,1,0:T(8,128)(2,1)S(1)} %copy-done.11, f32[8,128]{1,0:T(8,128)S(1)} %copy-done.40), kind=kOutput, calls=%fused_computation.17 | convolution fusion | flops 13432258560 | bytes 65540096 | tf_op jit(solution)/shard_map/bsd,bsf->df/dot_general | solution.py:27
  789.3 28.6 %bitcast_add_fusion = f32[5120,1280]{1,0:T(8,128)} fusion(f32[5120,1280,1]{1,0,2:T(8,128)} %fusion.40, bf16[8,128,1280]{2,1,0:T(8,128)(2,1)S(1)} %copy-done.16, bf16[8,128,5120]{2,1,0:T(8,128)(2,1)} %fusion.52), kind=kOutput, calls=%fused_computation.16 | convolution fusion | flops 13480755200 | bytes 65536000 | tf_op jit(solution)/shard_map/bsf,bsd->fd/dot_general | solution.py:27
  817.9 209.1 %scatter_sum_2.1 = (f32[80,5120]{1,0:T(8,128)}, f32[320,1280]{1,0:T(8,128)}) custom-call(f32[2,2,2,2,80,5120]{5,4,3,2,1,0:T(8,128)} %bitcast.262, f32[2,2,2,2,320,1280]{5,4,3,2,1,0:T(8,128)} %bitcast.301), custom_call_target="tpu_custom_call" | custom-call | flops 419430400000 | bytes 104857600 | tf_op jit(solution)/shard_map/scatter_sum_2/pallas_call | solution.py:147
  1027.7 7.3 place_rows_1.7.refs_1_
  1035.0 7.3 place_rows_1.6.refs_1_
  1042.3 7.3 place_rows_1.5.refs_1_
  1049.6 7.3 place_rows_1.4.refs_1_
  1056.9 7.3 place_rows_0.7
  1064.2 7.3 place_rows_0.6
  1071.5 7.3 place_rows_0.5
  1078.8 7.3 place_rows_0.4
  1086.1 47.5 %all-gather.27.cloned.1.call-done = f32[1280,5120]{1,0:T(8,128)} async-done(((f32[80,5120]{1,0:T(8,128)}), f32[1280,5120]{1,0:T(8,128)}) %all-gather.27.cloned.1.call-update) | async-done | bytes 26214416 | tf_op jit(solution)/shard_map/all_gather | solution.py:165
  1133.6 109.4 %all-gather.29.cloned.1.call-done = f32[5120,1280]{1,0:T(8,128)} async-done(((f32[320,1280]{1,0:T(8,128)}), f32[5120,1280]{1,0:T(8,128)}) %all-gather.29.cloned.1.call-update) | async-done | bytes 26214416 | tf_op jit(solution)/shard_map/all_gather | solution.py:165
  1243.0 19.1 %copy.175 = f32[1280,5120]{1,0:T(8,128)} copy(f32[1280,5120]{1,0:T(8,128)} %all-gather.27.cloned.1.call-done) | data formatting | bytes 52428800
  1262.1 6.0 copy-done.6
  1268.1 9.3 copy.176
  (211 shorter events, 66.9 us)
Async XLA Ops:
  7.2 1020.5 %all-gather.25.cloned.1.call-start = ((), (), s32[]{:S(2)}) async-start(), calls=%async_computation.7 | async-start | bytes 6963200 | tf_op jit(solution)/shard_map/all_gather | solution.py:165
  10.1 23.8 %copy-start.45 = (f32[8,128]{1,0:T(8,128)}, f32[8,128]{1,0:T(8,128)S(1)}, u32[]{:S(2)}) copy-start(f32[8,128]{1,0:T(8,128)S(1)} %fusion.177) | copy-start | bytes 12292
  44.1 17.2 %copy-start.2 = (bf16[8,128,1280]{1,2,0:T(8,128)(2,1)}, bf16[8,128,1280]{1,2,0:T(8,128)(2,1)S(1)}, u32[]{:S(2)}) copy-start(bf16[8,128,1280]{1,2,0:T(8,128)(2,1)S(1)} %copy.70) | copy-start | bytes 7864324
  63.9 7.3 copy-start.23
  65.0 52.9 %slice-start = ((s8[6553600]{0:T(1024)(128)(4,1)}), s8[2359296]{0:T(1024)(128)(4,1)S(1)}, s32[]{:S(2)}) async-start(s8[6553600]{0:T(1024)(128)(4,1)} %bitcast.289), calls=%async_computation.10 | async-start | bytes 4718592
  71.3 22.1 %copy-start.9 = (bf16[8,128,1280]{2,1,0:T(8,128)(2,1)}, bf16[8,128,1280]{2,1,0:T(8,128)(2,1)S(1)}, u32[]{:S(2)}) copy-start(bf16[8,128,1280]{2,1,0:T(8,128)(2,1)S(1)} %get-tuple-element.34) | copy-start | bytes 7864324
  71.9 46.0 %slice-start.1 = ((s8[6553600]{0:T(1024)(128)(4,1)}), s8[4194304]{0:T(1024)(128)(4,1)S(1)}, s32[]{:S(2)}) async-start(s8[6553600]{0:T(1024)(128)(4,1)} %bitcast.289), calls=%async_computation.11 | async-start | bytes 8388608
  117.8 11.0 copy-start.35
  117.8 10.9 copy-start.47
  117.9 10.9 slice-start.6
  122.8 6.0 slice-start.7
  144.4 17.2 %copy-start.4 = (bf16[8,128,1280]{1,2,0:T(8,128)(2,1)}, bf16[8,128,1280]{1,2,0:T(8,128)(2,1)S(1)}, u32[]{:S(2)}) copy-start(bf16[8,128,1280]{1,2,0:T(8,128)(2,1)S(1)} %copy.73) | copy-start | bytes 7864324
  164.3 7.2 copy-start.25
  172.2 73.1 %copy-start.43 = (f32[8,128]{1,0:T(8,128)}, f32[8,128]{1,0:T(8,128)S(1)}, u32[]{:S(2)}) copy-start(f32[8,128]{1,0:T(8,128)S(1)} %fusion.180) | copy-start | bytes 12292
  173.1 21.0 %copy-start.31 = (bf16[8,128,1280]{2,1,0:T(8,128)(2,1)S(1)}, bf16[8,128,1280]{2,1,0:T(8,128)(2,1)}, u32[]{:S(2)}) copy-start(bf16[8,128,1280]{2,1,0:T(8,128)(2,1)} %param.9) | copy-start | bytes 7864324
  224.0 21.3 %copy-start.54 = (f32[8,128]{1,0:T(8,128)S(1)}, f32[8,128]{1,0:T(8,128)}, u32[]{:S(2)}) copy-start(f32[8,128]{1,0:T(8,128)} %copy-done.53) | copy-start | bytes 12292
  224.0 21.3 %copy-start.34 = (bf16[8,128,1280]{2,1,0:T(8,128)(2,1)S(1)}, bf16[8,128,1280]{2,1,0:T(8,128)(2,1)}, u32[]{:S(2)}) copy-start(bf16[8,128,1280]{2,1,0:T(8,128)(2,1)} %copy-done.33) | copy-start | bytes 7864324
  278.8 14.0 %copy-start.7 = (bf16[8,128,1280]{1,2,0:T(8,128)(2,1)S(1)}, bf16[8,128,1280]{1,2,0:T(8,128)(2,1)}, u32[]{:S(2)}) copy-start(bf16[8,128,1280]{1,2,0:T(8,128)(2,1)} %copy.78) | copy-start | bytes 7864324
  292.8 6.3 copy-start.57
  292.8 13.4 %slice-start.2 = ((s8[6553600]{0:T(1024)(128)(4,1)}), s8[2359296]{0:T(1024)(128)(4,1)S(1)}, s32[]{:S(2)}) async-start(s8[6553600]{0:T(1024)(128)(4,1)} %bitcast.291), calls=%async_computation.12 | async-start | bytes 4718592
  299.1 12.6 copy-start.27
  299.1 7.1 slice-start.3
  299.1 7.1 copy-start.59
  299.2 12.5 slice-start.8
  311.7 6.5 copy-start.52
  311.7 6.5 copy-start.18
  311.7 6.5 copy-start.48
  324.6 9.1 copy-start.29
  324.6 9.1 copy-start.58
  333.6 5.7 copy-start.60
  339.4 5.5 copy-start.19
  339.4 5.5 copy-start.26
  447.3 587.7 %all-gather.21.cloned.1.call-start = ((), (), s32[]{:S(2)}) async-start(), calls=%async_computation.5 | async-start | bytes 6963200 | tf_op jit(solution)/shard_map/all_gather | solution.py:165
  448.0 594.3 %all-gather.17.cloned.1.call-start = ((), (), s32[]{:S(2)}) async-start(), calls=%async_computation.3 | async-start | bytes 6963200 | tf_op jit(solution)/shard_map/all_gather | solution.py:165
  448.8 600.9 %all-gather.13.cloned.1.call-start = ((), (), s32[]{:S(2)}) async-start(), calls=%async_computation.1 | async-start | bytes 6963200 | tf_op jit(solution)/shard_map/all_gather | solution.py:165
  449.3 607.6 %all-gather.23.cloned.1.call-start = ((), (), s32[]{:S(2)}) async-start(), calls=%async_computation.6 | async-start | bytes 6963200 | tf_op jit(solution)/shard_map/all_gather | solution.py:165
  449.4 32.0 %copy-start.10 = (bf16[8,128,1280]{2,1,0:T(8,128)(2,1)S(1)}, bf16[8,128,1280]{2,1,0:T(8,128)(2,1)}, u32[]{:S(2)}) copy-start(bf16[8,128,1280]{2,1,0:T(8,128)(2,1)} %copy-done.9) | copy-start | bytes 7864324
  481.4 21.6 %copy-start.50 = (f32[8,128]{1,0:T(8,128)S(1)}, f32[8,128]{1,0:T(8,128)}, u32[]{:S(2)}) copy-start(f32[8,128]{1,0:T(8,128)} %copy-done.49) | copy-start | bytes 12292
  481.4 21.6 %copy-start.15 = (bf16[8,128,1280]{2,1,0:T(8,128)(2,1)S(1)}, bf16[8,128,1280]{2,1,0:T(8,128)(2,1)}, u32[]{:S(2)}) copy-start(bf16[8,128,1280]{2,1,0:T(8,128)(2,1)} %get-tuple-element.30) | copy-start | bytes 7864324
  481.4 21.6 %copy-start.39 = (f32[8,128]{1,0:T(8,128)S(1)}, f32[8,128]{1,0:T(8,128)}, u32[]{:S(2)}) copy-start(f32[8,128]{1,0:T(8,128)} %copy-done.38) | copy-start | bytes 12292
  536.0 13.9 %copy-start.8 = (bf16[8,128,1280]{1,2,0:T(8,128)(2,1)S(1)}, bf16[8,128,1280]{1,2,0:T(8,128)(2,1)}, u32[]{:S(2)}) copy-start(bf16[8,128,1280]{1,2,0:T(8,128)(2,1)} %copy.85) | copy-start | bytes 7864324
  549.9 6.3 copy-start.61
  549.9 13.1 %slice-start.4 = ((s8[6553600]{0:T(1024)(128)(4,1)}), s8[2359296]{0:T(1024)(128)(4,1)S(1)}, s32[]{:S(2)}) async-start(s8[6553600]{0:T(1024)(128)(4,1)} %bitcast.293), calls=%async_computation.14 | async-start | bytes 4718592
  556.2 12.3 copy-start.28
  556.2 6.8 slice-start.5
  556.3 6.8 copy-start.63
  556.3 12.2 slice-start.10
  568.5 6.5 copy-start.42
  568.5 6.5 copy-start.21
  568.5 6.5 copy-start.46
  581.4 9.0 copy-start.30
  581.4 9.0 copy-start.62
  590.3 5.7 copy-start.64
  607.8 105.0 %copy-start.44 = (f32[8,128]{1,0:T(8,128)S(1)}, f32[8,128]{1,0:T(8,128)}, u32[]{:S(2)}) copy-start(f32[8,128]{1,0:T(8,128)} %copy-done.43) | copy-start | bytes 12292
  710.6 353.6 %all-gather.19.cloned.1.call-start = ((), (), s32[]{:S(2)}) async-start(), calls=%async_computation.4 | async-start | bytes 6963200 | tf_op jit(solution)/shard_map/all_gather | solution.py:165
  711.2 360.3 %all-gather.15.cloned.1.call-start = ((), (), s32[]{:S(2)}) async-start(), calls=%async_computation.2 | async-start | bytes 6963200 | tf_op jit(solution)/shard_map/all_gather | solution.py:165
  712.0 366.9 %all-gather.11.cloned.1.call-start = ((), (), s32[]{:S(2)}) async-start(), calls=%async_computation | async-start | bytes 6963200 | tf_op jit(solution)/shard_map/all_gather | solution.py:165
  712.7 22.7 %copy-start.32 = (bf16[8,128,1280]{2,1,0:T(8,128)(2,1)S(1)}, bf16[8,128,1280]{2,1,0:T(8,128)(2,1)}, u32[]{:S(2)}) copy-start(bf16[8,128,1280]{2,1,0:T(8,128)(2,1)} %param.9) | copy-start | bytes 7864324
  712.7 420.9 %all-gather.27.cloned.1.call-start = ((), (), s32[]{:S(2)}) async-start(), calls=%async_computation.8 | async-start | bytes 27852800 | tf_op jit(solution)/shard_map/all_gather | solution.py:165
  735.5 25.9 %copy-start.11 = (bf16[8,128,1280]{2,1,0:T(8,128)(2,1)S(1)}, bf16[8,128,1280]{2,1,0:T(8,128)(2,1)}, u32[]{:S(2)}) copy-start(bf16[8,128,1280]{2,1,0:T(8,128)(2,1)} %copy-done.9) | copy-start | bytes 7864324
  735.5 25.9 %copy-start.40 = (f32[8,128]{1,0:T(8,128)S(1)}, f32[8,128]{1,0:T(8,128)}, u32[]{:S(2)}) copy-start(f32[8,128]{1,0:T(8,128)} %copy-done.38) | copy-start | bytes 12292
  761.4 27.9 %copy-start.16 = (bf16[8,128,1280]{2,1,0:T(8,128)(2,1)S(1)}, bf16[8,128,1280]{2,1,0:T(8,128)(2,1)}, u32[]{:S(2)}) copy-start(bf16[8,128,1280]{2,1,0:T(8,128)(2,1)} %get-tuple-element.30) | copy-start | bytes 7864324
  1027.1 215.9 %all-gather.29.cloned.1.call-start = ((), (), s32[]{:S(2)}) async-start(), calls=%async_computation.9 | async-start | bytes 27852800 | tf_op jit(solution)/shard_map/all_gather | solution.py:165
  1243.0 25.1 %copy-start.6 = (f32[5120,1280]{1,0:T(8,128)S(1)}, f32[5120,1280]{1,0:T(8,128)}, u32[]{:S(2)}) copy-start(f32[5120,1280]{1,0:T(8,128)} %all-gather.29.cloned.1.call-done) | copy-start | bytes 78643200
  (23 other events, 80.6 us)
Sparse Core Ops, SparseCore 0:
  447.4 42.0 all-gather.24
  491.7 42.6 all-gather.20
  536.6 42.7 all-gather.16
  581.5 52.6 all-gather.12
  710.8 42.0 all-gather.22
  754.9 42.6 all-gather.18
  799.9 57.2 all-gather.14
  859.4 64.3 all-gather.10
  1027.2 106.3 all-gather.26
  1135.7 107.2 all-gather.28

commit v2 on v0

v2 whole, which is shorter than its diff:
```python
import functools
import jax, jax.numpy as jnp
from jax import lax
from jax.experimental import pallas as pl
from jax.experimental.pallas import tpu as pltpu
from jax.sharding import PartitionSpec as P

EPS = 1e-6
F32, BF16 = jnp.float32, jnp.bfloat16
TOK, D, FF, SEQ = 1024, 1280, 5120, 128
WB = 1280
NB = 256
PAIRS = 10
SLOTS = 2
MC, MCG, MCQ_, MCD_ = 128, 256, 256, 512
AHEAD = 1


def nn(a, b):
    return lax.dot_general(a, b, (((1,), (0,)), ((), ())), preferred_element_type=F32)


def nt(a, b):
    return lax.dot_general(a, b, (((1,), (1,)), ((), ())), preferred_element_type=F32)


def tn(a, b):
    return lax.dot_general(a, b, (((0,), (0,)), ((), ())), preferred_element_type=F32)


class Stage:
    def __init__(self, count, sub, start, step):
        self.count, self.sub, self.start, self.step = count, sub, start, step


def block_of(ref, row, col):
    return ref.at[pl.ds(row, D), pl.ds(col, WB)]


def run_stages(items, ring, sem):
    stages = [it for it in items if isinstance(it, Stage)]
    base, total = {}, 0
    for st in stages:
        base[id(st)] = total
        total += st.count * st.sub
    nxt = {id(a): b for a, b in zip(stages, stages[1:])}

    def begin(st, i, part, slot):
        for cond, src in st.start(i, part):
            if cond is None:
                pltpu.make_async_copy(src, ring.at[slot], sem.at[slot]).start()
            else:
                @pl.when(cond)
                def _():
                    pltpu.make_async_copy(src, ring.at[slot], sem.at[slot]).start()

    def wait(st, slot):
        pltpu.make_async_copy(st.start(0, 0)[0][1], ring.at[slot], sem.at[slot]).wait()

    flat = [(st, i, p) for st in stages for i in range(st.count) for p in range(st.sub)]
    for g in range(min(AHEAD, total)):
        st, i, p = flat[g]
        begin(st, i, p, g % SLOTS)
    for it in items:
        if not isinstance(it, Stage):
            it()
            continue
        st, n = it, it.count * it.sub

        def take(i, part, st=st, n=n):
            local = i * st.sub + part
            slot = lax.rem(base[id(st)] + local, SLOTS)
            wait(st, slot)
            ahead = local + AHEAD
            to = lax.rem(base[id(st)] + ahead, SLOTS)
            follow = nxt.get(id(st))
            inside = [None]

            @pl.when(ahead < n)
            def _():
                begin(st, ahead // st.sub, (part + AHEAD) % st.sub, to)
            if follow is not None:
                over = ahead - n

                @pl.when(over >= 0)
                def _():
                    if follow.sub == 1:
                        begin(follow, over, 0, to)
                    else:
                        for p in range(AHEAD):
                            @pl.when(over == p)
                            def _():
                                begin(follow, p // follow.sub, p % follow.sub, to)
            return slot

        if st.count == 1:
            st.step(0, functools.partial(take, 0))
        else:
            @pl.loop(0, st.count)
            def _(i):
                st.step(i, functools.partial(take, i))


C0 = 0.7978845608028654
C1 = C0 * 0.044715


def gelu(x):
    half = 0.5 * x
    return half * jnp.tanh(x * (C0 + C1 * (x * x))) + half


def gelu_grad(x, d):
    x2 = x * x
    t = jnp.tanh(x * (C0 + C1 * x2))
    return d * ((0.5 + 0.5 * t) + (x * (0.5 * C0 + 1.5 * C1 * x2)) * (1.0 - t * t))


def rms_rows(src, dst, rows=128):
    @pl.loop(0, TOK // rows)
    def _(i):
        r = pl.ds(pl.multiple_of(i * rows, rows), rows)
        x = src[r, :].astype(F32)
        dst[r, :] = (x * lax.rsqrt(jnp.mean(x * x, axis=-1, keepdims=True) + EPS)).astype(BF16)


def add_rms_rows(res, acc, out, dst, rows=128):
    @pl.loop(0, TOK // rows)
    def _(i):
        r = pl.ds(pl.multiple_of(i * rows, rows), rows)
        y = (res[r, :].astype(F32) + acc[r, :].astype(BF16).astype(F32)).astype(BF16)
        out[r, :] = y
        x = y.astype(F32)
        dst[r, :] = (x * lax.rsqrt(jnp.mean(x * x, axis=-1, keepdims=True) + EPS)).astype(BF16)


def rms_back_rows(x_ref, dy_acc, dres_ref, dst, rows=128):
    @pl.loop(0, TOK // rows)
    def _(i):
        r = pl.ds(pl.multiple_of(i * rows, rows), rows)
        x = x_ref[r, :].astype(F32)
        dy = dy_acc[r, :].astype(BF16).astype(F32)
        inv = lax.rsqrt(jnp.mean(x * x, axis=-1, keepdims=True) + EPS)
        dot = jnp.mean(dy * x, axis=-1, keepdims=True)
        dst[r, :] = (dres_ref[r, :].astype(F32) + (dy * inv - x * (inv * inv * inv * dot))).astype(BF16)


def lane_mask():
    return lax.broadcasted_iota(jnp.int32, (SEQ, 2 * 64), 1) < 64


def split_heads(x, mask):
    zero = jnp.zeros_like(x)
    return jnp.concatenate([jnp.where(mask, x, zero), jnp.where(mask, zero, x)], axis=0)


def attention_fwd(qkv, pt, mixed):
    mask = lane_mask()

    @pl.loop(0, TOK // SEQ)
    def _(s):
        rows = pl.ds(pl.multiple_of(s * SEQ, SEQ), SEQ)
        for h in range(PAIRS):
            lanes = lambda part: pl.ds(part * D + h * 128, 128)
            q, k, v = qkv[rows, lanes(0)], qkv[rows, lanes(1)], qkv[rows, lanes(2)]
            st = nt(k, split_heads(q, mask)) * 0.125
            e = jnp.exp(st - jnp.max(st, axis=0, keepdims=True))
            p = (e / jnp.sum(e, axis=0, keepdims=True)).astype(BF16)
            pt[s * PAIRS + h] = p
            o = tn(p, v)
            mixed[rows, pl.ds(h * 128, 128)] = jnp.where(mask, o[:SEQ], o[SEQ:]).astype(BF16)


def attention_bwd(qkv, pt, dmixed):
    mask = lane_mask()

    @pl.loop(0, TOK // SEQ)
    def _(s):
        rows = pl.ds(pl.multiple_of(s * SEQ, SEQ), SEQ)
        for h in range(PAIRS):
            lanes = lambda part: pl.ds(part * D + h * 128, 128)
            q, k, v = qkv[rows, lanes(0)], qkv[rows, lanes(1)], qkv[rows, lanes(2)]
            do = split_heads(dmixed[rows, pl.ds(h * 128, 128)], mask)
            p = pt[s * PAIRS + h]
            dp = nt(v, do).astype(BF16).astype(F32)
            pf = p.astype(F32)
            dot = jnp.sum(dp * pf, axis=0, keepdims=True)
            ds = (pf * (dp - dot) * 0.125).astype(BF16)
            dq = tn(ds, k)
            qkv[rows, lanes(0)] = jnp.where(mask, dq[:SEQ], dq[SEQ:]).astype(BF16)
            qkv[rows, lanes(1)] = nn(ds, split_heads(q, mask)).astype(BF16)
            qkv[rows, lanes(2)] = nn(p, do).astype(BF16)


def lane(i, width):
    return pl.ds(pl.multiple_of(i * width, 128), width)


class Saver:
    def __init__(self, sems):
        self.sems, self.n, self.open = sems, 0, {}

    def put(self, key, src, dst):
        cp = pltpu.make_async_copy(src, dst, self.sems.at[self.n])
        self.n += 1
        cp.start()
        self.open[key] = cp

    def done(self, *keys):
        for key in keys:
            if key in self.open:
                self.open.pop(key).wait()

    def finish(self):
        self.done(*list(self.open))


N_SAVE = 20


def front_kernel(x0, cot, wq, wk, wv, wo, w1, w2,
                 n0, qkv0, pt0, mx0, h0, nn0, pre0, act0, xmid, n1, dqkv1, mx1, nn1, act1, dpre1, dh1,
                 x, nrm, qkv, pt, mx, h, n2, big, g, acc, stg, ring, wsem, sems, stg_sem, in_sem):
    save = Saver(sems)
    cx = pltpu.make_async_copy(x0, x, in_sem.at[0])
    cg = pltpu.make_async_copy(cot, g, in_sem.at[1])
    cx.start()
    cg.start()

    def stage_wait(i, dst):
        @pl.when(i >= 2)
        def _():
            slot = lax.rem(i, 2)
            pltpu.make_async_copy(stg.at[slot], dst.at[:, pl.ds(0, D)], stg_sem.at[slot]).wait()

    def stage_put(i, dst):
        slot = lax.rem(i, 2)
        pltpu.make_async_copy(stg.at[slot], dst.at[:, lane(i, D)], stg_sem.at[slot]).start()

    def drain(dst):
        for slot in range(2):
            pltpu.make_async_copy(stg.at[slot], dst.at[:, pl.ds(0, D)], stg_sem.at[slot]).wait()

    MCQ, MCD = [[pl.ds(k * z, z) for k in range(TOK // z)] for z in (MCQ_, MCD_)]
    MGH = [pl.ds(k * MCG, MCG) for k in range(TOK // MCG)]
    MCH = [pl.ds(k * MC, MC) for k in range(TOK // MC)]
    subs = [pl.ds(j * NB, NB) for j in range(D // NB)]

    def sub(i, j):
        return pl.ds(pl.multiple_of(i * D + j * NB, NB), NB)

    def qkv_stage(layer):
        def start(i, part):
            return [(i == m, w.at[layer]) for m, w in enumerate((wq, wk, wv))]

        def step(i, take):
            slot = take(0)
            for j, c in enumerate(subs):
                for r in MCQ:
                    qkv[r, sub(i, j)] = nn(nrm[r, :], ring[slot, :, c]).astype(BF16)
        return Stage(3, 1, start, step)

    def proj_stage(layer):
        def step(i, take):
            slot = take(0)
            for c in subs:
                y = nn(mx[...], ring[slot, :, c]).astype(BF16).astype(F32)
                h[:, c] = (x[:, c].astype(F32) + y).astype(BF16)
        return Stage(1, 1, lambda i, part: [(None, wo.at[layer])], step)

    def up_stage(layer):
        to = pre0 if layer == 0 else act1

        def step(i, take):
            slot, half = take(0), lax.rem(i, 2)
            stage_wait(i, to)
            for j, c in enumerate(subs):
                for r in MCH:
                    pre = nn(n2[r, :], ring[slot, :, c]).astype(BF16)
                    act = gelu(pre.astype(F32)).astype(BF16)
                    big[r, sub(i, j)] = act if layer == 0 else pre
                    stg[half, r, c] = pre if layer == 0 else act
            stage_put(i, to)
        return Stage(4, 1, lambda i, part: [(None, w1.at[:, lane(i, D)])], step)

    def down_stage():
        def step(i, take):
            slot = take(0)

            @pl.when(i == 0)
            def _():
                for c in subs:
                    for r in MCD:
                        acc[r, c] = nn(big[r, lane(i, D)], ring[slot, :, c])

            @pl.when(i > 0)
            def _():
                for c in subs:
                    for r in MCD:
                        acc[r, c] += nn(big[r, lane(i, D)], ring[slot, :, c])
        return Stage(4, 1, lambda i, part: [(None, w2.at[lane(i, D)])], step)

    def dact_stage():
        def step(i, take):
            slot = take(0)
            for j, c in enumerate(subs):
                for r in MGH:
                    d = nt(g[r, :], ring[slot, c]).astype(BF16).astype(F32)
                    big[r, sub(i, j)] = gelu_grad(big[r, sub(i, j)].astype(F32), d).astype(BF16)
        return Stage(4, 1, lambda i, part: [(None, w2.at[lane(i, D)])], step)

    def dn2_stage():
        def step(i, take):
            slot = take(0)

            @pl.when(i == 0)
            def _():
                for c in subs:
                    for r in MCD:
                        acc[r, c] = nt(big[r, lane(i, D)], ring[slot, c])

            @pl.when(i > 0)
            def _():
                for c in subs:
                    for r in MCD:
                        acc[r, c] += nt(big[r, lane(i, D)], ring[slot, c])
        return Stage(4, 1, lambda i, part: [(None, w1.at[:, lane(i, D)])], step)

    def dmix_stage(layer, src, dst):
        def step(i, take):
            slot = take(0)
            for c in subs:
                dst[:, c] = nt(src[...], ring[slot, c]).astype(BF16)
        return Stage(1, 1, lambda i, part: [(None, wo.at[layer])], step)

    def first():
        cx.wait()
        rms_rows(x, nrm)
        save.put("nrm", nrm, n0)

    def attend0():
        save.put("qkv", qkv, qkv0)
        attention_fwd(qkv, pt, mx)
        save.put("pt", pt, pt0)
        save.put("mx", mx, mx0)

    def mid0():
        rms_rows(h, n2)
        save.put("h", h, h0)
        save.put("n2", n2, nn0)

    def after_up0():
        save.put("big", big, act0)
        drain(pre0)

    def second():
        save.done("nrm")
        add_rms_rows(h, acc, x, nrm)
        save.put("x", x, xmid)
        save.put("nrm", nrm, n1)
        save.done("qkv", "pt", "mx")

    def attend1():
        attention_fwd(qkv, pt, mx)
        save.put("mx", mx, mx1)
        save.done("h", "n2")

    def mid1():
        rms_rows(h, n2)
        save.put("n2", n2, nn1)
        save.done("big")

    def after_up1():
        drain(act1)
        cg.wait()

    def after_dact():
        save.put("big", big, dpre1)

    def after_dn2():
        save.done("x")
        rms_back_rows(h, acc, g, x)
        save.put("x", x, dh1)
        save.done("nrm")

    def last():
        attention_bwd(qkv, pt, nrm)
        save.put("qkv", qkv, dqkv1)
        save.finish()

    run_stages([first, qkv_stage(0), attend0, proj_stage(0), mid0, up_stage(0), after_up0, down_stage(), second,
                qkv_stage(1), attend1, proj_stage(1), mid1, up_stage(1), after_up1, dact_stage(), after_dact, dn2_stage(),
                after_dn2, dmix_stage(1, x, nrm), last], ring, wsem)


def front(x0, cot, wq, wk, wv, wo, w1, w2):
    td, t3, tf, tp = (TOK, D), (TOK, 3 * D), (TOK, FF), (TOK // SEQ * PAIRS, SEQ, 2 * SEQ)
    outs = [td, t3, tp, td, td, td, tf, tf, td, td, t3, td, td, tf, tf, td]
    return pl.pallas_call(
        front_kernel,
        out_shape=[jax.ShapeDtypeStruct(s, BF16) for s in outs],
        in_specs=[pl.BlockSpec(memory_space=pl.ANY)] * 8,
        out_specs=[pl.BlockSpec(memory_space=pl.ANY)] * len(outs),
        scratch_shapes=[pltpu.VMEM(td, BF16), pltpu.VMEM(td, BF16), pltpu.VMEM(t3, BF16), pltpu.VMEM(tp, BF16), pltpu.VMEM(td, BF16),
                        pltpu.VMEM(td, BF16), pltpu.VMEM(td, BF16), pltpu.VMEM(tf, BF16), pltpu.VMEM(td, BF16), pltpu.VMEM(td, F32),
                        pltpu.VMEM((2, TOK, D), BF16), pltpu.VMEM((SLOTS, D, D), BF16),
                        pltpu.SemaphoreType.DMA((SLOTS,)), pltpu.SemaphoreType.DMA((N_SAVE,)), pltpu.SemaphoreType.DMA((2,)),
                        pltpu.SemaphoreType.DMA((2,))],
        compiler_params=pltpu.CompilerParams(vmem_limit_bytes=67043328),
        name="front",
    )(x0.reshape(td), cot.reshape(td), wq, wk, wv, wo, w1, w2)


def mid_kernel(x0, xmid, h0, dh1, dqkv1, qkv0, pt0, pre0, wq, wk, wv, wo, w1, w2, _,
               dmid, dpre0, dh0, dqkv0, dx,
               x, h, g, t, dqkv, qkv, pt, big, acc, ring, wsem, sems, in_sem):
    save = Saver(sems)
    loads = {}
    for n, (key, src, dst) in enumerate([("dqkv", dqkv1, dqkv), ("x", xmid, x), ("t", dh1, t), ("big", pre0, big), ("h", h0, h),
                                         ("qkv", qkv0, qkv), ("pt", pt0, pt)]):
        loads[key] = pltpu.make_async_copy(src, dst, in_sem.at[n])
        loads[key].start()
    subs = [pl.ds(j * NB, NB) for j in range(D // NB)]
    MGH, MCD = [[pl.ds(k * z, z) for k in range(TOK // z)] for z in (MCG, MCD_)]

    def sub(i, j):
        return pl.ds(pl.multiple_of(i * D + j * NB, NB), NB)

    def sum_stage(count, start, src):
        def step(i, take):
            slot = take(0)

            @pl.when(i == 0)
            def _():
                for c in subs:
                    for r in MCD:
                        acc[r, c] = nt(src[r, lane(i, D)], ring[slot, c])

            @pl.when(i > 0)
            def _():
                for c in subs:
                    for r in MCD:
                        acc[r, c] += nt(src[r, lane(i, D)], ring[slot, c])
        return Stage(count, 1, start, step)

    def dn_stage(layer, src):
        return sum_stage(3, lambda i, part: [(i == m, w.at[layer]) for m, w in enumerate((wq, wk, wv))], src)

    def dact_stage():
        def step(i, take):
            slot = take(0)
            for j, c in enumerate(subs):
                for r in MGH:
                    d = nt(g[r, :], ring[slot, c]).astype(BF16).astype(F32)
                    big[r, sub(i, j)] = gelu_grad(big[r, sub(i, j)].astype(F32), d).astype(BF16)
        return Stage(4, 1, lambda i, part: [(None, w2.at[lane(i, D)])], step)

    def dmix_stage():
        def step(i, take):
            slot = take(0)
            for c in subs:
                x[:, c] = nt(t[...], ring[slot, c]).astype(BF16)
        return Stage(1, 1, lambda i, part: [(None, wo.at[0])], step)

    def first():
        loads["dqkv"].wait()

    def after_dn1():
        loads["x"].wait()
        loads["t"].wait()
        rms_back_rows(x, acc, t, g)
        save.put("g", g, dmid)
        loads["big"].wait()

    def after_dact():
        save.put("big", big, dpre0)
        loads["h"].wait()

    def after_dn2():
        rms_back_rows(h, acc, g, t)
        save.put("t", t, dh0)

    def attend():
        loads["qkv"].wait()
        loads["pt"].wait()
        attention_bwd(qkv, pt, x)
        save.put("qkv", qkv, dqkv0)
        again = pltpu.make_async_copy(x0, h, in_sem.at[0])
        again.start()
        again.wait()

    def last():
        save.done("g")
        rms_back_rows(h, acc, t, g)
        save.put("dx", g, dx)
        save.finish()

    run_stages([first, dn_stage(1, dqkv), after_dn1, dact_stage(), after_dact,
                sum_stage(4, lambda i, part: [(None, w1.at[:, lane(i, D)])], big), after_dn2, dmix_stage(), attend,
                dn_stage(0, qkv), last], ring, wsem)


def mid(x0, kept, wq, wk, wv, wo, w1, w2, after):
    td, t3, tf, tp = (TOK, D), (TOK, 3 * D), (TOK, FF), (TOK // SEQ * PAIRS, SEQ, 2 * SEQ)
    outs = [td, tf, td, t3, td]
    args = (x0.reshape(td), *kept, wq, wk, wv, wo, w1, w2, after)
    return pl.pallas_call(
        mid_kernel,
        out_shape=[jax.ShapeDtypeStruct(s, BF16) for s in outs],
        in_specs=[pl.BlockSpec(memory_space=pl.ANY)] * len(args),
        out_specs=[pl.BlockSpec(memory_space=pl.ANY)] * len(outs),
        scratch_shapes=[pltpu.VMEM(td, BF16)] * 4 + [pltpu.VMEM(t3, BF16), pltpu.VMEM(t3, BF16), pltpu.VMEM(tp, BF16),
                        pltpu.VMEM(tf, BF16), pltpu.VMEM(td, F32), pltpu.VMEM((SLOTS, D, D), BF16),
                        pltpu.SemaphoreType.DMA((SLOTS,)), pltpu.SemaphoreType.DMA((N_SAVE,)), pltpu.SemaphoreType.DMA((7,))],
        compiler_params=pltpu.CompilerParams(vmem_limit_bytes=67043328),
        cost_estimate=pl.CostEstimate(flops=100 * 10 ** 9, bytes_accessed=10 ** 8, transcendentals=0),
        name="mid",
    )(*args)


MESH = pl.DeviceIdType.MESH
ROWS, LANES = 40, 128
LAG = 2
TILES = 4
ORDERS = ("xyz", "yzx", "zxy")


def scatter_kernel(groups, n_tiles, depth, n_src, n_after, *refs):
    srcs, out_ref = refs[:n_src], refs[n_src + n_after]
    a_buf, b_buf, tiles, own, rc, r1, r2, r3, a_sem, b_sem, out_sem, send_sem, recv_sem = refs[n_src + n_after + 1:]
    me = lax.axis_index("data")
    bit = {"c": lax.rem(me, 2), "x": lax.rem(me // 2, 2), "y": lax.rem(me // 4, 2), "z": me // 8}
    step = {"c": 1, "x": 2, "y": 4, "z": 8}
    peer = {d: me + step[d] * (1 - 2 * bit[d]) for d in step}
    n_own, n_in = own.shape[1], rc.shape[1]
    n_chunks = 4 * n_tiles
    bufs = (rc, r1, r2, r3)

    def group_of(m):
        a = 0
        for first in groups[1:]:
            a = a + (m >= first[0]).astype(jnp.int32)
        return a

    def a_load(a, layer):
        return pltpu.make_async_copy(srcs[groups[a][1][layer]].at[:, pl.ds(groups[a][2], D)], a_buf.at[a % 2, layer], a_sem.at[a % 2, layer])

    def b_load(a, m, layer, first=None):
        col = pl.multiple_of(groups[a][4] + (m - groups[a][0]) * NB, NB) if first is None else first
        slot = lax.rem(m, 2)
        return pltpu.make_async_copy(srcs[groups[a][3][layer]].at[:, pl.ds(col, NB)], b_buf.at[slot, layer], b_sem.at[slot, layer])

    def in_group(a, m, fn):
        last = groups[a + 1][0] if a + 1 < len(groups) else n_tiles

        @pl.when(jnp.logical_and(m >= groups[a][0], m < last))
        def _():
            fn()

    def b_start(m):
        for a in range(len(groups)):
            def go(a=a):
                for layer in range(depth):
                    b_load(a, m, layer).start()
            in_group(a, m, go)

    def produce(m):
        for layer in range(depth):
            b_load(0, m, layer, 0).wait()
        for a in range(len(groups)):
            @pl.when(m == groups[a][0])
            def _():
                for layer in range(depth):
                    a_load(a, layer).wait()
                if a + 1 < len(groups):
                    for layer in range(depth):
                        a_load(a + 1, layer).start()
        b_start(m + 1)
        half, slot, to = lax.rem(group_of(m), 2), lax.rem(m, 2), lax.rem(m, TILES)
        for z in range(2):
            tot = None
            for layer in range(depth):
                y = tn(a_buf[half, layer, :, pl.ds(z * 640, 640)], b_buf[slot, layer])
                tot = y if tot is None else tot + y
            tiles[to, z] = tot.reshape(2, 2, 2, 2 * ROWS, NB)

    def pick(color, stage, other):
        idx = {"z": slice(None), "y": slice(None), "x": slice(None)}
        for s in range(stage):
            d = ORDERS[color][s]
            idx[d] = 1 - bit[d] if (other and s == stage - 1) else bit[d]
        return tuple(idx[d] for d in "zyx")

    def piece(k):
        sub = lax.rem(k, 4)
        return (lax.rem(k // 4, TILES), pl.multiple_of(lax.rem(sub, 2) * ROWS, 8), pl.multiple_of((sub // 2) * LANES, LANES))

    def send(color, stage, j):
        slot, so = lax.rem(j, n_in), lax.rem(j, n_own)
        if stage == 0:
            tile, row, col = piece(3 * j + color)
            src, to = tiles.at[tile, :, :, :, 1 - bit["c"], pl.ds(row, ROWS), pl.ds(col, LANES)], peer["c"]
        else:
            src, to = own.at[(color, so) + pick(color, stage, True)], peer[ORDERS[color][stage - 1]]
        return pltpu.make_async_remote_copy(src, bufs[stage].at[color, slot], send_sem.at[color, stage, slot],
                                            recv_sem.at[color, stage, slot], device_id=(to,), device_id_type=MESH)

    def store(color, j):
        so, k = lax.rem(j, n_own), 3 * j + color
        _, row, col = piece(k)
        col = pl.multiple_of((k // 4) * NB + col, LANES)
        return pltpu.make_async_copy(own.at[(color, so) + pick(color, 3, False)],
                                     out_ref.at[pl.ds(row, ROWS), pl.ds(col, LANES)], out_sem.at[color, so])

    def live(j, color):
        return jnp.logical_and(j >= 0, 3 * j + color < n_chunks)

    def tick(t, carry):
        for color in range(3):
            j = t - 4 * LAG - 1

            @pl.when(live(j, color))
            def _():
                store(color, j).wait()
        for stage in (3, 2, 1, 0):
            j = t - (stage + 1) * LAG
            for color in range(3):
                @pl.when(live(j, color))
                def _():
                    slot, so = lax.rem(j, n_in), lax.rem(j, n_own)
                    copy = send(color, stage, j)
                    copy.wait_send()
                    copy.wait_recv()
                    keep = (color, so) + pick(color, stage, False)
                    if stage == 0:
                        tile, row, col = piece(3 * j + color)
                        mine = tiles[tile, :, :, :, bit["c"], pl.ds(row, ROWS), pl.ds(col, LANES)]
                    else:
                        mine = own[keep]
                    own[keep] = mine + bufs[stage][color, slot]
                    if stage < 3:
                        send(color, stage + 1, j).start()
                    else:
                        store(color, j).start()
        for color in range(3):
            @pl.when(live(t, color))
            def _():
                send(color, 0, t).start()
        m = (3 * t + 5) // 4

        @pl.when(jnp.logical_and(m != (3 * t + 2) // 4, m < n_tiles))
        def _():
            produce(m)
        return carry

    for layer in range(depth):
        a_load(0, layer).start()
    b_start(jnp.int32(0))
    barrier = pltpu.get_barrier_semaphore()
    for d in "cxyz":
        pl.semaphore_signal(barrier, inc=1, device_id=(peer[d],), device_id_type=MESH)
    pl.semaphore_wait(barrier, 4)
    produce(jnp.int32(0))
    lax.fori_loop(0, pl.cdiv(n_chunks, 3) + 4 * LAG + 1, tick, 0)


def scatter_sum(srcs, groups, n_tiles, collective_id, after=()):
    depth = len(groups[0][1])
    n_own, n_in, blk = 4 * LAG + 2, 2 * LAG, (ROWS, LANES)
    size = D * NB * n_tiles * 4
    return pl.pallas_call(
        functools.partial(scatter_kernel, groups, n_tiles, depth, len(srcs), len(after)),
        out_shape=jax.ShapeDtypeStruct((2 * ROWS, NB * n_tiles), F32),
        in_specs=[pl.BlockSpec(memory_space=pl.ANY)] * (len(srcs) + len(after)),
        out_specs=pl.BlockSpec(memory_space=pl.ANY),
        scratch_shapes=[
            pltpu.VMEM((2, depth, TOK, D), BF16), pltpu.VMEM((2, depth, TOK, NB), BF16),
            pltpu.VMEM((TILES, 2, 2, 2, 2, 2 * ROWS, NB), F32),
            pltpu.VMEM((3, n_own, 2, 2, 2) + blk, F32), pltpu.VMEM((3, n_in, 2, 2, 2) + blk, F32),
            pltpu.VMEM((3, n_in, 2, 2) + blk, F32), pltpu.VMEM((3, n_in, 2) + blk, F32), pltpu.VMEM((3, n_in) + blk, F32),
            pltpu.SemaphoreType.DMA((2, depth)), pltpu.SemaphoreType.DMA((2, depth)), pltpu.SemaphoreType.DMA((3, n_own)),
            pltpu.SemaphoreType.DMA((3, 4, n_in)), pltpu.SemaphoreType.DMA((3, 4, n_in))],
        compiler_params=pltpu.CompilerParams(collective_id=collective_id, has_side_effects=True, vmem_limit_bytes=67043328),
        cost_estimate=pl.CostEstimate(flops=size * 4000, bytes_accessed=2 * size, transcendentals=0),
        name=f"scatter_sum_{collective_id}",
    )(*srcs, *after)


def gather(shard):
    return lax.all_gather(shard, "data", axis=0, tiled=True)


def place_attention(full, layer, dst):
    rows = 160

    def kernel(src, *refs):
        for n, out in enumerate(refs[-4:]):
            out[0] = src[:, n * D:(n + 1) * D]

    dst = dst or ()
    return pl.pallas_call(
        kernel,
        grid=(D // rows,),
        out_shape=[jax.ShapeDtypeStruct((2, D, D), F32)] * 4,
        in_specs=[pl.BlockSpec((rows, 4 * D), lambda i: (i, 0))] + [pl.BlockSpec(memory_space=pl.ANY)] * len(dst),
        out_specs=[pl.BlockSpec((1, rows, D), lambda i: (layer, i, 0))] * 4,
        input_output_aliases={n + 1: n for n in range(len(dst))},
        compiler_params=pltpu.CompilerParams(vmem_limit_bytes=60 << 20),
        cost_estimate=pl.CostEstimate(flops=D * D, bytes_accessed=32 * D * D, transcendentals=0),
        name=f"place_attention_{layer}",
    )(full, *dst)


def place_up(full, after):
    rows = 160
    return pl.pallas_call(
        lambda src, _, out: out.__setitem__(Ellipsis, src[...]),
        grid=(D // rows,),
        out_shape=jax.ShapeDtypeStruct((D, FF), F32),
        in_specs=[pl.BlockSpec((rows, FF), lambda i: (i, 0)), pl.BlockSpec(memory_space=pl.ANY)],
        out_specs=pl.BlockSpec((rows, FF), lambda i: (i, 0)),
        compiler_params=pltpu.CompilerParams(vmem_limit_bytes=60 << 20),
        cost_estimate=pl.CostEstimate(flops=D * D, bytes_accessed=32 * D * D, transcendentals=0),
        name="place_up",
    )(full, after)


def place_down(full, first, dst, after):
    rows = 640
    per, quarters = D // rows, full.shape[1] // D
    behind = (after,) if dst is None else (dst,)
    return pl.pallas_call(
        lambda src, _, out: out.__setitem__(Ellipsis, src[...]),
        grid=(quarters, per),
        out_shape=jax.ShapeDtypeStruct((FF, D), F32),
        in_specs=[pl.BlockSpec((rows, D), lambda q, i: (i, q)), pl.BlockSpec(memory_space=pl.ANY)],
        out_specs=pl.BlockSpec((rows, D), lambda q, i: ((first + q) * per + i, 0)),
        input_output_aliases={} if dst is None else {1: 0},
        compiler_params=pltpu.CompilerParams(vmem_limit_bytes=60 << 20),
        cost_estimate=pl.CostEstimate(flops=D * D, bytes_accessed=8 * quarters * D * D, transcendentals=0),
        name=f"place_down_{first}",
    )(full, *behind)


def solution(mesh):
    def local_step(x_init, cot_out, w_query, w_key, w_value, w_proj, w_up, w_down):
        weights = (w_query, w_key, w_value, w_proj, w_up, w_down)
        (n0, qkv0, pt0, mx0, h0, nn0, pre0, act0, xmid, n1, dqkv1, mx1, nn1, act1, dpre1, dh1) = front(x_init, cot_out, *weights)
        attention = ((0, (0,), 0, (1,), 0), (15, (2,), 0, (3,), 0))
        shard1 = scatter_sum((n1, dqkv1, mx1, dh1), attention, 20, 1)
        full1 = gather(shard1)
        dmid, dpre0, dh0, dqkv0, dx = mid(x_init, (xmid, h0, dh1, dqkv1, qkv0, pt0, pre0), *weights, shard1)
        shard0 = scatter_sum((n0, dqkv0, mx0, dh0), attention, 20, 2)
        full0 = gather(shard0)
        cot = cot_out.reshape(TOK, D)
        up = ((0, (0, 1), 0, (2, 3), 0),)
        shard_up = scatter_sum((nn0, nn1, dpre0, dpre1), up, 20, 3, (shard0,))
        full_up = gather(shard_up)
        down = [tuple((5 * n, (0, 1), q * D, (2, 3), 0) for n, q in enumerate(qs)) for qs in ((0, 1, 2), (3,))]
        shard_a = scatter_sum((act0, act1, dmid, cot), down[0], 15, 4, (shard_up,))
        full_a = gather(shard_a)
        shard_b = scatter_sum((act0, act1, dmid, cot), down[1], 5, 5, (shard_a,))
        full_b = gather(shard_b)
        attn = place_attention(full0, 0, place_attention(full1, 1, None))
        g_up = place_up(full_up, attn[0])
        g_down = place_down(full_b, 3, place_down(full_a, 0, None, g_up), None)
        return (*attn, g_up, g_down, dx.reshape(x_init.shape))

    data_spec = P("data")
    full_spec = P()
    in_specs = (data_spec, data_spec, full_spec, full_spec, full_spec, full_spec, full_spec, full_spec)
    out_specs = (full_spec, full_spec, full_spec, full_spec, full_spec, full_spec, data_spec)
    return jax.shard_map(local_step, mesh=mesh, in_specs=in_specs, out_specs=out_specs, check_vma=False)
```

time: 1580 us -> 963 us (0.61)
  Pallas kernels: 0 us -> 873 us
  waiting for transfers between devices: 884 us -> 67.7 us
  matrix products: 539 us -> 0 us
  local copies, waits for them, and re-layouts: 72.9 us -> 0 us
  other arithmetic: 62.1 us -> 0 us
    psum x1 -> x0, waiting for transfers between devices: 884 us -> none  [local_step(): lax.psum((attn_part, up_part, down_part), 'data')]
    pallas_call x0 -> x12, Pallas kernels: none -> 873 us  [the longest x5 531 us: scatter_sum(): pl.pallas_call(functools.partial(scatter_kernel, groups, n_tiles, depth,...]
    dot_general x45 -> x0, matrix products: 517 us -> none  [product(): return jnp.einsum(subscripts, lhs, rhs, preferred_element_type=jnp.float32)]
    all_gather x0 -> x5, waiting for transfers between devices: none -> 67.6 us  [gather(): return lax.all_gather(shard, 'data', axis=0, tiled=True)]
    unnamed x150 -> x0, local copies, waits for them, and re-layouts: 41.1 us -> none
    another operation x2 -> x0, other arithmetic: 36.7 us -> none  [the longest x1 18.5 us: local_step(): g_query = jnp.stack([part[0] for part in attn_grads])]
    convert_element_type x8 -> x0, local copies, waits for them, and re-layouts: 31.7 us -> none  [the longest x2 8.98 us: layer_backward(): product('bse,de->bsd', d_hidden, w_proj).astype(jnp.bfloat16)]
    convert_element_type x6 -> x0, other arithmetic: 23 us -> none  [the longest x2 11.4 us: layer_forward(): probs = jax.nn.softmax(scores, axis=-1).astype(jnp.bfloat16)]
  transfers between devices with their start and end apart: 1 -> 5, of which waited for: 1 -> 2; matrix products, arithmetic and copies ran while one was open for 2% -> 0% of each run, Pallas kernels for 0% -> 63%
where the time goes in v2:
time: 963 us; the launch traced here: 955 us
  Pallas kernels  873 us (91%)
  waiting for transfers between devices  67.7 us (7%)
  between operations  14.3 us (1%)
    pallas_call x5, Pallas kernels, scatter_sum(): pl.pallas_call(functools.partial(scatter_kernel, groups, n_tiles, depth,...  531 us
    pallas_call x1, Pallas kernels, front(): pl.pallas_call(front_kernel, out_shape=[jax.ShapeDtypeStruct(s, BF16) for...  165 us
    pallas_call x1, Pallas kernels, mid(): pl.pallas_call(mid_kernel, out_shape=[jax.ShapeDtypeStruct(s, BF16) for s...  101 us
    all_gather x5, waiting for transfers between devices, gather(): return lax.all_gather(shard, 'data', axis=0, tiled=True)  67.6 us
    pallas_call x2, Pallas kernels, place_attention(): pl.pallas_call(kernel, grid=(D // rows,), out_shape=[jax.ShapeDtypeStruct...  37.6 us
  transfers between devices with their start and end apart: 5, of which 2 were waited for; matrix products, arithmetic and copies ran while one was open for 0% of the time, Pallas kernels for 63%

profile of v2, /device:TPU:0, one launch (start us, length us, event | category | flops | bytes accessed | tf_op | source)
XLA Modules:
  0.0 955.2 jit_solution(5613498357076464443)
XLA Ops:
  7.2 0.0 all-gather.8.cloned.1.call-start
  7.2 164.9 %front.1 = (bf16[1024,1280]{1,0:T(8,128)(2,1)}, bf16[1024,3840]{1,0:T(8,128)(2,1)}, bf16[80,128,256]{2,1,0:T(8,128)(2,1)}, bf16[1024,1280]{1,0:T(8,128)(2,1)}, b...) custom-call(bf16[1024,1280]{1,0:T(8,128)(2,1)} %bitcast.3, ...), custom_call_target="tpu_custom_call" | custom-call | tf_op jit(solution)/shard_map/front/pallas_call | solution.py:399
  172.1 98.9 %scatter_sum_1.1._ = f32[80,5120]{1,0:T(8,128)} custom-call(bf16[1024,1280]{1,0:T(8,128)(2,1)} %get-tuple-element.44.refs_0_, bf16[1024,3840]{1,0:T(8,128)(2,1)} %get-tuple-element.40.refs_1_.dqkv1, bf16[1024,1280]{1,0:T(8,128)(2,1)} %get-tuple-element.45.refs_2_, bf16[1024,1280]{1,0:T(8,128)(2,1)} %get-tuple-element.39.refs_3_.dh1), custom_call_target="tpu_custom_call" | custom-call | flops 104857600000 | bytes 52428800 | tf_op jit(solution)/shard_map/scatter_sum_1/pallas_call | solution.py:671
  271.0 0.0 all-gather.8.cloned.1.call-update
  271.0 0.0 all-gather.6.cloned.1.call-start
  271.1 101.4 %mid.1 = (bf16[1024,1280]{1,0:T(8,128)(2,1)}, bf16[1024,5120]{1,0:T(8,128)(2,1)}, bf16[1024,1280]{1,0:T(8,128)(2,1)}, bf16[1024,3840]{1,0:T(8,128)(2,1)}, bf16[1024,1280]{1,0:T(8,128)(2,1)}) custom-call(bf16[1024,1280]{1,0:T(8,128)(2,1)} %bitcast.4, bf16[1024,1280]{1,0:T(8,128)(2,1)} %get-tuple-element.37.xmid, bf16[1024,1280]{1,0:T(8,128)(2,1)} %get-tuple-element.38.h0, ...), custom_call_target="tpu_custom_call" | custom-call | flops 99999997952 | bytes 100000000 | tf_op jit(solution)/shard_map/mid/pallas_call | solution.py:507
  372.5 95.6 %scatter_sum_2.1.refs_4_ = f32[80,5120]{1,0:T(8,128)} custom-call(bf16[1024,1280]{1,0:T(8,128)(2,1)} %get-tuple-element.36.refs_0_, bf16[1024,3840]{1,0:T(8,128)(2,1)} %get-tuple-element.46.refs_1_, bf16[1024,1280]{1,0:T(8,128)(2,1)} %get-tuple-element.47.refs_2_, bf16[1024,1280]{1,0:T(8,128)(2,1)} %get-tuple-element.48.refs_3_), custom_call_target="tpu_custom_call" | custom-call | flops 104857600000 | bytes 52428800 | tf_op jit(solution)/shard_map/scatter_sum_2/pallas_call | solution.py:671
  468.0 0.0 all-gather.6.cloned.1.call-update
  468.1 0.0 all-gather.10.cloned.1.call-start
  468.1 164.7 %scatter_sum_3.1.refs_4_ = f32[80,5120]{1,0:T(8,128)} custom-call(bf16[1024,1280]{1,0:T(8,128)(2,1)} %get-tuple-element.57.refs_0_, bf16[1024,1280]{1,0:T(8,128)(2,1)} %get-tuple-element.58.refs_1_, bf16[1024,5120]{1,0:T(8,128)(2,1)} %get-tuple-element.59.refs_2_, bf16[1024,5120]{1,0:T(8,128)(2,1)} %get-tuple-element.60.refs_3_, f32[80,5120]{1,0:T(8,128)} %scatter_sum_2.1.refs_4_), custom_call_target="tpu_custom_call" | custom-call | flops 104857600000 | bytes 52428800 | tf_op jit(solution)/shard_map/scatter_sum_3/pallas_call | solution.py:671
  632.8 0.0 all-gather.10.cloned.1.call-update
  632.8 0.3 all-gather.14.cloned.1.call-start
  633.1 115.3 %scatter_sum_4.1.refs_4_ = f32[80,3840]{1,0:T(8,128)} custom-call(bf16[1024,5120]{1,0:T(8,128)(2,1)} %get-tuple-element.61.refs_0_, bf16[1024,5120]{1,0:T(8,128)(2,1)} %get-tuple-element.62.refs_1_, bf16[1024,1280]{1,0:T(8,128)(2,1)} %get-tuple-element.63.refs_2_, bf16[1024,1280]{1,0:T(8,128)(2,1)} %bitcast.6, f32[80,5120]{1,0:T(8,128)} %scatter_sum_3.1.refs_4_), custom_call_target="tpu_custom_call" | custom-call | flops 78643200000 | bytes 39321600 | tf_op jit(solution)/shard_map/scatter_sum_4/pallas_call | solution.py:671
  748.4 0.0 all-gather.14.cloned.1.call-update
  748.4 0.0 all-gather.12.cloned.1.call-start
  748.5 56.5 %scatter_sum_5.1 = f32[80,1280]{1,0:T(8,128)} custom-call(bf16[1024,5120]{1,0:T(8,128)(2,1)} %get-tuple-element.61.refs_0_, bf16[1024,5120]{1,0:T(8,128)(2,1)} %get-tuple-element.62.refs_1_, bf16[1024,1280]{1,0:T(8,128)(2,1)} %get-tuple-element.63.refs_2_, bf16[1024,1280]{1,0:T(8,128)(2,1)} %bitcast.7, f32[80,3840]{1,0:T(8,128)} %scatter_sum_4.1.refs_4_), custom_call_target="tpu_custom_call" | custom-call | flops 26214400000 | bytes 13107200 | tf_op jit(solution)/shard_map/scatter_sum_5/pallas_call | solution.py:671
  805.0 0.0 all-gather.12.cloned.1.call-update
  805.0 0.0 all-gather.8.cloned.1.call-done.src
  805.1 18.8 %place_attention_1.1 = (f32[2,1280,1280]{2,1,0:T(8,128)}, f32[2,1280,1280]{2,1,0:T(8,128)}, f32[2,1280,1280]{2,1,0:T(8,128)}, f32[2,1280,1280]{2,1,0:T(8,128)}) custom-call(f32[1280,5120]{1,0:T(8,128)} %all-gather.8.cloned.1.call-done.src), custom_call_target="tpu_custom_call" | custom-call | flops 1638400 | bytes 52428800 | tf_op jit(solution)/shard_map/place_attention_1/pallas_call | solution.py:701
  823.8 0.0 all-gather.6.cloned.1.call-done.src
  823.8 18.8 %place_attention_0.1 = (f32[2,1280,1280]{2,1,0:T(8,128)}, f32[2,1280,1280]{2,1,0:T(8,128)}, f32[2,1280,1280]{2,1,0:T(8,128)}, f32[2,1280,1280]{2,1,0:T(8,128)}) custom-call(f32[1280,5120]{1,0:T(8,128)} %all-gather.6.cloned.1.call-done.src, ...), custom_call_target="tpu_custom_call", output_to_operand_aliasing={{0}: (1, {}), {1}: (2, {}), {2}: (3, {}), {3}: (4, {})} | custom-call | flops 1638400 | bytes 52428800 | tf_op jit(solution)/shard_map/place_attention_0/pallas_call | solution.py:701
  842.6 0.0 all-gather.10.cloned.1.call-done.src
  842.6 18.8 %place_up.1._ = f32[1280,5120]{1,0:T(8,128)} custom-call(f32[1280,5120]{1,0:T(8,128)} %all-gather.10.cloned.1.call-done.src, f32[2,1280,1280]{2,1,0:T(8,128)} %get-tuple-element.29._), custom_call_target="tpu_custom_call" | custom-call | flops 1638400 | bytes 52428800 | tf_op jit(solution)/shard_map/place_up/pallas_call | solution.py:716
  861.4 37.0 %all-gather.14.cloned.1.call-done.src = f32[1280,3840]{1,0:T(8,128)} async-done(((f32[80,3840]{1,0:T(8,128)}), f32[1280,3840]{1,0:T(8,128)}) %all-gather.14.cloned.1.call-update) | async-done | bytes 19660816 | tf_op jit(solution)/shard_map/all_gather | solution.py:690
  898.5 14.3 %place_down_0.1._ = f32[5120,1280]{1,0:T(8,128)} custom-call(f32[1280,3840]{1,0:T(8,128)} %all-gather.14.cloned.1.call-done.src, f32[1280,5120]{1,0:T(8,128)} %place_up.1._), custom_call_target="tpu_custom_call" | custom-call | flops 1638400 | bytes 39321600 | tf_op jit(solution)/shard_map/place_down_0/pallas_call | solution.py:732
  912.7 30.6 %all-gather.12.cloned.1.call-done.src = f32[1280,1280]{1,0:T(8,128)} async-done(((f32[80,1280]{1,0:T(8,128)}), f32[1280,1280]{1,0:T(8,128)}) %all-gather.12.cloned.1.call-update) | async-done | bytes 6553616 | tf_op jit(solution)/shard_map/all_gather | solution.py:690
  943.3 4.9 place_down_3.1
Async XLA Ops:
  7.2 797.9 %all-gather.8.cloned.1.call-start = ((), (), s32[]{:S(2)}) async-start(), calls=%async_computation.1 | async-start | bytes 27852800 | tf_op jit(solution)/shard_map/all_gather | solution.py:690
  271.0 552.8 %all-gather.6.cloned.1.call-start = ((), (), s32[]{:S(2)}) async-start(), calls=%async_computation | async-start | bytes 27852800 | tf_op jit(solution)/shard_map/all_gather | solution.py:690
  468.1 374.5 %all-gather.10.cloned.1.call-start = ((), (), s32[]{:S(2)}) async-start(), calls=%async_computation.2 | async-start | bytes 27852800 | tf_op jit(solution)/shard_map/all_gather | solution.py:690
  632.8 265.7 %all-gather.14.cloned.1.call-start = ((), (), s32[]{:S(2)}) async-start(), calls=%async_computation.4 | async-start | bytes 20889600 | tf_op jit(solution)/shard_map/all_gather | solution.py:690
  748.4 194.9 %all-gather.12.cloned.1.call-start = ((), (), s32[]{:S(2)}) async-start(), calls=%async_computation.3 | async-start | bytes 6963200 | tf_op jit(solution)/shard_map/all_gather | solution.py:690
Sparse Core Ops, SparseCore 0:
  271.1 107.2 all-gather.7
  468.2 176.6 all-gather.5
  647.1 163.9 all-gather.9
  813.2 85.2 all-gather.13
  900.6 42.6 all-gather.11

commit v3 on v2

v3 whole, which is shorter than its diff:
```python
import functools
import jax, jax.numpy as jnp
from jax import lax
from jax.experimental import pallas as pl
from jax.experimental.pallas import tpu as pltpu
from jax.sharding import PartitionSpec as P

EPS = 1e-6
F32, BF16 = jnp.float32, jnp.bfloat16
TOK, D, FF, SEQ = 1024, 1280, 5120, 128
WB = 1280
NB = 256
PAIRS = 10
SLOTS = 2
MC, MCG, MCQ_, MCD_ = 128, 256, 256, 512
AHEAD = 1


def nn(a, b):
    return lax.dot_general(a, b, (((1,), (0,)), ((), ())), preferred_element_type=F32)


def nt(a, b):
    return lax.dot_general(a, b, (((1,), (1,)), ((), ())), preferred_element_type=F32)


def tn(a, b):
    return lax.dot_general(a, b, (((0,), (0,)), ((), ())), preferred_element_type=F32)


class Stage:
    def __init__(self, count, sub, start, step):
        self.count, self.sub, self.start, self.step = count, sub, start, step


def block_of(ref, row, col):
    return ref.at[pl.ds(row, D), pl.ds(col, WB)]


def run_stages(items, ring, sem):
    stages = [it for it in items if isinstance(it, Stage)]
    base, total = {}, 0
    for st in stages:
        base[id(st)] = total
        total += st.count * st.sub
    nxt = {id(a): b for a, b in zip(stages, stages[1:])}

    def begin(st, i, part, slot):
        for cond, src in st.start(i, part):
            if cond is None:
                pltpu.make_async_copy(src, ring.at[slot], sem.at[slot]).start()
            else:
                @pl.when(cond)
                def _():
                    pltpu.make_async_copy(src, ring.at[slot], sem.at[slot]).start()

    def wait(st, slot):
        pltpu.make_async_copy(st.start(0, 0)[0][1], ring.at[slot], sem.at[slot]).wait()

    flat = [(st, i, p) for st in stages for i in range(st.count) for p in range(st.sub)]
    for g in range(min(AHEAD, total)):
        st, i, p = flat[g]
        begin(st, i, p, g % SLOTS)
    for it in items:
        if not isinstance(it, Stage):
            it()
            continue
        st, n = it, it.count * it.sub

        def take(i, part, st=st, n=n):
            local = i * st.sub + part
            slot = lax.rem(base[id(st)] + local, SLOTS)
            wait(st, slot)
            ahead = local + AHEAD
            to = lax.rem(base[id(st)] + ahead, SLOTS)
            follow = nxt.get(id(st))
            inside = [None]

            @pl.when(ahead < n)
            def _():
                begin(st, ahead // st.sub, (part + AHEAD) % st.sub, to)
            if follow is not None:
                over = ahead - n

                @pl.when(over >= 0)
                def _():
                    if follow.sub == 1:
                        begin(follow, over, 0, to)
                    else:
                        for p in range(AHEAD):
                            @pl.when(over == p)
                            def _():
                                begin(follow, p // follow.sub, p % follow.sub, to)
            return slot

        if st.count == 1:
            st.step(0, functools.partial(take, 0))
        else:
            @pl.loop(0, st.count)
            def _(i):
                st.step(i, functools.partial(take, i))


C0 = 0.7978845608028654
C1 = C0 * 0.044715


def gelu(x):
    half = 0.5 * x
    return half * jnp.tanh(x * (C0 + C1 * (x * x))) + half


def gelu_grad(x, d):
    x2 = x * x
    t = jnp.tanh(x * (C0 + C1 * x2))
    return d * ((0.5 + 0.5 * t) + (x * (0.5 * C0 + 1.5 * C1 * x2)) * (1.0 - t * t))


def rms_rows(src, dst, rows=128):
    @pl.loop(0, TOK // rows)
    def _(i):
        r = pl.ds(pl.multiple_of(i * rows, rows), rows)
        x = src[r, :].astype(F32)
        dst[r, :] = (x * lax.rsqrt(jnp.mean(x * x, axis=-1, keepdims=True) + EPS)).astype(BF16)


def add_rms_rows(res, acc, out, dst, rows=128):
    @pl.loop(0, TOK // rows)
    def _(i):
        r = pl.ds(pl.multiple_of(i * rows, rows), rows)
        y = (res[r, :].astype(F32) + acc[r, :].astype(BF16).astype(F32)).astype(BF16)
        out[r, :] = y
        x = y.astype(F32)
        dst[r, :] = (x * lax.rsqrt(jnp.mean(x * x, axis=-1, keepdims=True) + EPS)).astype(BF16)


def rms_back_rows(x_ref, dy_acc, dres_ref, dst, rows=128):
    @pl.loop(0, TOK // rows)
    def _(i):
        r = pl.ds(pl.multiple_of(i * rows, rows), rows)
        x = x_ref[r, :].astype(F32)
        dy = dy_acc[r, :].astype(BF16).astype(F32)
        inv = lax.rsqrt(jnp.mean(x * x, axis=-1, keepdims=True) + EPS)
        dot = jnp.mean(dy * x, axis=-1, keepdims=True)
        dst[r, :] = (dres_ref[r, :].astype(F32) + (dy * inv - x * (inv * inv * inv * dot))).astype(BF16)


def lane_mask():
    return lax.broadcasted_iota(jnp.int32, (SEQ, 2 * 64), 1) < 64


def split_heads(x, mask):
    zero = jnp.zeros_like(x)
    return jnp.concatenate([jnp.where(mask, x, zero), jnp.where(mask, zero, x)], axis=0)


def split_heads_t(x):
    y = x.T
    top = lax.broadcasted_iota(jnp.int32, y.shape, 0) < 64
    zero = jnp.zeros_like(y)
    return jnp.concatenate([jnp.where(top, y, zero), jnp.where(top, zero, y)], axis=1)


def attention_fwd(qkv, pt, mixed):
    mask = lane_mask()

    @pl.loop(0, TOK // SEQ)
    def _(s):
        rows = pl.ds(pl.multiple_of(s * SEQ, SEQ), SEQ)
        for h in range(PAIRS):
            lanes = lambda part: pl.ds(part * D + h * 128, 128)
            q, k, v = qkv[rows, lanes(0)], qkv[rows, lanes(1)], qkv[rows, lanes(2)]
            st = nn(k, split_heads_t(q)) * 0.125
            e = jnp.exp(st - jnp.max(st, axis=0, keepdims=True))
            p = (e / jnp.sum(e, axis=0, keepdims=True)).astype(BF16)
            pt[rows, pl.ds(h * 256, 256)] = p
            o = tn(p, v)
            mixed[rows, pl.ds(h * 128, 128)] = jnp.where(mask, o[:SEQ], o[SEQ:]).astype(BF16)


def attention_bwd(s, qkv, pt, dmixed):
    mask = lane_mask()
    rows = pl.ds(pl.multiple_of(s * SEQ, SEQ), SEQ)
    for h in range(PAIRS):
        lanes = lambda part: pl.ds(part * D + h * 128, 128)
        q, k, v = qkv[rows, lanes(0)], qkv[rows, lanes(1)], qkv[rows, lanes(2)]
        do = split_heads(dmixed[rows, pl.ds(h * 128, 128)], mask)
        p = pt[rows, pl.ds(h * 256, 256)]
        dp = nt(v, do).astype(BF16).astype(F32)
        pf = p.astype(F32)
        dot = jnp.sum(dp * pf, axis=0, keepdims=True)
        ds = (pf * (dp - dot) * 0.125).astype(BF16)
        dq = tn(ds, k)
        qkv[rows, lanes(0)] = jnp.where(mask, dq[:SEQ], dq[SEQ:]).astype(BF16)
        qkv[rows, lanes(1)] = nn(ds, split_heads(q, mask)).astype(BF16)
        qkv[rows, lanes(2)] = nn(p, do).astype(BF16)


def lane(i, width):
    return pl.ds(pl.multiple_of(i * width, 128), width)


class Saver:
    def __init__(self, sems):
        self.sems, self.n, self.open = sems, 0, {}

    def put(self, key, src, dst):
        cp = pltpu.make_async_copy(src, dst, self.sems.at[self.n])
        self.n += 1
        cp.start()
        self.open[key] = cp

    def done(self, *keys):
        for key in keys:
            if key in self.open:
                self.open.pop(key).wait()

    def finish(self):
        self.done(*list(self.open))


N_SAVE = 20
SUBS = [pl.ds(j * NB, NB) for j in range(D // NB)]
MGH, MCD = [[pl.ds(k * z, z) for k in range(TOK // z)] for z in (MCG, MCD_)]


def front_kernel(x0, cot, wq, wk, wv, wo, w1, w2,
                 n0, qkv0, pt0, mx0, h0, nn0, pre0, act0, xmid, n1, qkv1, pt1, dmix1, mx1, nn1, act1, dpre1, dh1,
                 x, nrm, qkv, pt, mx, h, n2, big, g, acc, stg, ring, wsem, sems, stg_sem, in_sem):
    save = Saver(sems)
    cx = pltpu.make_async_copy(x0, x, in_sem.at[0])
    cg = pltpu.make_async_copy(cot, g, in_sem.at[1])
    cx.start()
    cg.start()

    def stage_wait(i, dst):
        @pl.when(i >= 2)
        def _():
            slot = lax.rem(i, 2)
            pltpu.make_async_copy(stg.at[slot], dst.at[:, pl.ds(0, D)], stg_sem.at[slot]).wait()

    def stage_put(i, dst):
        slot = lax.rem(i, 2)
        pltpu.make_async_copy(stg.at[slot], dst.at[:, lane(i, D)], stg_sem.at[slot]).start()

    def drain(dst):
        for slot in range(2):
            pltpu.make_async_copy(stg.at[slot], dst.at[:, pl.ds(0, D)], stg_sem.at[slot]).wait()

    MCQ, MCD = [[pl.ds(k * z, z) for k in range(TOK // z)] for z in (MCQ_, MCD_)]
    MGH = [pl.ds(k * MCG, MCG) for k in range(TOK // MCG)]
    MCH = [pl.ds(k * MC, MC) for k in range(TOK // MC)]
    subs = [pl.ds(j * NB, NB) for j in range(D // NB)]

    def sub(i, j):
        return pl.ds(pl.multiple_of(i * D + j * NB, NB), NB)

    def qkv_stage(layer):
        def start(i, part):
            return [(i == m, w.at[layer]) for m, w in enumerate((wq, wk, wv))]

        def step(i, take):
            slot = take(0)
            for j, c in enumerate(subs):
                for r in MCQ:
                    qkv[r, sub(i, j)] = nn(nrm[r, :], ring[slot, :, c]).astype(BF16)
        return Stage(3, 1, start, step)

    def proj_stage(layer):
        def step(i, take):
            slot = take(0)
            for c in subs:
                y = nn(mx[...], ring[slot, :, c]).astype(BF16).astype(F32)
                h[:, c] = (x[:, c].astype(F32) + y).astype(BF16)
        return Stage(1, 1, lambda i, part: [(None, wo.at[layer])], step)

    def up_stage(layer):
        to = pre0 if layer == 0 else act1

        def step(i, take):
            slot, half = take(0), lax.rem(i, 2)
            stage_wait(i, to)
            for j, c in enumerate(subs):
                for r in MCH:
                    pre = nn(n2[r, :], ring[slot, :, c]).astype(BF16)
                    act = gelu(pre.astype(F32)).astype(BF16)
                    big[r, sub(i, j)] = act if layer == 0 else pre
                    stg[half, r, c] = pre if layer == 0 else act
            stage_put(i, to)
        return Stage(4, 1, lambda i, part: [(None, w1.at[:, lane(i, D)])], step)

    def down_stage():
        def step(i, take):
            slot = take(0)

            for c in subs:
                for r in MCD:
                    acc[r, c] = jnp.where(i == 0, 0.0, acc[r, c]) + nn(big[r, lane(i, D)], ring[slot, :, c])
        return Stage(4, 1, lambda i, part: [(None, w2.at[lane(i, D)])], step)

    def dact_stage():
        def step(i, take):
            slot = take(0)
            for j, c in enumerate(subs):
                for r in MGH:
                    d = nt(g[r, :], ring[slot, c]).astype(BF16).astype(F32)
                    big[r, sub(i, j)] = gelu_grad(big[r, sub(i, j)].astype(F32), d).astype(BF16)
        return Stage(4, 1, lambda i, part: [(None, w2.at[lane(i, D)])], step)

    def dn2_stage():
        def step(i, take):
            slot = take(0)

            for c in subs:
                for r in MCD:
                    acc[r, c] = jnp.where(i == 0, 0.0, acc[r, c]) + nt(big[r, lane(i, D)], ring[slot, c])
        return Stage(4, 1, lambda i, part: [(None, w1.at[:, lane(i, D)])], step)

    def dmix_stage(layer, src, dst):
        def step(i, take):
            slot = take(0)
            for c in subs:
                dst[:, c] = nt(src[...], ring[slot, c]).astype(BF16)
        return Stage(1, 1, lambda i, part: [(None, wo.at[layer])], step)

    def first():
        cx.wait()
        rms_rows(x, nrm)
        save.put("nrm", nrm, n0)

    def attend0():
        save.put("qkv", qkv, qkv0)
        attention_fwd(qkv, pt, mx)
        save.put("pt", pt, pt0)
        save.put("mx", mx, mx0)

    def mid0():
        rms_rows(h, n2)
        save.put("h", h, h0)
        save.put("n2", n2, nn0)

    def after_up0():
        save.put("big", big, act0)
        drain(pre0)

    def second():
        save.done("nrm")
        add_rms_rows(h, acc, x, nrm)
        save.put("x", x, xmid)
        save.put("nrm", nrm, n1)
        save.done("qkv", "pt", "mx")

    def attend1():
        save.put("qkv", qkv, qkv1)
        attention_fwd(qkv, pt, mx)
        save.put("pt", pt, pt1)
        save.put("mx", mx, mx1)
        save.done("h", "n2")

    def mid1():
        rms_rows(h, n2)
        save.put("n2", n2, nn1)
        save.done("big")

    def after_up1():
        drain(act1)
        cg.wait()

    def after_dact():
        save.put("big", big, dpre1)

    def after_dn2():
        save.done("x")
        rms_back_rows(h, acc, g, x)
        save.put("x", x, dh1)
        save.done("nrm")

    def last():
        save.put("dmix", nrm, dmix1)
        save.finish()

    run_stages([first, qkv_stage(0), attend0, proj_stage(0), mid0, up_stage(0), after_up0, down_stage(), second,
                qkv_stage(1), attend1, proj_stage(1), mid1, up_stage(1), after_up1, dact_stage(), after_dact, dn2_stage(),
                after_dn2, dmix_stage(1, x, nrm), last], ring, wsem)


def front(x0, cot, wq, wk, wv, wo, w1, w2):
    td, t3, tf, tp = (TOK, D), (TOK, 3 * D), (TOK, FF), (TOK, PAIRS * 2 * SEQ)
    outs = [td, t3, tp, td, td, td, tf, tf, td, td, t3, tp, td, td, td, tf, tf, td]
    return pl.pallas_call(
        front_kernel,
        out_shape=[jax.ShapeDtypeStruct(s, BF16) for s in outs],
        in_specs=[pl.BlockSpec(memory_space=pl.ANY)] * 8,
        out_specs=[pl.BlockSpec(memory_space=pl.ANY)] * len(outs),
        scratch_shapes=[pltpu.VMEM(td, BF16), pltpu.VMEM(td, BF16), pltpu.VMEM(t3, BF16), pltpu.VMEM(tp, BF16), pltpu.VMEM(td, BF16),
                        pltpu.VMEM(td, BF16), pltpu.VMEM(td, BF16), pltpu.VMEM(tf, BF16), pltpu.VMEM(td, BF16), pltpu.VMEM(td, F32),
                        pltpu.VMEM((2, TOK, D), BF16), pltpu.VMEM((SLOTS, D, D), BF16),
                        pltpu.SemaphoreType.DMA((SLOTS,)), pltpu.SemaphoreType.DMA((N_SAVE,)), pltpu.SemaphoreType.DMA((2,)),
                        pltpu.SemaphoreType.DMA((2,))],
        compiler_params=pltpu.CompilerParams(vmem_limit_bytes=67043328),
        name="front",
    )(x0.reshape(td), cot.reshape(td), wq, wk, wv, wo, w1, w2)


MESH = pl.DeviceIdType.MESH
ROWS, LANES = 40, 128
GAP = 2
EARLY = TOK // SEQ
ORDERS = ("xyz", "yzx", "zxy")


def scatter_kernel(groups, n_tiles, depth, n_src, n_after, chain, layer_in, lag, *refs):
    srcs, refs = refs[:n_src], refs[n_src + n_after:]
    n_out = (1, 2, 4)[chain]
    out_ref, more, refs = refs[0], refs[1:n_out], refs[n_out:]
    a_buf, b_buf, tiles, own, rc, r1, r2, r3, a_sem, b_sem, out_sem, send_sem, recv_sem = refs[:13]
    if chain:
        xb, gb, tb, acc, wring, w_sem, at_sem, big = refs[13:21]
    if chain == 1:
        qkv = refs[21]
        dmixed_in, qkv_in, pt_in, x_in, d_in, wq, wk, wv = srcs[3:]
        pt = big
    if chain == 2:
        h_in, pre_in, d_in, wo, w1, w2 = srcs[4:]
    me = lax.axis_index("data")
    bit = {"c": lax.rem(me, 2), "x": lax.rem(me // 2, 2), "y": lax.rem(me // 4, 2), "z": me // 8}
    step = {"c": 1, "x": 2, "y": 4, "z": 8}
    peer = {d: me + step[d] * (1 - 2 * bit[d]) for d in step}
    n_own, n_in, ring = own.shape[1], rc.shape[1], tiles.shape[0]
    gap = GAP if chain == 1 else 0
    n_chunks = 4 * (n_tiles + gap)
    bufs = (rc, r1, r2, r3)

    def group_of(m):
        a = 0
        for first in groups[1:]:
            a = a + (m >= first[0]).astype(jnp.int32)
        return a

    def a_load(a, layer):
        return pltpu.make_async_copy(srcs[groups[a][1][layer]].at[:, pl.ds(groups[a][2], D)], a_buf.at[a % 2, layer], a_sem.at[a % 2, layer])

    def b_load(a, m, layer, first=None):
        col = pl.multiple_of(groups[a][4] + (m - groups[a][0]) * NB, NB) if first is None else first
        slot = lax.rem(m, 2)
        return pltpu.make_async_copy(srcs[groups[a][3][layer]].at[:, pl.ds(col, NB)], b_buf.at[slot, layer], b_sem.at[slot, layer])

    def in_group(a, m, fn):
        last = groups[a + 1][0] - gap if a + 1 < len(groups) else n_tiles + gap

        @pl.when(jnp.logical_and(m >= groups[a][0], m < last))
        def _():
            fn()

    def b_start(m):
        for a in range(len(groups)):
            if groups[a][3] is None:
                continue

            def go(a=a):
                for layer in range(depth):
                    b_load(a, m, layer).start()
            in_group(a, m, go)

    def produce(m):
        loaded = m < groups[-1][0] if gap else m >= 0

        @pl.when(loaded)
        def _():
            for layer in range(depth):
                b_load(0, m, layer, 0).wait()
        for a in range(len(groups)):
            @pl.when(m == groups[a][0])
            def _():
                for layer in range(depth):
                    a_load(a, layer).wait()
                if a + 1 < len(groups):
                    for layer in range(depth):
                        a_load(a + 1, layer).start()
        b_start(m + 1)
        half, slot, to = lax.rem(group_of(m), 2), lax.rem(m, 2), lax.rem(m, ring)

        def fill(b_of):
            for z in range(2):
                tot = None
                for layer in range(depth):
                    y = tn(a_buf[half, layer, :, pl.ds(z * 640, 640)], b_of(layer))
                    tot = y if tot is None else tot + y
                tiles[to, z] = tot.reshape(2, 2, 2, 2 * ROWS, NB)

        if gap:
            @pl.when(loaded)
            def _():
                fill(lambda layer: b_buf[slot, layer])

            @pl.when(jnp.logical_not(loaded))
            def _():
                fill(lambda layer: qkv[:, pl.ds(pl.multiple_of((m - groups[-1][0]) * NB, NB), NB)])
        else:
            fill(lambda layer: b_buf[slot, layer])

    def pick(color, stage, other):
        idx = {"z": slice(None), "y": slice(None), "x": slice(None)}
        for s in range(stage):
            d = ORDERS[color][s]
            idx[d] = 1 - bit[d] if (other and s == stage - 1) else bit[d]
        return tuple(idx[d] for d in "zyx")

    def piece(k):
        sub = lax.rem(k, 4)
        return (lax.rem(k // 4, ring), pl.multiple_of(lax.rem(sub, 2) * ROWS, 8), pl.multiple_of((sub // 2) * LANES, LANES))

    def send(color, stage, j):
        slot, so = lax.rem(j, n_in), lax.rem(j, n_own)
        if stage == 0:
            tile, row, col = piece(3 * j + color)
            src, to = tiles.at[tile, :, :, :, 1 - bit["c"], pl.ds(row, ROWS), pl.ds(col, LANES)], peer["c"]
        else:
            src, to = own.at[(color, so) + pick(color, stage, True)], peer[ORDERS[color][stage - 1]]
        return pltpu.make_async_remote_copy(src, bufs[stage].at[color, slot], send_sem.at[color, stage, slot],
                                            recv_sem.at[color, stage, slot], device_id=(to,), device_id_type=MESH)

    def store(color, j):
        so, k = lax.rem(j, n_own), 3 * j + color
        _, row, col = piece(k)
        tile = k // 4
        if gap:
            tile = tile - gap * (tile >= groups[1][0]).astype(jnp.int32)
        col = pl.multiple_of(tile * NB + col, LANES)
        return pltpu.make_async_copy(own.at[(color, so) + pick(color, 3, False)],
                                     out_ref.at[pl.ds(row, ROWS), pl.ds(col, LANES)], out_sem.at[color, so])

    def live(j, color):
        k = 3 * j + color
        ok = jnp.logical_and(j >= 0, k < n_chunks)
        if gap:
            ok = jnp.logical_and(ok, jnp.logical_or(k < 4 * (groups[1][0] - gap), k >= 4 * groups[1][0]))
        return ok

    n_steps = (0, 16, 46)[chain]

    def w_begin(w):
        def go(cond, src):
            @pl.when(cond)
            def _():
                slot = lax.rem(w, 3)
                pltpu.make_async_copy(src, wring.at[slot], w_sem.at[slot]).start()
        j = pl.multiple_of(lax.rem(w, 5) * NB, NB)
        if chain == 1:
            for m, ref in enumerate((wq, wk, wv)):
                go(jnp.logical_and(w >= 5 * m, w < 5 * m + 5), ref.at[layer_in, pl.ds(j, NB)])
        else:
            go(w < 20, w2.at[pl.ds(pl.multiple_of(w * NB, NB), NB)])
            go(jnp.logical_and(w >= 20, w < 40), w1.at[pl.ds(j, NB), pl.ds(pl.multiple_of(((w - 20) // 5) * D, 128), D)])
            go(jnp.logical_and(w >= 40, w < 45), wo.at[layer_in, pl.ds(j, NB)])

    def w_take(w):
        slot = lax.rem(w, 3)
        pltpu.make_async_copy((wq if chain == 1 else wo).at[0, pl.ds(0, NB)], wring.at[slot], w_sem.at[slot]).wait()
        w_begin(w + 2)
        return slot

    def start(*names):
        for name in names:
            copies[name].start()

    def wait(*names):
        for name in names:
            copies[name].wait()

    if chain:
        if chain == 1:
            table = dict(dmixed=(dmixed_in, xb), qkv=(qkv_in, qkv), pt=(pt_in, pt), x=(x_in, xb), d=(d_in, tb), first=(gb, more[0]))
        else:
            table = dict(d=(d_in, gb), h=(h_in, xb), pre=(pre_in, big), dpre=(big, more[0]), dh=(tb, more[1]), dmix=(xb, more[2]))
        copies = {name: pltpu.make_async_copy(src, dst, at_sem.at[n]) for n, (name, (src, dst)) in enumerate(table.items())}

    def sum_step(g, src, slot):
        c, m = pl.ds(pl.multiple_of(lax.rem(g, 5) * NB, NB), NB), g // 5
        for r in MCD:
            acc[r, c] = jnp.where(m == 0, 0.0, acc[r, c]) + nt(src[r, lane(m, D)], wring[slot])

    def input_step(g):
        @pl.when(g < 15)
        def _():
            sum_step(g, qkv, w_take(g))

        @pl.when(g == 15)
        def _():
            wait("x", "d")
            rms_back_rows(xb, acc, tb, gb)
            start("first")

    def mlp_step(g):
        @pl.when(g == 0)
        def _():
            wait("d", "pre")

        @pl.when(g < 20)
        def _():
            slot = w_take(g)
            c = pl.ds(pl.multiple_of(g * NB, NB), NB)
            for r in MGH:
                d = nt(gb[r, :], wring[slot]).astype(BF16).astype(F32)
                big[r, c] = gelu_grad(big[r, c].astype(F32), d).astype(BF16)

        @pl.when(g == 20)
        def _():
            start("dpre")

        @pl.when(jnp.logical_and(g >= 20, g < 40))
        def _():
            sum_step(g - 20, big, w_take(g))

        @pl.when(g == 40)
        def _():
            wait("h")
            rms_back_rows(xb, acc, gb, tb)
            start("dh")

        @pl.when(jnp.logical_and(g >= 41, g < 46))
        def _():
            slot = w_take(g - 1)
            c = pl.ds(pl.multiple_of((g - 41) * NB, NB), NB)
            for r in MCD:
                xb[r, c] = nt(tb[r, :], wring[slot]).astype(BF16)

        @pl.when(g == 45)
        def _():
            start("dmix")

    def tick(t, carry):
        for color in range(3):
            j = t - 4 * lag - 1

            @pl.when(live(j, color))
            def _():
                store(color, j).wait()
        for stage in (3, 2, 1, 0):
            j = t - (stage + 1) * lag
            for color in range(3):
                @pl.when(live(j, color))
                def _():
                    slot, so = lax.rem(j, n_in), lax.rem(j, n_own)
                    copy = send(color, stage, j)
                    copy.wait_send()
                    copy.wait_recv()
                    keep = (color, so) + pick(color, stage, False)
                    if stage == 0:
                        tile, row, col = piece(3 * j + color)
                        mine = tiles[tile, :, :, :, bit["c"], pl.ds(row, ROWS), pl.ds(col, LANES)]
                    else:
                        mine = own[keep]
                    own[keep] = mine + bufs[stage][color, slot]
                    if stage < 3:
                        send(color, stage + 1, j).start()
                    else:
                        store(color, j).start()
        for color in range(3):
            @pl.when(live(t, color))
            def _():
                send(color, 0, t).start()
        m = (3 * t + 5) // 4

        fresh = jnp.logical_and(m != (3 * t + 2) // 4, m < n_tiles + gap)
        if gap:
            fresh = jnp.logical_and(fresh, jnp.logical_or(m < groups[1][0] - gap, m >= groups[1][0]))

        @pl.when(fresh)
        def _():
            produce(m)
        if chain == 1:
            @pl.when(t == 0)
            def _():
                wait("dmixed", "qkv", "pt")

            @pl.when(t < EARLY)
            def _():
                attention_bwd(t, qkv, pt, xb)

            @pl.when(t == EARLY)
            def _():
                start("x")

            @pl.when(jnp.logical_and(t >= EARLY, t < EARLY + 16))
            def _():
                input_step(t - EARLY)
        if chain == 2:
            @pl.when(t < 23)
            def _():
                @pl.loop(0, 2)
                def _(u):
                    mlp_step(2 * t + u)
        return carry

    for layer in range(depth):
        a_load(0, layer).start()
    b_start(jnp.int32(0))
    if chain:
        start(*(("dmixed", "qkv", "pt", "d") if chain == 1 else ("d", "pre", "h")))
        w_begin(jnp.int32(0))
        w_begin(jnp.int32(1))
    barrier = pltpu.get_barrier_semaphore()
    for d in "cxyz":
        pl.semaphore_signal(barrier, inc=1, device_id=(peer[d],), device_id_type=MESH)
    pl.semaphore_wait(barrier, 4)
    produce(jnp.int32(0))
    ticks = pl.cdiv(n_chunks, 3) + 4 * lag + 1
    lax.fori_loop(0, ticks, tick, 0)
    if chain:
        wait(*(("first",) if chain == 1 else ("dpre", "dh", "dmix")))


def scatter_sum(srcs, groups, n_tiles, collective_id, after=(), chain=0, layer=0, lag=2):
    depth = len(groups[0][1])
    n_own, n_in, ring, blk = 4 * lag + 2, 2 * lag + (4 if chain == 1 else 0), lag + 2, (ROWS, LANES)
    size = D * NB * n_tiles * 4
    td, t3, tf = (TOK, D), (TOK, 3 * D), (TOK, FF)
    outs = [(), (td,), (tf, td, td)][chain]
    args = (*srcs, *after)
    scratch = [
        pltpu.VMEM((2, depth, TOK, D), BF16), pltpu.VMEM((2, depth, TOK, NB), BF16),
        pltpu.VMEM((ring, 2, 2, 2, 2, 2 * ROWS, NB), F32),
        pltpu.VMEM((3, n_own, 2, 2, 2) + blk, F32), pltpu.VMEM((3, n_in, 2, 2, 2) + blk, F32),
        pltpu.VMEM((3, n_in, 2, 2) + blk, F32), pltpu.VMEM((3, n_in, 2) + blk, F32), pltpu.VMEM((3, n_in) + blk, F32),
        pltpu.SemaphoreType.DMA((2, depth)), pltpu.SemaphoreType.DMA((2, depth)), pltpu.SemaphoreType.DMA((3, n_own)),
        pltpu.SemaphoreType.DMA((3, 4, n_in)), pltpu.SemaphoreType.DMA((3, 4, n_in))]
    if chain:
        scratch += [pltpu.VMEM(td, BF16), pltpu.VMEM(td, BF16), pltpu.VMEM(td, BF16), pltpu.VMEM(td, F32),
                    pltpu.VMEM((3, NB, D), BF16), pltpu.SemaphoreType.DMA((3,)), pltpu.SemaphoreType.DMA((6,))]
        scratch += [pltpu.VMEM((TOK, PAIRS * 2 * SEQ), BF16), pltpu.VMEM(t3, BF16)] if chain == 1 else [pltpu.VMEM(tf, BF16)]
    return pl.pallas_call(
        functools.partial(scatter_kernel, groups, n_tiles, depth, len(srcs), len(after), chain, layer, lag),
        out_shape=[jax.ShapeDtypeStruct((2 * ROWS, NB * n_tiles), F32)] + [jax.ShapeDtypeStruct(o, BF16) for o in outs],
        in_specs=[pl.BlockSpec(memory_space=pl.ANY)] * len(args),
        out_specs=[pl.BlockSpec(memory_space=pl.ANY)] * (1 + len(outs)),
        scratch_shapes=scratch,
        compiler_params=pltpu.CompilerParams(collective_id=collective_id, has_side_effects=True, vmem_limit_bytes=67043328),
        cost_estimate=pl.CostEstimate(flops=size * 4000, bytes_accessed=2 * size, transcendentals=0),
        name=f"scatter_sum_{collective_id}",
    )(*args)


def gather(shard):
    return lax.all_gather(shard, "data", axis=0, tiled=True)


ANY = pl.BlockSpec(memory_space=pl.ANY)


def place_attention(full, layer, dst, carry, after):
    rows, part = 160, TOK * 160 // D

    def kernel(src, *refs):
        outs = refs[-4 - len(carry):]
        for n, out in zip((1, 2, 3, 0), outs):
            out[0] = src[:, n * D:(n + 1) * D]
        for ref, out in zip(refs, outs[4:]):
            out[...] = ref[...]

    strip = pl.BlockSpec((part, D), lambda i: (i, 0))
    return pl.pallas_call(
        kernel,
        grid=(D // rows,),
        out_shape=[jax.ShapeDtypeStruct((2, D, D), F32)] * 4 + [jax.ShapeDtypeStruct((TOK, D), BF16)] * len(carry),
        in_specs=[pl.BlockSpec((rows, 4 * D), lambda i: (i, 0))] + [strip] * len(carry) + [ANY] * (len(dst) + len(after)),
        out_specs=[pl.BlockSpec((1, rows, D), lambda i: (layer, i, 0))] * 4 + [strip] * len(carry),
        input_output_aliases={n + 1 + len(carry): n for n in range(len(dst))},
        compiler_params=pltpu.CompilerParams(vmem_limit_bytes=60 << 20),
        cost_estimate=pl.CostEstimate(flops=D * D, bytes_accessed=32 * D * D, transcendentals=0),
        name=f"place_attention_{layer}",
    )(full, *carry, *dst, *after)


def place_blocks(full, shape, where, dst, after, name):
    rows = 640
    per, blocks = D // rows, full.shape[1] // D

    def to(n, i):
        row, col = where(n)
        return row * per + i, col

    def kernel(src, *refs):
        refs[-1][...] = src[...]

    return pl.pallas_call(
        kernel,
        grid=(blocks, per),
        out_shape=jax.ShapeDtypeStruct(shape, F32),
        in_specs=[pl.BlockSpec((rows, D), lambda n, i: (i, n))] + [ANY] * (len(dst) + len(after)),
        out_specs=pl.BlockSpec((rows, D), to),
        input_output_aliases={1: 0} if dst else {},
        compiler_params=pltpu.CompilerParams(vmem_limit_bytes=60 << 20),
        cost_estimate=pl.CostEstimate(flops=D * D, bytes_accessed=8 * blocks * D * D, transcendentals=0),
        name=name,
    )(full, *dst, *after)


def solution(mesh):
    def local_step(x_init, cot_out, w_query, w_key, w_value, w_proj, w_up, w_down):
        weights = (w_query, w_key, w_value, w_proj, w_up, w_down)
        (n0, qkv0, pt0, mx0, h0, nn0, pre0, act0, xmid, n1, qkv1, pt1, dmix1, mx1, nn1, act1, dpre1, dh1) = front(
            x_init, cot_out, *weights)
        cot, x0 = cot_out.reshape(TOK, D), x_init.reshape(TOK, D)
        w_in = (w_query, w_key, w_value)
        attention = ((0, (0,), 0, (1,), 0), (5 + GAP, (2,), 0, None, 0))
        down = [tuple((5 * n, (0, 1), q * D, (2, 3), 0) for n, q in enumerate(qs)) for qs in ((0, 1, 2), (3,))]
        up = ((0, (0, 1), 0, (2, 3), 0),)
        shard1, dmid = scatter_sum((mx1, dh1, n1, dmix1, qkv1, pt1, xmid, dh1, *w_in), attention, 20, 1, chain=1, layer=1)
        full1 = gather(shard1)
        shard_a, dpre0, dh0, dmix0 = scatter_sum(
            (act0, act1, dmid, cot, h0, pre0, dmid, w_proj, w_up, w_down), down[0], 15, 2, (shard1,), chain=2, layer=0)
        full_a = gather(shard_a)
        shard0, dx = scatter_sum((mx0, dh0, n0, dmix0, qkv0, pt0, x0, dh0, *w_in), attention, 20, 3, (shard_a,), chain=1, layer=0)
        full0 = gather(shard0)
        shard_up, = scatter_sum((nn0, nn1, dpre0, dpre1), up, 20, 4, (shard0,))
        full_up = gather(shard_up)
        shard_b, = scatter_sum((act0, act1, dmid, cot), down[1], 5, 5, (shard_up,))
        full_b = gather(shard_b)
        half = place_attention(full1, 1, (), (), (shard_b,))
        g_down = place_blocks(full_a, (FF, D), lambda n: (n, 0), (), (half[0],), "place_down_0")
        *attn, dx = place_attention(full0, 0, half, (dx,), (g_down,))
        g_up = place_blocks(full_up, (D, FF), lambda n: (0, n), (), (attn[0],), "place_up")
        g_down = place_blocks(full_b, (FF, D), lambda n: (3 + n, 0), (g_down,), (g_up,), "place_down_3")
        return (*attn, g_up, g_down, dx.reshape(x_init.shape))

    data_spec = P("data")
    full_spec = P()
    in_specs = (data_spec, data_spec, full_spec, full_spec, full_spec, full_spec, full_spec, full_spec)
    out_specs = (full_spec, full_spec, full_spec, full_spec, full_spec, full_spec, data_spec)
    return jax.shard_map(local_step, mesh=mesh, in_specs=in_specs, out_specs=out_specs, check_vma=False)
```

time: 963 us -> 929 us (0.965)
  Pallas kernels: 873 us -> 848 us
  waiting for transfers between devices: 67.7 us -> 56.5 us
    pallas_call x4 -> x3, Pallas kernels: 139 us -> 38.1 us  [place_blocks(): pl.pallas_call(kernel, grid=(blocks, per), out_shape=jax.ShapeDtypeStruct...]
    pallas_call x5, Pallas kernels: 531 us -> 630 us  [scatter_sum(): pl.pallas_call(functools.partial(scatter_kernel, groups, n_tiles, depth,...]
    pallas_call x1, Pallas kernels: 165 us -> 141 us  [front(): pl.pallas_call(front_kernel, out_shape=[jax.ShapeDtypeStruct(s, BF16) for...]
    all_gather x5, waiting for transfers between devices: 67.6 us -> 56.4 us  [gather(): return lax.all_gather(shard, 'data', axis=0, tiled=True)]
  transfers between devices with their start and end apart: 5 -> 5, of which waited for: 2 -> 2; matrix products, arithmetic and copies ran while one was open for 0% -> 0% of each run, Pallas kernels for 63% -> 64%
where the time goes in v3:
time: 929 us; the launch traced here: 920 us
  Pallas kernels  848 us (91%)
  waiting for transfers between devices  56.5 us (6%)
  between operations  14.3 us (2%)
    pallas_call x5, Pallas kernels, scatter_sum(): pl.pallas_call(functools.partial(scatter_kernel, groups, n_tiles, depth,...  630 us
    pallas_call x1, Pallas kernels, front(): pl.pallas_call(front_kernel, out_shape=[jax.ShapeDtypeStruct(s, BF16) for...  141 us
    all_gather x5, waiting for transfers between devices, gather(): return lax.all_gather(shard, 'data', axis=0, tiled=True)  56.4 us
    pallas_call x2, Pallas kernels, place_attention(): pl.pallas_call(kernel, grid=(D // rows,), out_shape=[jax.ShapeDtypeStruct...  38.5 us
    pallas_call x3, Pallas kernels, place_blocks(): pl.pallas_call(kernel, grid=(blocks, per), out_shape=jax.ShapeDtypeStruct...  38.1 us
  transfers between devices with their start and end apart: 5, of which 2 were waited for; matrix products, arithmetic and copies ran while one was open for 0% of the time, Pallas kernels for 64%

profile of v3, /device:TPU:0, one launch (start us, length us, event | category | flops | bytes accessed | tf_op | source)
XLA Modules:
  0.0 919.6 jit_solution(10965114600442002349)
XLA Ops:
  7.2 0.0 all-gather.8.cloned.1.call-start
  7.2 141.5 %front.1 = (bf16[1024,1280]{1,0:T(8,128)(2,1)}, bf16[1024,3840]{1,0:T(8,128)(2,1)}, bf16[1024,2560]{1,0:T(8,128)(2,1)}, bf16[1024,1280]{1,0:T(8,128)(2,1)}, bf16...) custom-call(bf16[1024,1280]{1,0:T(8,128)(2,1)} %bitcast.3, ...), custom_call_target="tpu_custom_call" | custom-call | tf_op jit(solution)/shard_map/front/pallas_call | solution.py:390
  148.7 116.0 %scatter_sum_1.1 = (f32[80,5120]{1,0:T(8,128)}, bf16[1024,1280]{1,0:T(8,128)(2,1)}) custom-call(bf16[1024,1280]{1,0:T(8,128)(2,1)} %get-tuple-element.45.refs_0_, bf16[1024,1280]{1,0:T(8,128)(2,1)} %get-tuple-element.46.refs_1_.refs_7_, bf16[1024,1280]{1,0:T(8,128)(2,1)} %get-tuple-element.47.refs_2_, bf16[1024,1280]{1,0:T(8,128)(2,1)} %get-tuple-element.48.refs_3_, ...), custom_call_target="tpu_custom_call" | custom-call | flops 104857600000 | bytes 52428800 | tf_op jit(solution)/shard_map/scatter_sum_1/pallas_call | solution.py:732
  264.7 0.0 all-gather.8.cloned.1.call-update
  264.7 0.0 all-gather.10.cloned.1.call-start
  264.7 139.0 %scatter_sum_2.1 = (f32[80,3840]{1,0:T(8,128)}, bf16[1024,5120]{1,0:T(8,128)(2,1)}, bf16[1024,1280]{1,0:T(8,128)(2,1)}, bf16[1024,1280]{1,0:T(8,128)(2,1)}) custom-call(bf16[1024,5120]{1,0:T(8,128)(2,1)} %get-tuple-element.43.refs_0_, bf16[1024,5120]{1,0:T(8,128)(2,1)} %get-tuple-element.44.refs_1_, bf16[1024,1280]{1,0:T(8,128)(2,1)} %get-tuple-element.52.refs_2_.refs_6_, ...), custom_call_target="tpu_custom_call" | custom-call | flops 78643200000 | bytes 39321600 | tf_op jit(solution)/shard_map/scatter_sum_2/pallas_call | solution.py:732
  403.8 0.0 all-gather.10.cloned.1.call-update
  403.8 0.3 all-gather.6.cloned.1.call-start
  404.1 166.0 %scatter_sum_3.1 = (f32[80,5120]{1,0:T(8,128)}, bf16[1024,1280]{1,0:T(8,128)(2,1)}) custom-call(bf16[1024,1280]{1,0:T(8,128)(2,1)} %get-tuple-element.42.refs_0_, bf16[1024,1280]{1,0:T(8,128)(2,1)} %get-tuple-element.56.refs_1_.refs_7_, bf16[1024,1280]{1,0:T(8,128)(2,1)} %get-tuple-element.57.refs_2_, bf16[1024,1280]{1,0:T(8,128)(2,1)} %get-tuple-element.58.refs_3_, ...), custom_call_target="tpu_custom_call" | custom-call | flops 104857600000 | bytes 52428800 | tf_op jit(solution)/shard_map/scatter_sum_3/pallas_call | solution.py:732
  570.1 0.0 all-gather.6.cloned.1.call-update
  570.1 0.0 all-gather.12.cloned.1.call-start
  570.1 165.9 %scatter_sum_4.1.refs_4_ = f32[80,5120]{1,0:T(8,128)} custom-call(bf16[1024,1280]{1,0:T(8,128)(2,1)} %get-tuple-element.64.refs_0_, bf16[1024,1280]{1,0:T(8,128)(2,1)} %get-tuple-element.65.refs_1_, bf16[1024,5120]{1,0:T(8,128)(2,1)} %get-tuple-element.66.refs_2_, bf16[1024,5120]{1,0:T(8,128)(2,1)} %get-tuple-element.67.refs_3_, ...), custom_call_target="tpu_custom_call" | custom-call | flops 104857600000 | bytes 52428800 | tf_op jit(solution)/shard_map/scatter_sum_4/pallas_call | solution.py:732
  736.0 0.0 all-gather.12.cloned.1.call-update
  736.1 0.3 all-gather.14.cloned.1.call-start
  736.4 43.2 %scatter_sum_5.1.refs_0_ = f32[80,1280]{1,0:T(8,128)} custom-call(bf16[1024,5120]{1,0:T(8,128)(2,1)} %get-tuple-element.43.refs_0_, bf16[1024,5120]{1,0:T(8,128)(2,1)} %get-tuple-element.44.refs_1_, bf16[1024,1280]{1,0:T(8,128)(2,1)} %get-tuple-element.52.refs_2_.refs_6_, bf16[1024,1280]{1,0:T(8,128)(2,1)} %bitcast.7, f32[80,5120]{1,0:T(8,128)} %scatter_sum_4.1.refs_4_), custom_call_target="tpu_custom_call" | custom-call | flops 26214400000 | bytes 13107200 | tf_op jit(solution)/shard_map/scatter_sum_5/pallas_call | solution.py:732
  779.6 0.0 all-gather.14.cloned.1.call-update
  779.6 0.0 all-gather.8.cloned.1.call-done.src
  779.6 18.8 %place_attention_1.1 = (f32[2,1280,1280]{2,1,0:T(8,128)}, f32[2,1280,1280]{2,1,0:T(8,128)}, f32[2,1280,1280]{2,1,0:T(8,128)}, f32[2,1280,1280]{2,1,0:T(8,128)}) custom-call(f32[1280,5120]{1,0:T(8,128)} %all-gather.8.cloned.1.call-done.src, f32[80,1280]{1,0:T(8,128)} %scatter_sum_5.1.refs_0_), custom_call_target="tpu_custom_call" | custom-call | flops 1638400 | bytes 52428800 | tf_op jit(solution)/shard_map/place_attention_1/pallas_call | solution.py:762
  798.4 0.0 all-gather.10.cloned.1.call-done.src
  798.4 14.3 %place_down_0.1.refs_5_.refs_0_ = f32[5120,1280]{1,0:T(8,128)} custom-call(f32[1280,3840]{1,0:T(8,128)} %all-gather.10.cloned.1.call-done.src, f32[2,1280,1280]{2,1,0:T(8,128)} %get-tuple-element.68.refs_0_.refs_1_), custom_call_target="tpu_custom_call" | custom-call | flops 1638400 | bytes 39321600 | tf_op jit(solution)/shard_map/place_down_0/pallas_call | solution.py:786
  812.7 0.0 all-gather.6.cloned.1.call-done.src
  812.7 19.7 %place_attention_0.1 = (f32[2,1280,1280]{2,1,0:T(8,128)}, f32[2,1280,1280]{2,1,0:T(8,128)}, f32[2,1280,1280]{2,1,0:T(8,128)}, f32[2,1280,1280]{2,1,0:T(8,128)}, bf16[1024,1280]{1,0:T(8,128)(2,1)}) custom-call(f32[1280,5120]{1,0:T(8,128)} %all-gather.6.cloned.1.call-done.src, ...), custom_call_target="tpu_custom_call", output_to_operand_aliasing={{0}: (2, {}), {1}: (3, {}), {2}: (4, {}), {3}: (5, {})} | custom-call | flops 1638400 | bytes 52428800 | tf_op jit(solution)/shard_map/place_attention_0/pallas_call | solution.py:762
  832.4 30.4 %all-gather.12.cloned.1.call-done.src = f32[1280,5120]{1,0:T(8,128)} async-done(((f32[80,5120]{1,0:T(8,128)}), f32[1280,5120]{1,0:T(8,128)}) %all-gather.12.cloned.1.call-update) | async-done | bytes 26214416 | tf_op jit(solution)/shard_map/all_gather | solution.py:745
  862.8 18.9 %place_up.1.refs_1_ = f32[1280,5120]{1,0:T(8,128)} custom-call(f32[1280,5120]{1,0:T(8,128)} %all-gather.12.cloned.1.call-done.src, f32[2,1280,1280]{2,1,0:T(8,128)} %get-tuple-element.35.refs_0_), custom_call_target="tpu_custom_call" | custom-call | flops 1638400 | bytes 52428800 | tf_op jit(solution)/shard_map/place_up/pallas_call | solution.py:786
  881.7 25.9 %all-gather.14.cloned.1.call-done.src = f32[1280,1280]{1,0:T(8,128)} async-done(((f32[80,1280]{1,0:T(8,128)}), f32[1280,1280]{1,0:T(8,128)}) %all-gather.14.cloned.1.call-update) | async-done | bytes 6553616 | tf_op jit(solution)/shard_map/all_gather | solution.py:745
  907.7 4.9 place_down_3.1
Async XLA Ops:
  7.2 772.5 %all-gather.8.cloned.1.call-start = ((), (), s32[]{:S(2)}) async-start(), calls=%async_computation.1 | async-start | bytes 27852800 | tf_op jit(solution)/shard_map/all_gather | solution.py:745
  264.7 533.7 %all-gather.10.cloned.1.call-start = ((), (), s32[]{:S(2)}) async-start(), calls=%async_computation.2 | async-start | bytes 20889600 | tf_op jit(solution)/shard_map/all_gather | solution.py:745
  403.8 408.9 %all-gather.6.cloned.1.call-start = ((), (), s32[]{:S(2)}) async-start(), calls=%async_computation | async-start | bytes 27852800 | tf_op jit(solution)/shard_map/all_gather | solution.py:745
  570.1 292.8 %all-gather.12.cloned.1.call-start = ((), (), s32[]{:S(2)}) async-start(), calls=%async_computation.3 | async-start | bytes 27852800 | tf_op jit(solution)/shard_map/all_gather | solution.py:745
  736.1 171.6 %all-gather.14.cloned.1.call-start = ((), (), s32[]{:S(2)}) async-start(), calls=%async_computation.4 | async-start | bytes 6963200 | tf_op jit(solution)/shard_map/all_gather | solution.py:745
Sparse Core Ops, SparseCore 0:
  264.8 161.3 all-gather.7
  428.4 141.7 all-gather.9
  572.4 174.5 all-gather.5
  749.2 113.6 all-gather.11
  864.9 42.6 all-gather.13

commit v4 on v0

v4 whole, which is shorter than its diff:
```python
import functools

import jax
import jax.numpy as jnp
from jax import lax
from jax.experimental import pallas as pl
from jax.experimental.pallas import tpu as pltpu
from jax.sharding import PartitionSpec as P

EPS = 1e-6
F32, BF16 = jnp.float32, jnp.bfloat16
TOK, D, FF, SEQ = 1024, 1280, 5120, 128
NB = 256
DB, FB = D // NB, FF // NB
PAIRS = 10
VMEM_MOST = 67043328
SUBS = [pl.ds(j * NB, NB) for j in range(DB)]
ANY = pl.BlockSpec(memory_space=pl.ANY)
C0 = 0.7978845608028654
C1 = C0 * 0.044715


def nn(a, b):
    return lax.dot_general(a, b, (((1,), (0,)), ((), ())), preferred_element_type=F32)


def nt(a, b):
    return lax.dot_general(a, b, (((1,), (1,)), ((), ())), preferred_element_type=F32)


def tn(a, b):
    return lax.dot_general(a, b, (((0,), (0,)), ((), ())), preferred_element_type=F32)


def part(i, width):
    return pl.ds(pl.multiple_of(i * width, 128), width)


def rows_of(size):
    return [pl.ds(k * size, size) for k in range(TOK // size)]


class Stage:
    def __init__(self, count, source, step):
        self.count, self.source, self.step = count, source, step


def begin(sources, ring, sem, slot):
    for cond, src in sources:
        copy = pltpu.make_async_copy(src, ring.at[slot], sem.at[slot])
        if cond is None:
            copy.start()
        else:
            pl.when(cond)(copy.start)


def run_stages(items, ring, sem, follow=()):
    stages = [it for it in items if isinstance(it, Stage)]
    base = 0
    for it in items:
        if not isinstance(it, Stage):
            it()
            continue
        after = stages[stages.index(it) + 1].source(0) if it is not stages[-1] else follow

        def one(i, it=it, base=base, after=after):
            slot = lax.rem(base + i, 2)
            pltpu.make_async_copy(it.source(0)[0][1], ring.at[slot], sem.at[slot]).wait()
            other = lax.rem(base + i + 1, 2)

            @pl.when(i + 1 < it.count)
            def _():
                begin(it.source(i + 1), ring, sem, other)

            @pl.when(i + 1 >= it.count)
            def _():
                begin(after, ring, sem, other)
            it.step(i, slot)

        pl.loop(0, it.count)(one)
        base += it.count


def gelu(x):
    half = 0.5 * x
    return half * jnp.tanh(x * (C0 + C1 * (x * x))) + half


def gelu_grad(x, d):
    x2 = x * x
    t = jnp.tanh(x * (C0 + C1 * x2))
    return d * ((0.5 + 0.5 * t) + (x * (0.5 * C0 + 1.5 * C1 * x2)) * (1.0 - t * t))


def by_rows(fn, rows=128):
    @pl.loop(0, TOK // rows)
    def _(i):
        fn(part(i, rows))


def inverse_rms(x):
    return lax.rsqrt(jnp.mean(x * x, axis=-1, keepdims=True) + EPS)


def rms_rows(src, dst):
    def one(r):
        x = src[r, :].astype(F32)
        dst[r, :] = (x * inverse_rms(x)).astype(BF16)
    by_rows(one)


def add_rms_rows(res, acc, out, dst):
    def one(r):
        y = (res[r, :].astype(F32) + acc[r, :].astype(BF16).astype(F32)).astype(BF16)
        out[r, :] = y
        x = y.astype(F32)
        dst[r, :] = (x * inverse_rms(x)).astype(BF16)
    by_rows(one)


def rms_back_rows(x_ref, dy_acc, dres_ref, dst):
    def one(r):
        x = x_ref[r, :].astype(F32)
        dy = dy_acc[r, :].astype(BF16).astype(F32)
        inv = inverse_rms(x)
        dot = jnp.mean(dy * x, axis=-1, keepdims=True)
        dst[r, :] = (dres_ref[r, :].astype(F32) + (dy * inv - x * (inv * inv * inv * dot))).astype(BF16)
    by_rows(one)


def lane_mask():
    return lax.broadcasted_iota(jnp.int32, (SEQ, 2 * 64), 1) < 64


def split_heads(x, mask):
    zero = jnp.zeros_like(x)
    return jnp.concatenate([jnp.where(mask, x, zero), jnp.where(mask, zero, x)], axis=0)


def split_heads_t(x):
    y = x.T
    top = lax.broadcasted_iota(jnp.int32, y.shape, 0) < 64
    zero = jnp.zeros_like(y)
    return jnp.concatenate([jnp.where(top, y, zero), jnp.where(top, zero, y)], axis=1)


def attention_fwd(qkv, pt, mixed):
    mask = lane_mask()

    def one(rows):
        for h in range(PAIRS):
            q, k, v = (qkv[rows, pl.ds(n * D + h * SEQ, SEQ)] for n in range(3))
            st = nn(k, split_heads_t(q)) * 0.125
            e = jnp.exp(st - jnp.max(st, axis=0, keepdims=True))
            p = (e / jnp.sum(e, axis=0, keepdims=True)).astype(BF16)
            pt[rows, pl.ds(h * NB, NB)] = p
            o = tn(p, v)
            mixed[rows, pl.ds(h * SEQ, SEQ)] = jnp.where(mask, o[:SEQ], o[SEQ:]).astype(BF16)
    by_rows(one, SEQ)


def attention_bwd(s, duo, qkv, pt, dmixed):
    mask = lane_mask()
    rows = part(s, SEQ)
    for h in range(2):
        lanes = [pl.ds(pl.multiple_of(n * D + duo * NB + h * SEQ, SEQ), SEQ) for n in range(3)]
        q, k, v = (qkv[rows, c] for c in lanes)
        do = split_heads(dmixed[rows, lanes[0]], mask)
        p = pt[rows, part(2 * duo + h, NB)]
        dp = nt(v, do).astype(BF16).astype(F32)
        pf = p.astype(F32)
        dot = jnp.sum(dp * pf, axis=0, keepdims=True)
        ds = (pf * (dp - dot) * 0.125).astype(BF16)
        dq = tn(ds, k)
        qkv[rows, lanes[0]] = jnp.where(mask, dq[:SEQ], dq[SEQ:]).astype(BF16)
        qkv[rows, lanes[1]] = nn(ds, split_heads(q, mask)).astype(BF16)
        qkv[rows, lanes[2]] = nn(p, do).astype(BF16)


def front_kernel(x0, cot, wq, wk, wv, wo, w1, w2,
                 n_out, qkv_out, pt_out, mx_out, nn_out, act_out, h0, pre0, xmid, dmix1, dpre1, dh1,
                 x, nrm, qkv, pt, mx, h, n2, big, g, acc, stg, ring, wsem, sems, stg_sem):
    def copy(n, src, dst):
        return pltpu.make_async_copy(src, dst, sems.at[n])

    cx, cg = copy(0, x0, x), copy(1, cot, g)
    cx.start()
    cg.start()
    begin([(None, wq.at[0])], ring, wsem, 0)
    cx.wait()
    rms_rows(x, nrm)

    def stage_copy(i, dst):
        slot = lax.rem(i, 2)
        return pltpu.make_async_copy(stg.at[slot], dst.at[:, part(i, D)], stg_sem.at[slot])

    def sums(stage_count, source, src, times, weight):
        def step(i, slot):
            for c in SUBS:
                for r in rows_of(512):
                    acc[r, c] = jnp.where(i == 0, 0.0, acc[r, c]) + times(src[r, part(i, D)], weight(slot, c))
        return Stage(stage_count, source, step)

    @pl.loop(0, 2)
    def _(l):
        first = l == 0
        outs = dict(n=copy(2, nrm, n_out.at[l]), qkv=copy(3, qkv, qkv_out.at[l]), pt=copy(4, pt, pt_out.at[l]),
                    mx=copy(5, mx, mx_out.at[l]), nn=copy(6, n2, nn_out.at[l]))
        only = dict(h=copy(7, h, h0), act=copy(8, big, act_out.at[0]))

        def qkv_step(i, slot):
            for j, c in enumerate(SUBS):
                for r in rows_of(256):
                    qkv[r, pl.ds(pl.multiple_of(i * D + j * NB, NB), NB)] = nn(nrm[r, :], ring[slot, :, c]).astype(BF16)

        def attend():
            outs["qkv"].start()
            attention_fwd(qkv, pt, mx)
            outs["pt"].start()
            outs["mx"].start()

        def proj_step(i, slot):
            for c in SUBS:
                y = nn(mx[...], ring[slot, :, c]).astype(BF16).astype(F32)
                h[:, c] = (x[:, c].astype(F32) + y).astype(BF16)

        def middle():
            rms_rows(h, n2)
            outs["nn"].start()
            pl.when(first)(only["h"].start)

        def up_step(i, slot):
            half = lax.rem(i, 2)
            pl.when(i >= 2)(stage_copy(i, pre0).wait)
            for j, c in enumerate(SUBS):
                for r in rows_of(128):
                    pre = nn(n2[r, :], ring[slot, :, c]).astype(BF16)
                    act = gelu(pre.astype(F32)).astype(BF16)
                    big[r, pl.ds(pl.multiple_of(i * D + j * NB, NB), NB)] = jnp.where(first, act, pre)
                    stg[half, r, c] = jnp.where(first, pre, act)
            pl.when(first)(stage_copy(i, pre0).start)
            pl.when(l == 1)(stage_copy(i, act_out.at[1]).start)

        outs["n"].start()
        run_stages([Stage(3, lambda i: [(i == m, w.at[l]) for m, w in enumerate((wq, wk, wv))], qkv_step), attend,
                    Stage(1, lambda i: [(None, wo.at[l])], proj_step), middle,
                    Stage(4, lambda i: [(None, w1.at[:, part(i, D)])], up_step)], ring, wsem, [(None, w2.at[pl.ds(0, D)])])
        for i in range(2):
            stage_copy(i, pre0).wait()

        @pl.when(first)
        def _():
            only["act"].start()
            run_stages([sums(4, lambda i: [(None, w2.at[part(i, D)])], big, nn, lambda slot, c: ring[slot, :, c])],
                       ring, wsem, [(None, wq.at[1])])
            for cp in (*outs.values(), *only.values()):
                cp.wait()
            add_rms_rows(h, acc, x, nrm)
            copy(9, x, xmid).start()

    def dact_step(i, slot):
        for j, c in enumerate(SUBS):
            to = pl.ds(pl.multiple_of(i * D + j * NB, NB), NB)
            for r in rows_of(256):
                d = nt(g[r, :], ring[slot, c]).astype(BF16).astype(F32)
                big[r, to] = gelu_grad(big[r, to].astype(F32), d).astype(BF16)

    def after_dact():
        copy(8, big, dpre1).start()

    def after_dn2():
        copy(9, x, xmid).wait()
        rms_back_rows(h, acc, g, x)
        copy(9, x, dh1).start()
        copy(2, nrm, n_out.at[1]).wait()

    def dmix_step(i, slot):
        for c in SUBS:
            nrm[:, c] = nt(x[...], ring[slot, c]).astype(BF16)

    cg.wait()
    run_stages([Stage(4, lambda i: [(None, w2.at[part(i, D)])], dact_step), after_dact,
                sums(4, lambda i: [(None, w1.at[:, part(i, D)])], big, nt, lambda slot, c: ring[slot, c]), after_dn2,
                Stage(1, lambda i: [(None, wo.at[1])], dmix_step)], ring, wsem)
    copy(2, nrm, dmix1).start()
    for n, src, dst in ((2, nrm, dmix1), (3, qkv, qkv_out.at[1]), (4, pt, pt_out.at[1]), (5, mx, mx_out.at[1]),
                        (6, n2, nn_out.at[1]), (8, big, dpre1), (9, x, dh1)):
        copy(n, src, dst).wait()


TD, T3, TF, TP = (TOK, D), (TOK, 3 * D), (TOK, FF), (TOK, PAIRS * NB)


def front(x0, cot, *weights):
    both = [(2,) + s for s in (TD, T3, TP, TD, TD, TF)]
    outs = both + [TD, TF, TD, TD, TF, TD]
    vmem = [pltpu.VMEM(s, BF16) for s in (TD, TD, T3, TP, TD, TD, TD, TF, TD)]
    return pl.pallas_call(
        front_kernel,
        out_shape=[jax.ShapeDtypeStruct(s, BF16) for s in outs],
        in_specs=[ANY] * (2 + len(weights)),
        out_specs=[ANY] * len(outs),
        scratch_shapes=vmem + [pltpu.VMEM(TD, F32), pltpu.VMEM((2, TOK, D), BF16), pltpu.VMEM((2, D, D), BF16),
                               pltpu.SemaphoreType.DMA((2,)), pltpu.SemaphoreType.DMA((10,)), pltpu.SemaphoreType.DMA((2,))],
        compiler_params=pltpu.CompilerParams(vmem_limit_bytes=VMEM_MOST),
        name="front",
    )(x0, cot, *weights)


MESH = pl.DeviceIdType.MESH
ROWS, LANES = 40, 128
OFFSETS = (1, 3, 5, 7)
LAST = OFFSETS[3] + 1
ORDERS = ("xyz", "yzx", "zxy")
CUBE = (2, 2, 2)
HEADS, MLP = 1, 2
N_OUT = (1, 2, 4)


def scatter_kernel(groups, n_tiles, n_src, n_after, chain, layer_in, spread, *refs):
    srcs, refs = refs[:n_src], refs[n_src + n_after:]
    out_ref, more, refs = refs[0], refs[1:N_OUT[chain]], refs[N_OUT[chain]:]
    a_buf, b_buf, tiles, own, rc, r1, r2, r3, a_sem, b_sem, out_sem, send_sem, recv_sem, *refs = refs
    heads, mlp, depth = chain == HEADS, chain == MLP, len(groups[0][1])
    if spread:
        all_send, all_recv = refs
    if chain:
        xb, gb, tb, acc, wring, w_sem, at_sem, big, *refs = refs
    if heads:
        (qkv, head_sem), pt = refs, big
        _, _, _, dmixed_in, qkv_in, pt_in, x_in, d_in, wq, wk, wv = srcs
        qkv_in, pt_in = qkv_in.at[layer_in], pt_in.at[layer_in]
    if mlp:
        _, _, _, h_in, pre_in, d_in, wo, w1, w2 = srcs
    me = lax.axis_index("data")
    bit, peer = {}, {}
    for n, d in enumerate("cxyz"):
        bit[d] = lax.rem(me // 2 ** n, 2)
        peer[d] = me + 2 ** n * (1 - 2 * bit[d])
    n_own, n_in, ring = own.shape[1], rc.shape[1], tiles.shape[0]
    n_chunks = 4 * n_tiles
    bufs = (rc, r1, r2, r3)

    def group_of(m):
        a = 0
        for first in groups[1:]:
            a = a + (m >= first[0]).astype(jnp.int32)
        return a

    def source(spec):
        n, layer = spec
        return srcs[n] if layer is None else srcs[n].at[layer]

    def a_load(a, layer):
        _, ins, col, _, _ = groups[a]
        return pltpu.make_async_copy(source(ins[layer]).at[:, pl.ds(col, D)], a_buf.at[a % 2, layer], a_sem.at[a % 2, layer])

    def b_load(a, m, layer, ahead=True):
        first, _, _, ins, col = groups[a]
        if ahead:
            col = pl.multiple_of(col + (m - first) * NB, NB)
        slot = lax.rem(m, 2)
        return pltpu.make_async_copy(source(ins[layer]).at[:, pl.ds(col, NB)], b_buf.at[slot, layer], b_sem.at[slot, layer])

    def in_group(a, m, fn):
        last = groups[a + 1][0] if a + 1 < len(groups) else n_tiles

        @pl.when(jnp.logical_and(m >= groups[a][0], m < last))
        def _():
            fn()

    def b_start(m):
        for a in range(len(groups)):
            if groups[a][3] is None:
                continue

            def go(a=a):
                for layer in range(depth):
                    b_load(a, m, layer).start()
            in_group(a, m, go)

    def produce(m):
        half, slot, to = lax.rem(group_of(m), 2), lax.rem(m, 2), lax.rem(m, ring)

        @pl.when(m < (DB if heads else n_tiles))
        def _():
            for layer in range(depth):
                b_load(0, m, layer, False).wait()
        if heads:
            @pl.when(m >= DB)
            def _():
                b_buf[slot, 0] = qkv[:, pl.ds(pl.multiple_of(lax.rem(m - DB, 3) * D + ((m - DB) // 3) * NB, NB), NB)]
        for a in range(len(groups)):
            @pl.when(m == groups[a][0])
            def _():
                for layer in range(depth):
                    a_load(a, layer).wait()
                if a + 1 < len(groups):
                    for layer in range(depth):
                        a_load(a + 1, layer).start()
        b_start(m + 1)

        for z in range(2):
            tot = None
            for layer in range(depth):
                y = tn(a_buf[half, layer, :, part(z, D // 2)], b_buf[slot, layer])
                tot = y if tot is None else tot + y
            tiles[to, z] = tot.reshape(CUBE + (2 * ROWS, NB))

    def pick(color, stage, other):
        idx = {d: slice(None) for d in "zyx"}
        for s in range(stage):
            d = ORDERS[color][s]
            idx[d] = 1 - bit[d] if (other and s == stage - 1) else bit[d]
        return tuple(idx[d] for d in "zyx")

    def piece(k):
        sub = lax.rem(k, 4)
        return (lax.rem(k // 4, ring), pl.multiple_of(lax.rem(sub, 2) * ROWS, 8), pl.multiple_of((sub // 2) * LANES, LANES))

    def send(color, stage, j):
        slot, so = lax.rem(j, n_in), lax.rem(j, n_own)
        if stage == 0:
            tile, row, col = piece(3 * j + color)
            src, to = tiles.at[tile, :, :, :, 1 - bit["c"], pl.ds(row, ROWS), pl.ds(col, LANES)], peer["c"]
        else:
            src, to = own.at[(color, so) + pick(color, stage, True)], peer[ORDERS[color][stage - 1]]
        return pltpu.make_async_remote_copy(src, bufs[stage].at[color, slot], send_sem.at[color, stage, slot],
                                            recv_sem.at[color, stage, slot], device_id=(to,), device_id_type=MESH)

    def place(color, j):
        k = 3 * j + color
        _, row, col = piece(k)
        tile = k // 4
        if heads:
            tile = jnp.where(tile < DB, tile, DB + DB * lax.rem(tile - DB, 3) + (tile - DB) // 3)
        return pl.ds(row, ROWS), pl.ds(pl.multiple_of(tile * NB + col, LANES), LANES)

    def store(color, j):
        so = lax.rem(j, n_own)
        where = place(color, j)
        if spread:
            where = (bit["z"], bit["y"], bit["x"], bit["c"]) + where
        return pltpu.make_async_copy(own.at[(color, so) + pick(color, 3, False)], out_ref.at[where], out_sem.at[color, so])

    def hand_on(color, stage, j):
        slot, so = lax.rem(j, n_in), lax.rem(j, n_own)
        idx = {d: bit[d] for d in "zyxc"}
        for d in ORDERS[color][3 - stage:]:
            idx[d] = slice(None)
        dst = out_ref.at[(idx["z"], idx["y"], idx["x"], idx["c"]) + place(color, j)]
        src = dst if stage else own.at[(color, so) + pick(color, 3, False)]
        to = peer[ORDERS[color][2 - stage] if stage < 3 else "c"]
        return pltpu.make_async_remote_copy(src, dst, all_send.at[color, stage, slot], all_recv.at[color, stage, slot],
                                            device_id=(to,), device_id_type=MESH)

    def live(j, color):
        return jnp.logical_and(j >= 0, 3 * j + color < n_chunks)

    up_from, norm_at, end = FB, 2 * FB, 2 * FB + 1 + DB

    def w_begin(w):
        slot = lax.rem(w, 3)
        begin([(w < up_from, w2.at[part(w, NB)]),
               (jnp.logical_and(w >= up_from, w < norm_at), w1.at[part(lax.rem(w, DB), NB), part((w - up_from) // DB, D)]),
               (jnp.logical_and(w >= norm_at, w < end - 1), wo.at[layer_in, part(lax.rem(w, DB), NB)])], wring, w_sem, slot)

    def w_take(w):
        slot = lax.rem(w, 3)
        pltpu.make_async_copy(wo.at[0, pl.ds(0, NB)], wring.at[slot], w_sem.at[slot]).wait()
        w_begin(w + 2)
        return slot

    def head_weights(duo):
        col = pl.multiple_of(duo * NB, NB)
        base = 3 * lax.rem(duo, 2)
        return [pltpu.make_async_copy(ref.at[layer_in, :, pl.ds(col, NB)], wring.at[base + m], w_sem.at[base + m])
                for m, ref in enumerate((wq, wk, wv))]

    def start(*names):
        for name in names:
            copies[name].start()

    def wait(*names):
        for name in names:
            copies[name].wait()

    if chain:
        if heads:
            table = dict(x=(x_in, xb), d=(d_in, tb), first=(gb, *more))
        else:
            table = dict(d=(d_in, gb), h=(h_in, xb), pre=(pre_in, big), dpre=(big, more[0]), dh=(tb, more[1]), dmix=(xb, more[2]))
        copies = {name: pltpu.make_async_copy(src, dst, at_sem.at[n]) for n, (name, (src, dst)) in enumerate(table.items())}

    def head_loads(duo):
        cols = [pl.ds(n * D + duo * NB, NB) for n in range(3)]
        pairs = [(dmixed_in, xb, cols[0]), (pt_in, pt, pl.ds(duo * 2 * NB, 2 * NB))] + [(qkv_in, qkv, c) for c in cols]
        return [pltpu.make_async_copy(src.at[:, c], dst.at[:, c], head_sem.at[duo, n]) for n, (src, dst, c) in enumerate(pairs)]

    def input_step(duo, turn):
        @pl.when(turn == 0)
        def _():
            for copy in head_weights(duo):
                copy.wait()

            @pl.when(duo < DB - 1)
            def _():
                for copy in head_weights(duo + 1):
                    copy.start()
        base = 3 * lax.rem(duo, 2)

        @pl.loop(jnp.where(turn == 0, 0, turn + 1), turn + 2)
        def _(n):
            c = part(n, NB)
            tot = jnp.where(duo == 0, 0.0, acc[:, c])
            for m in range(3):
                tot = tot + nt(qkv[:, pl.ds(pl.multiple_of(m * D + duo * NB, NB), NB)], wring[base + m, c])
            acc[:, c] = tot

    def sum_step(g, src, slot):
        c, m = part(lax.rem(g, DB), NB), g // DB

        for r in rows_of(512):
            acc[r, c] = jnp.where(m == 0, 0.0, acc[r, c]) + nt(src[r, part(m, D)], wring[slot])

    def mlp_step(g):
        @pl.when(g == 0)
        def _():
            wait("d", "pre")

        @pl.when(g < up_from)
        def _():
            slot, c = w_take(g), part(g, NB)

            for r in rows_of(256):
                d = nt(gb[r, :], wring[slot]).astype(BF16).astype(F32)
                big[r, c] = gelu_grad(big[r, c].astype(F32), d).astype(BF16)

        @pl.when(g == up_from)
        def _():
            start("dpre")

        @pl.when(jnp.logical_and(g >= up_from, g < norm_at))
        def _():
            sum_step(g - up_from, big, w_take(g))

        @pl.when(g == norm_at)
        def _():
            wait("h")
            rms_back_rows(xb, acc, gb, tb)
            start("dh")

        @pl.when(jnp.logical_and(g > norm_at, g < end))
        def _():
            slot, c = w_take(g - 1), part(g - norm_at - 1, NB)

            for r in rows_of(512):
                xb[r, c] = nt(tb[r, :], wring[slot]).astype(BF16)

        @pl.when(g == end - 1)
        def _():
            start("dmix")

    def tick(t, carry):
        for stage in (3, 2, 1, 0) if spread else ():
            j = t - OFFSETS[3] - 2 * (stage + 1)
            for color in range(3):
                @pl.when(live(j, color))
                def _():
                    copy = hand_on(color, stage, j)
                    copy.wait_send()
                    copy.wait_recv()
                    if stage == 0:
                        store(color, j).wait()
                    if stage < 3:
                        hand_on(color, stage + 1, j).start()
        for color in () if spread else range(3):
            j = t - LAST

            @pl.when(live(j, color))
            def _():
                store(color, j).wait()
        for stage in (3, 2, 1, 0):
            j = t - OFFSETS[stage]
            for color in range(3):
                @pl.when(live(j, color))
                def _():
                    slot, so = lax.rem(j, n_in), lax.rem(j, n_own)
                    copy = send(color, stage, j)
                    copy.wait_send()
                    copy.wait_recv()
                    keep = (color, so) + pick(color, stage, False)
                    if stage == 0:
                        tile, row, col = piece(3 * j + color)
                        mine = tiles[tile, :, :, :, bit["c"], pl.ds(row, ROWS), pl.ds(col, LANES)]
                    else:
                        mine = own[keep]
                    own[keep] = mine + bufs[stage][color, slot]
                    if stage < 3:
                        send(color, stage + 1, j).start()
                    else:
                        store(color, j).start()
                        if spread:
                            hand_on(color, 0, j).start()
        for color in range(3):
            @pl.when(live(t, color))
            def _():
                send(color, 0, t).start()
        if heads:
            for duo in range(DB):
                @pl.when(t == 1 + 4 * duo)
                def _():
                    for copy in head_loads(duo):
                        copy.wait()

            @pl.when(jnp.logical_and(t > 0, t <= 4 * DB))
            def _():
                for u in range(2):
                    attention_bwd(2 * lax.rem(t - 1, 4) + u, (t - 1) // 4, qkv, pt, xb)
        m = (3 * t + 5) // 4

        @pl.when(jnp.logical_and(m != (3 * t + 2) // 4, m < n_tiles))
        def _():
            produce(m)
        if heads:
            first_tick, last_attend = DB, 4 * DB
            since = t - first_tick
            quarter = jnp.where(t > last_attend, since - last_attend // 2 + 2, since // 2)
            norm_tick = first_tick + last_attend + last_attend // 2 - 2

            @pl.when(jnp.logical_and(jnp.logical_and(since >= 0, t < norm_tick), jnp.logical_or(t > last_attend, lax.rem(since, 2) == 0)))
            def _():
                input_step(quarter // 4, lax.rem(quarter, 4))

            @pl.when(t == last_attend + 1)
            def _():
                start("x")

            @pl.when(t == norm_tick)
            def _():
                wait("x", "d")
                rms_back_rows(xb, acc, tb, gb)
                start("first")
        if mlp:
            @pl.when(2 * t < end)
            def _():
                @pl.loop(0, 2)
                def _(u):
                    mlp_step(2 * t + u)
        return carry

    for layer in range(depth):
        a_load(0, layer).start()
    b_start(jnp.int32(0))
    if heads:
        for duo in range(DB):
            for copy in head_loads(duo):
                copy.start()
        for copy in head_weights(jnp.int32(0)):
            copy.start()
        start("d")
    if mlp:
        start("d", "pre", "h")
        for n in range(2):
            w_begin(jnp.int32(n))
    barrier = pltpu.get_barrier_semaphore()
    for d in "cxyz":
        pl.semaphore_signal(barrier, inc=1, device_id=(peer[d],), device_id_type=MESH)
    pl.semaphore_wait(barrier, 4)
    produce(jnp.int32(0))
    ticks = pl.cdiv(n_chunks, 3) + LAST + 8 * spread
    lax.fori_loop(0, ticks, tick, 0)
    if heads:
        wait("first")
    if mlp:
        wait("dpre", "dh", "dmix")


def scatter_sum(srcs, groups, n_tiles, collective_id, after=(), chain=0, layer=0, spread=False):
    depth = len(groups[0][1])
    n_own, n_in, blk = LAST + 1 + spread, 4, (ROWS, LANES)
    size = D * NB * n_tiles * 4
    outs = [(), (TD,), (TF, TD, TD)][chain]
    sums = (CUBE + (2,)) * spread + (2 * ROWS, NB * n_tiles)
    args = (*srcs, *after)
    dma = pltpu.SemaphoreType.DMA
    scratch = [
        pltpu.VMEM((2, depth, TOK, D), BF16), pltpu.VMEM((2, depth, TOK, NB), BF16), pltpu.VMEM((n_in, 2) + CUBE + (2 * ROWS, NB), F32),
        pltpu.VMEM((3, n_own) + CUBE + blk, F32)] + [pltpu.VMEM((3, n_in) + CUBE[n:] + blk, F32) for n in range(4)] + [
        dma((2, depth)), dma((2, depth)), dma((3, n_own)), dma((3, 4, n_in)), dma((3, 4, n_in))]
    if spread:
        scratch += [dma((3, 4, n_in))] * 2
    if chain:
        scratch += [pltpu.VMEM(TD, BF16)] * 3 + [
            pltpu.VMEM(TD, F32), pltpu.VMEM((6, D, NB) if chain == HEADS else (3, NB, D), BF16), dma((6,)), dma((6,))]
        scratch += [pltpu.VMEM(TP, BF16), pltpu.VMEM(T3, BF16), dma((DB, DB))] if chain == HEADS else [pltpu.VMEM(TF, BF16)]
    return pl.pallas_call(
        functools.partial(scatter_kernel, groups, n_tiles, len(srcs), len(after), chain, layer, spread),
        out_shape=[jax.ShapeDtypeStruct(sums, F32)] + [jax.ShapeDtypeStruct(o, BF16) for o in outs],
        in_specs=[ANY] * len(args),
        out_specs=[ANY] * (1 + len(outs)),
        scratch_shapes=scratch,
        compiler_params=pltpu.CompilerParams(collective_id=collective_id, has_side_effects=True, vmem_limit_bytes=VMEM_MOST),
        cost_estimate=pl.CostEstimate(flops=size * 4000, bytes_accessed=2 * size, transcendentals=0),
        name=f"scatter_sum_{collective_id}",
    )(*args)


def gather(shard):
    return lax.all_gather(shard, "data", axis=0, tiled=True)


def place_attention(full, layer, dst, carry, after):
    rows, part = 160, TOK * 160 // D

    def kernel(src, *refs):
        outs = refs[-4 - len(carry):]
        for n, out in zip((1, 2, 3, 0), outs):
            out[0] = src[:, n * D:(n + 1) * D]
        for ref, out in zip(refs, outs[4:]):
            out[...] = ref[...]

    strip = pl.BlockSpec((part, D), lambda i: (i, 0))
    return pl.pallas_call(
        kernel,
        grid=(D // rows,),
        out_shape=[jax.ShapeDtypeStruct((2, D, D), F32)] * 4 + [jax.ShapeDtypeStruct((TOK, D), BF16)] * len(carry),
        in_specs=[pl.BlockSpec((rows, 4 * D), lambda i: (i, 0))] + [strip] * len(carry) + [ANY] * (len(dst) + len(after)),
        out_specs=[pl.BlockSpec((1, rows, D), lambda i: (layer, i, 0))] * 4 + [strip] * len(carry),
        input_output_aliases={n + 1 + len(carry): n for n in range(len(dst))},
        compiler_params=pltpu.CompilerParams(vmem_limit_bytes=60 << 20),
        cost_estimate=pl.CostEstimate(flops=D * D, bytes_accessed=32 * D * D, transcendentals=0),
        name=f"place_attention_{layer}",
    )(full, *carry, *dst, *after)


def place_blocks(full, shape, where, dst, after, name):
    rows = 640
    per, blocks = D // rows, full.shape[1] // D

    def to(n, i):
        row, col = where(n)
        return row * per + i, col

    def kernel(src, *refs):
        refs[-1][...] = src[...]

    return pl.pallas_call(
        kernel,
        grid=(blocks, per),
        out_shape=jax.ShapeDtypeStruct(shape, F32),
        in_specs=[pl.BlockSpec((rows, D), lambda n, i: (i, n))] + [ANY] * (len(dst) + len(after)),
        out_specs=pl.BlockSpec((rows, D), to),
        input_output_aliases={1: 0} if dst else {},
        compiler_params=pltpu.CompilerParams(vmem_limit_bytes=60 << 20),
        cost_estimate=pl.CostEstimate(flops=D * D, bytes_accessed=8 * blocks * D * D, transcendentals=0),
        name=name,
    )(full, *dst, *after)


def solution(mesh):
    def local_step(x_init, cot_out, w_query, w_key, w_value, w_proj, w_up, w_down):
        cot, x0 = cot_out.reshape(TD), x_init.reshape(TD)
        (nrm, qkv, pt, mx, nn2, act, h0, pre0, xmid, dmix1, dpre1, dh1) = front(x0, cot, w_query, w_key, w_value, w_proj, w_up, w_down)
        w_in = (w_query, w_key, w_value)
        both, ends = ((0, 0), (0, 1)), ((1, None), (2, None))

        def attention(layer, d_hidden, d_mixed, x_in, number, after):
            groups = ((0, ((0, layer),), 0, ((1, None),), 0), (DB, ((2, layer),), 0, None, 0))
            srcs = (mx, d_hidden, nrm, d_mixed, qkv, pt, x_in, d_hidden, *w_in)
            return scatter_sum(srcs, groups, 4 * DB, number, after, chain=HEADS, layer=layer)

        down = [tuple((DB * n, both, q * D, ends, 0) for n, q in enumerate(qs)) for qs in ((0, 1, 2), (3,))]
        shard1, dmid = attention(1, dh1, dmix1, xmid, 1, ())
        full1 = gather(shard1)
        shard_a, dpre0, dh0, dmix0 = scatter_sum(
            (act, dmid, cot, h0, pre0, dmid, w_proj, w_up, w_down), down[0], 3 * DB, 2, (shard1,), chain=MLP)
        full_a = gather(shard_a)
        shard0, dx = attention(0, dh0, dmix0, x0, 3, (shard_a,))
        full0 = gather(shard0)
        shard_up, = scatter_sum((nn2, dpre0, dpre1), ((0, both, 0, ends, 0),), FB, 4, (shard0,))
        full_up = gather(shard_up)
        shard_b, = scatter_sum((act, dmid, cot), down[1], DB, 5, (shard_up,), spread=True)
        half = place_attention(full1, 1, (), (), (shard_b,))
        g_down = place_blocks(full_a, (FF, D), lambda n: (n, 0), (), (half[0],), "place_down_0")
        g_down = place_blocks(shard_b.reshape(D, D), (FF, D), lambda n: (3, 0), (g_down,), (), "place_down_3")
        *attn, dx = place_attention(full0, 0, half, (dx,), (g_down,))
        g_up = place_blocks(full_up, (D, FF), lambda n: (0, n), (), (attn[0],), "place_up")
        return (*attn, g_up, g_down, dx.reshape(x_init.shape))

    data_spec = P("data")
    full_spec = P()
    in_specs = (data_spec, data_spec) + (full_spec,) * 6
    out_specs = (full_spec,) * 6 + (data_spec,)
    return jax.shard_map(local_step, mesh=mesh, in_specs=in_specs, out_specs=out_specs, check_vma=False)
```

time: 1580 us -> 894 us (0.57)
  waiting for transfers between devices: 884 us -> 20 us
  Pallas kernels: 0 us -> 850 us
  matrix products: 539 us -> 0 us
  local copies, waits for them, and re-layouts: 72.9 us -> 0 us
  other arithmetic: 62.1 us -> 0 us
    psum x1 -> x0, waiting for transfers between devices: 884 us -> none  [local_step(): lax.psum((attn_part, up_part, down_part), 'data')]
    pallas_call x0 -> x11, Pallas kernels: none -> 850 us  [the longest x5 632 us: scatter_sum(): pl.pallas_call(functools.partial(scatter_kernel, groups, n_tiles, len(src...]
    dot_general x45 -> x0, matrix products: 517 us -> none  [product(): return jnp.einsum(subscripts, lhs, rhs, preferred_element_type=jnp.float32)]
    unnamed x150 -> x0, local copies, waits for them, and re-layouts: 41.1 us -> none
    another operation x2 -> x0, other arithmetic: 36.7 us -> none  [the longest x1 18.5 us: local_step(): g_query = jnp.stack([part[0] for part in attn_grads])]
    convert_element_type x8 -> x0, local copies, waits for them, and re-layouts: 31.7 us -> none  [the longest x2 8.98 us: layer_backward(): product('bse,de->bsd', d_hidden, w_proj).astype(jnp.bfloat16)]
    convert_element_type x6 -> x0, other arithmetic: 23 us -> none  [the longest x2 11.4 us: layer_forward(): probs = jax.nn.softmax(scores, axis=-1).astype(jnp.bfloat16)]
    sub x2 -> x0, matrix products: 22.1 us -> none  [layer_forward(): probs = jax.nn.softmax(scores, axis=-1).astype(jnp.bfloat16)]
  transfers between devices with their start and end apart: 1 -> 4, of which waited for: 1 -> 1; matrix products, arithmetic and copies ran while one was open for 2% -> 0% of each run, Pallas kernels for 0% -> 65%
where the time goes in v4:
time: 894 us; the launch traced here: 885 us
  Pallas kernels  850 us (95%)
  waiting for transfers between devices  20 us (2%)
  between operations  14.2 us (2%)
    pallas_call x5, Pallas kernels, scatter_sum(): pl.pallas_call(functools.partial(scatter_kernel, groups, n_tiles, len(src...  632 us
    pallas_call x1, Pallas kernels, front(): pl.pallas_call(front_kernel, out_shape=[jax.ShapeDtypeStruct(s, BF16) for...  142 us
    pallas_call x2, Pallas kernels, place_attention(): pl.pallas_call(kernel, grid=(D // rows,), out_shape=[jax.ShapeDtypeStruct...  38.5 us
    pallas_call x3, Pallas kernels, place_blocks(): pl.pallas_call(kernel, grid=(blocks, per), out_shape=jax.ShapeDtypeStruct...  38.1 us
    all_gather x4, waiting for transfers between devices, gather(): return lax.all_gather(shard, 'data', axis=0, tiled=True)  19.9 us
  transfers between devices with their start and end apart: 4, of which 1 were waited for; matrix products, arithmetic and copies ran while one was open for 0% of the time, Pallas kernels for 65%

profile of v4, /device:TPU:0, one launch (start us, length us, event | category | flops | bytes accessed | tf_op | source)
XLA Modules:
  0.0 884.8 jit_solution(17847720025366652646)
XLA Ops:
  7.2 0.0 all-gather.7.cloned.1.call-start
  7.2 141.6 %front.1 = (bf16[2,1024,1280]{2,1,0:T(8,128)(2,1)}, bf16[2,1024,3840]{2,1,0:T(8,128)(2,1)}, bf16[2,1024,2560]{2,1,0:T(8,128)(2,1)}, bf16[2,1024,1280]{2,1,0:T(8,...) custom-call(bf16[1024,1280]{1,0:T(8,128)(2,1)} %bitcast.5, ...), custom_call_target="tpu_custom_call" | custom-call | tf_op jit(solution)/shard_map/front/pallas_call | solution.py:298
  148.8 111.5 %scatter_sum_1.1 = (f32[80,5120]{1,0:T(8,128)}, bf16[1024,1280]{1,0:T(8,128)(2,1)}) custom-call(bf16[2,1024,1280]{2,1,0:T(8,128)(2,1)} %get-tuple-element.36.refs_0_, bf16[1024,1280]{1,0:T(8,128)(2,1)} %get-tuple-element.38.refs_1_.refs_7_, bf16[2,1024,1280]{2,1,0:T(8,128)(2,1)} %get-tuple-element.39.refs_2_, bf16[1024,1280]{1,0:T(8,128)(2,1)} %get-tuple-element.40.refs_3_, ...), custom_call_target="tpu_custom_call" | custom-call | flops 104857600000 | bytes 52428800 | tf_op jit(solution)/shard_map/scatter_sum_1/pallas_call | solution.py:697
  260.3 0.0 all-gather.7.cloned.1.call-update
  260.3 0.0 all-gather.9.cloned.1.call-start
  260.4 132.4 %scatter_sum_2.1 = (f32[80,3840]{1,0:T(8,128)}, bf16[1024,5120]{1,0:T(8,128)(2,1)}, bf16[1024,1280]{1,0:T(8,128)(2,1)}, bf16[1024,1280]{1,0:T(8,128)(2,1)}) custom-call(bf16[2,1024,5120]{2,1,0:T(8,128)(2,1)} %get-tuple-element.37.refs_0_, bf16[1024,1280]{1,0:T(8,128)(2,1)} %get-tuple-element.44.refs_1_.refs_5_, bf16[1024,1280]{1,0:T(8,128)(2,1)} %bitcast.8, ...), custom_call_target="tpu_custom_call" | custom-call | flops 78643200000 | bytes 39321600 | tf_op jit(solution)/shard_map/scatter_sum_2/pallas_call | solution.py:697
  392.7 0.0 all-gather.9.cloned.1.call-update
  392.8 0.0 all-gather.5.cloned.1.call-start
  392.8 158.2 %scatter_sum_3.1 = (f32[80,5120]{1,0:T(8,128)}, bf16[1024,1280]{1,0:T(8,128)(2,1)}) custom-call(bf16[2,1024,1280]{2,1,0:T(8,128)(2,1)} %get-tuple-element.36.refs_0_, bf16[1024,1280]{1,0:T(8,128)(2,1)} %get-tuple-element.48.refs_1_.refs_7_, bf16[2,1024,1280]{2,1,0:T(8,128)(2,1)} %get-tuple-element.39.refs_2_, bf16[1024,1280]{1,0:T(8,128)(2,1)} %get-tuple-element.49.refs_3_, ...), custom_call_target="tpu_custom_call" | custom-call | flops 104857600000 | bytes 52428800 | tf_op jit(solution)/shard_map/scatter_sum_3/pallas_call | solution.py:697
  551.0 0.0 all-gather.5.cloned.1.call-update
  551.0 0.0 all-gather.11.cloned.1.call-start
  551.1 152.3 %scatter_sum_4.1.refs_3_ = f32[80,5120]{1,0:T(8,128)} custom-call(bf16[2,1024,1280]{2,1,0:T(8,128)(2,1)} %get-tuple-element.53.refs_0_, bf16[1024,5120]{1,0:T(8,128)(2,1)} %get-tuple-element.54.refs_1_, bf16[1024,5120]{1,0:T(8,128)(2,1)} %get-tuple-element.55.refs_2_, f32[80,5120]{1,0:T(8,128)} %get-tuple-element.51.refs_3_), custom_call_target="tpu_custom_call" | custom-call | flops 104857600000 | bytes 52428800 | tf_op jit(solution)/shard_map/scatter_sum_4/pallas_call | solution.py:697
  703.4 0.0 all-gather.11.cloned.1.call-update
  703.4 78.0 %scatter_sum_5.1.refs_0_ = f32[2,2,2,2,80,1280]{5,4,3,2,1,0:T(8,128)} custom-call(bf16[2,1024,5120]{2,1,0:T(8,128)(2,1)} %get-tuple-element.37.refs_0_, bf16[1024,1280]{1,0:T(8,128)(2,1)} %get-tuple-element.44.refs_1_.refs_5_, bf16[1024,1280]{1,0:T(8,128)(2,1)} %bitcast.9, f32[80,5120]{1,0:T(8,128)} %scatter_sum_4.1.refs_3_), custom_call_target="tpu_custom_call" | custom-call | flops 26214400000 | bytes 13107200 | tf_op jit(solution)/shard_map/scatter_sum_5/pallas_call | solution.py:697
  781.4 0.0 all-gather.7.cloned.1.call-done.src
  781.4 18.8 %place_attention_1.1 = (f32[2,1280,1280]{2,1,0:T(8,128)}, f32[2,1280,1280]{2,1,0:T(8,128)}, f32[2,1280,1280]{2,1,0:T(8,128)}, f32[2,1280,1280]{2,1,0:T(8,128)}) custom-call(f32[1280,5120]{1,0:T(8,128)} %all-gather.7.cloned.1.call-done.src, f32[2,2,2,2,80,1280]{5,4,3,2,1,0:T(8,128)} %scatter_sum_5.1.refs_0_), custom_call_target="tpu_custom_call" | custom-call | flops 1638400 | bytes 52428800 | tf_op jit(solution)/shard_map/place_attention_1/pallas_call | solution.py:724
  800.2 0.0 all-gather.9.cloned.1.call-done.src
  800.2 14.3 %place_down_0.1.refs_0_ = f32[5120,1280]{1,0:T(8,128)} custom-call(f32[1280,3840]{1,0:T(8,128)} %all-gather.9.cloned.1.call-done.src, f32[2,1280,1280]{2,1,0:T(8,128)} %get-tuple-element.56.refs_0_.refs_1_), custom_call_target="tpu_custom_call" | custom-call | flops 1638400 | bytes 39321600 | tf_op jit(solution)/shard_map/place_down_0/pallas_call | solution.py:748
  814.4 4.9 place_down_3.1.refs_5_
  819.4 0.0 all-gather.5.cloned.1.call-done.src
  819.4 19.7 %place_attention_0.1 = (f32[2,1280,1280]{2,1,0:T(8,128)}, f32[2,1280,1280]{2,1,0:T(8,128)}, f32[2,1280,1280]{2,1,0:T(8,128)}, f32[2,1280,1280]{2,1,0:T(8,128)}, bf16[1024,1280]{1,0:T(8,128)(2,1)}) custom-call(f32[1280,5120]{1,0:T(8,128)} %all-gather.5.cloned.1.call-done.src, ...), custom_call_target="tpu_custom_call", output_to_operand_aliasing={{0}: (2, {}), {1}: (3, {}), {2}: (4, {}), {3}: (5, {})} | custom-call | flops 1638400 | bytes 52428800 | tf_op jit(solution)/shard_map/place_attention_0/pallas_call | solution.py:724
  839.1 19.9 %all-gather.11.cloned.1.call-done.src = f32[1280,5120]{1,0:T(8,128)} async-done(((f32[80,5120]{1,0:T(8,128)}), f32[1280,5120]{1,0:T(8,128)}) %all-gather.11.cloned.1.call-update) | async-done | bytes 26214416 | tf_op jit(solution)/shard_map/all_gather | solution.py:710
  859.0 18.9 %place_up.1 = f32[1280,5120]{1,0:T(8,128)} custom-call(f32[1280,5120]{1,0:T(8,128)} %all-gather.11.cloned.1.call-done.src, f32[2,1280,1280]{2,1,0:T(8,128)} %get-tuple-element.29.refs_0_), custom_call_target="tpu_custom_call" | custom-call | flops 1638400 | bytes 52428800 | tf_op jit(solution)/shard_map/place_up/pallas_call | solution.py:748
Async XLA Ops:
  7.2 774.2 %all-gather.7.cloned.1.call-start = ((), (), s32[]{:S(2)}) async-start(), calls=%async_computation.1 | async-start | bytes 27852800 | tf_op jit(solution)/shard_map/all_gather | solution.py:710
  260.3 539.9 %all-gather.9.cloned.1.call-start = ((), (), s32[]{:S(2)}) async-start(), calls=%async_computation.2 | async-start | bytes 20889600 | tf_op jit(solution)/shard_map/all_gather | solution.py:710
  392.8 426.6 %all-gather.5.cloned.1.call-start = ((), (), s32[]{:S(2)}) async-start(), calls=%async_computation | async-start | bytes 27852800 | tf_op jit(solution)/shard_map/all_gather | solution.py:710
  551.0 308.0 %all-gather.11.cloned.1.call-start = ((), (), s32[]{:S(2)}) async-start(), calls=%async_computation.3 | async-start | bytes 27852800 | tf_op jit(solution)/shard_map/all_gather | solution.py:710
Sparse Core Ops, SparseCore 0:
  260.4 167.8 all-gather.6
  430.6 130.3 all-gather.8
  563.3 175.0 all-gather.4
  740.4 118.5 all-gather.10

commit v5 on v4

--- a/solution.py
+++ b/solution.py
@@ -89,10 +89,10 @@
 def gelu_grad(x, d):
     x2 = x * x
     t = jnp.tanh(x * (C0 + C1 * x2))
-    return d * ((0.5 + 0.5 * t) + (x * (0.5 * C0 + 1.5 * C1 * x2)) * (1.0 - t * t))
-
-
-def by_rows(fn, rows=128):
+    return d * ((0.5 + 0.5 * t) + ((1.0 - t * t) * x) * (0.5 * C0 + 1.5 * C1 * x2))
+
+
+def by_rows(fn, rows=256):
     @pl.loop(0, TOK // rows)
     def _(i):
         fn(part(i, rows))
@@ -735,24 +735,33 @@
 
 
 def place_blocks(full, shape, where, dst, after, name):
-    rows = 640
-    per, blocks = D // rows, full.shape[1] // D
-
-    def to(n, i):
-        row, col = where(n)
-        return row * per + i, col
+    rows = D // 4
+    blocks = full.shape[1] // D
+    strips = [(n, i) for n in range(blocks) for i in range(D // rows)]
 
     def kernel(src, *refs):
-        refs[-1][...] = src[...]
+        out, buf, load_sem, store_sem = refs[len(dst) + len(after):]
+        loads, stores = [], []
+        for k, (n, i) in enumerate(strips):
+            row, col = where(n)
+            loads.append(pltpu.make_async_copy(src.at[pl.ds(i * rows, rows), pl.ds(n * D, D)], buf.at[k], load_sem.at[k]))
+            stores.append(pltpu.make_async_copy(buf.at[k], out.at[pl.ds(row * D + i * rows, rows), pl.ds(col * D, D)], store_sem.at[k]))
+        for load in loads:
+            load.start()
+        for load, store in zip(loads, stores):
+            load.wait()
+            store.start()
+        for store in stores:
+            store.wait()
 
     return pl.pallas_call(
         kernel,
-        grid=(blocks, per),
         out_shape=jax.ShapeDtypeStruct(shape, F32),
-        in_specs=[pl.BlockSpec((rows, D), lambda n, i: (i, n))] + [ANY] * (len(dst) + len(after)),
-        out_specs=pl.BlockSpec((rows, D), to),
+        in_specs=[ANY] * (1 + len(dst) + len(after)),
+        out_specs=ANY,
+        scratch_shapes=[pltpu.VMEM((len(strips), rows, D), F32)] + [pltpu.SemaphoreType.DMA((len(strips),))] * 2,
         input_output_aliases={1: 0} if dst else {},
-        compiler_params=pltpu.CompilerParams(vmem_limit_bytes=60 << 20),
+        compiler_params=pltpu.CompilerParams(vmem_limit_bytes=VMEM_MOST),
         cost_estimate=pl.CostEstimate(flops=D * D, bytes_accessed=8 * blocks * D * D, transcendentals=0),
         name=name,
     )(full, *dst, *after)

time: 894 us -> 892 us (level)
  transfers between devices with their start and end apart: 4 -> 4, of which waited for: 1 -> 1; matrix products, arithmetic and copies ran while one was open for 0% -> 0% of each run, Pallas kernels for 65% -> 66%
where the time goes in v5:
time: 892 us; the launch traced here: 883 us
  Pallas kernels  849 us (95%)
  waiting for transfers between devices  19.6 us (2%)
  between operations  14.3 us (2%)
    pallas_call x5, Pallas kernels, scatter_sum(): pl.pallas_call(functools.partial(scatter_kernel, groups, n_tiles, len(src...  632 us
    pallas_call x1, Pallas kernels, front(): pl.pallas_call(front_kernel, out_shape=[jax.ShapeDtypeStruct(s, BF16) for...  140 us
    pallas_call x2, Pallas kernels, place_attention(): pl.pallas_call(kernel, grid=(D // rows,), out_shape=[jax.ShapeDtypeStruct...  38.5 us
    pallas_call x3, Pallas kernels, place_blocks(): pl.pallas_call(kernel, out_shape=jax.ShapeDtypeStruct(shape, F32), in_spe...  37.9 us
    all_gather x4, waiting for transfers between devices, gather(): return lax.all_gather(shard, 'data', axis=0, tiled=True)  19.6 us
  transfers between devices with their start and end apart: 4, of which 1 were waited for; matrix products, arithmetic and copies ran while one was open for 0% of the time, Pallas kernels for 66%

profile of v5, /device:TPU:0, one launch (start us, length us, event | category | flops | bytes accessed | tf_op | source)
XLA Modules:
  0.0 883.0 jit_solution(8190443850132772825)
XLA Ops:
  7.2 0.0 all-gather.7.cloned.1.call-start
  7.2 140.2 %front.1 = (bf16[2,1024,1280]{2,1,0:T(8,128)(2,1)}, bf16[2,1024,3840]{2,1,0:T(8,128)(2,1)}, bf16[2,1024,2560]{2,1,0:T(8,128)(2,1)}, bf16[2,1024,1280]{2,1,0:T(8,...) custom-call(bf16[1024,1280]{1,0:T(8,128)(2,1)} %bitcast.5, ...), custom_call_target="tpu_custom_call" | custom-call | tf_op jit(solution)/shard_map/front/pallas_call | solution.py:298
  147.4 111.5 %scatter_sum_1.1 = (f32[80,5120]{1,0:T(8,128)}, bf16[1024,1280]{1,0:T(8,128)(2,1)}) custom-call(bf16[2,1024,1280]{2,1,0:T(8,128)(2,1)} %get-tuple-element.36.refs_0_, bf16[1024,1280]{1,0:T(8,128)(2,1)} %get-tuple-element.38.refs_1_.refs_7_, bf16[2,1024,1280]{2,1,0:T(8,128)(2,1)} %get-tuple-element.39.refs_2_, bf16[1024,1280]{1,0:T(8,128)(2,1)} %get-tuple-element.40.refs_3_, ...), custom_call_target="tpu_custom_call" | custom-call | flops 104857600000 | bytes 52428800 | tf_op jit(solution)/shard_map/scatter_sum_1/pallas_call | solution.py:697
  258.9 0.0 all-gather.7.cloned.1.call-update
  258.9 0.0 all-gather.9.cloned.1.call-start
  258.9 132.4 %scatter_sum_2.1 = (f32[80,3840]{1,0:T(8,128)}, bf16[1024,5120]{1,0:T(8,128)(2,1)}, bf16[1024,1280]{1,0:T(8,128)(2,1)}, bf16[1024,1280]{1,0:T(8,128)(2,1)}) custom-call(bf16[2,1024,5120]{2,1,0:T(8,128)(2,1)} %get-tuple-element.37.refs_0_, bf16[1024,1280]{1,0:T(8,128)(2,1)} %get-tuple-element.44.refs_1_.refs_5_, bf16[1024,1280]{1,0:T(8,128)(2,1)} %bitcast.8, ...), custom_call_target="tpu_custom_call" | custom-call | flops 78643200000 | bytes 39321600 | tf_op jit(solution)/shard_map/scatter_sum_2/pallas_call | solution.py:697
  391.3 0.0 all-gather.9.cloned.1.call-update
  391.3 0.0 all-gather.5.cloned.1.call-start
  391.4 158.1 %scatter_sum_3.1 = (f32[80,5120]{1,0:T(8,128)}, bf16[1024,1280]{1,0:T(8,128)(2,1)}) custom-call(bf16[2,1024,1280]{2,1,0:T(8,128)(2,1)} %get-tuple-element.36.refs_0_, bf16[1024,1280]{1,0:T(8,128)(2,1)} %get-tuple-element.48.refs_1_.refs_7_, bf16[2,1024,1280]{2,1,0:T(8,128)(2,1)} %get-tuple-element.39.refs_2_, bf16[1024,1280]{1,0:T(8,128)(2,1)} %get-tuple-element.49.refs_3_, ...), custom_call_target="tpu_custom_call" | custom-call | flops 104857600000 | bytes 52428800 | tf_op jit(solution)/shard_map/scatter_sum_3/pallas_call | solution.py:697
  549.5 0.0 all-gather.5.cloned.1.call-update
  549.6 0.0 all-gather.11.cloned.1.call-start
  549.6 152.3 %scatter_sum_4.1.refs_3_ = f32[80,5120]{1,0:T(8,128)} custom-call(bf16[2,1024,1280]{2,1,0:T(8,128)(2,1)} %get-tuple-element.53.refs_0_, bf16[1024,5120]{1,0:T(8,128)(2,1)} %get-tuple-element.54.refs_1_, bf16[1024,5120]{1,0:T(8,128)(2,1)} %get-tuple-element.55.refs_2_, f32[80,5120]{1,0:T(8,128)} %get-tuple-element.51.refs_3_), custom_call_target="tpu_custom_call" | custom-call | flops 104857600000 | bytes 52428800 | tf_op jit(solution)/shard_map/scatter_sum_4/pallas_call | solution.py:697
  701.9 0.0 all-gather.11.cloned.1.call-update
  701.9 78.0 %scatter_sum_5.1.refs_0_ = f32[2,2,2,2,80,1280]{5,4,3,2,1,0:T(8,128)} custom-call(bf16[2,1024,5120]{2,1,0:T(8,128)(2,1)} %get-tuple-element.37.refs_0_, bf16[1024,1280]{1,0:T(8,128)(2,1)} %get-tuple-element.44.refs_1_.refs_5_, bf16[1024,1280]{1,0:T(8,128)(2,1)} %bitcast.9, f32[80,5120]{1,0:T(8,128)} %scatter_sum_4.1.refs_3_), custom_call_target="tpu_custom_call" | custom-call | flops 26214400000 | bytes 13107200 | tf_op jit(solution)/shard_map/scatter_sum_5/pallas_call | solution.py:697
  779.9 0.0 all-gather.7.cloned.1.call-done.src
  780.0 18.8 %place_attention_1.1 = (f32[2,1280,1280]{2,1,0:T(8,128)}, f32[2,1280,1280]{2,1,0:T(8,128)}, f32[2,1280,1280]{2,1,0:T(8,128)}, f32[2,1280,1280]{2,1,0:T(8,128)}) custom-call(f32[1280,5120]{1,0:T(8,128)} %all-gather.7.cloned.1.call-done.src, f32[2,2,2,2,80,1280]{5,4,3,2,1,0:T(8,128)} %scatter_sum_5.1.refs_0_), custom_call_target="tpu_custom_call" | custom-call | flops 1638400 | bytes 52428800 | tf_op jit(solution)/shard_map/place_attention_1/pallas_call | solution.py:724
  798.8 0.0 all-gather.9.cloned.1.call-done.src
  798.8 14.1 %place_down_0.1.refs_0_ = f32[5120,1280]{1,0:T(8,128)} custom-call(f32[1280,3840]{1,0:T(8,128)} %all-gather.9.cloned.1.call-done.src, f32[2,1280,1280]{2,1,0:T(8,128)} %get-tuple-element.56.refs_0_.refs_1_), custom_call_target="tpu_custom_call" | custom-call | flops 1638400 | bytes 39321600 | tf_op jit(solution)/shard_map/place_down_0/pallas_call | solution.py:757
  812.9 5.4 place_down_3.1.refs_5_
  818.3 0.0 all-gather.5.cloned.1.call-done.src
  818.3 19.7 %place_attention_0.1 = (f32[2,1280,1280]{2,1,0:T(8,128)}, f32[2,1280,1280]{2,1,0:T(8,128)}, f32[2,1280,1280]{2,1,0:T(8,128)}, f32[2,1280,1280]{2,1,0:T(8,128)}, bf16[1024,1280]{1,0:T(8,128)(2,1)}) custom-call(f32[1280,5120]{1,0:T(8,128)} %all-gather.5.cloned.1.call-done.src, ...), custom_call_target="tpu_custom_call", output_to_operand_aliasing={{0}: (2, {}), {1}: (3, {}), {2}: (4, {}), {3}: (5, {})} | custom-call | flops 1638400 | bytes 52428800 | tf_op jit(solution)/shard_map/place_attention_0/pallas_call | solution.py:724
  838.1 19.5 %all-gather.11.cloned.1.call-done.src = f32[1280,5120]{1,0:T(8,128)} async-done(((f32[80,5120]{1,0:T(8,128)}), f32[1280,5120]{1,0:T(8,128)}) %all-gather.11.cloned.1.call-update) | async-done | bytes 26214416 | tf_op jit(solution)/shard_map/all_gather | solution.py:710
  857.6 18.4 %place_up.1 = f32[1280,5120]{1,0:T(8,128)} custom-call(f32[1280,5120]{1,0:T(8,128)} %all-gather.11.cloned.1.call-done.src, f32[2,1280,1280]{2,1,0:T(8,128)} %get-tuple-element.29.refs_0_), custom_call_target="tpu_custom_call" | custom-call | flops 1638400 | bytes 52428800 | tf_op jit(solution)/shard_map/place_up/pallas_call | solution.py:757
Async XLA Ops:
  7.2 772.8 %all-gather.7.cloned.1.call-start = ((), (), s32[]{:S(2)}) async-start(), calls=%async_computation.1 | async-start | bytes 27852800 | tf_op jit(solution)/shard_map/all_gather | solution.py:710
  258.9 539.9 %all-gather.9.cloned.1.call-start = ((), (), s32[]{:S(2)}) async-start(), calls=%async_computation.2 | async-start | bytes 20889600 | tf_op jit(solution)/shard_map/all_gather | solution.py:710
  391.3 427.0 %all-gather.5.cloned.1.call-start = ((), (), s32[]{:S(2)}) async-start(), calls=%async_computation | async-start | bytes 27852800 | tf_op jit(solution)/shard_map/all_gather | solution.py:710
  549.6 308.0 %all-gather.11.cloned.1.call-start = ((), (), s32[]{:S(2)}) async-start(), calls=%async_computation.3 | async-start | bytes 27852800 | tf_op jit(solution)/shard_map/all_gather | solution.py:710
Sparse Core Ops, SparseCore 0:
  259.0 167.8 all-gather.6
  429.1 130.5 all-gather.8
  562.0 174.9 all-gather.4
  739.1 118.4 all-gather.10

commit v6 on v5

--- a/solution.py
+++ b/solution.py
@@ -13,6 +13,7 @@
 NB = 256
 DB, FB = D // NB, FF // NB
 PAIRS = 10
+GROUP = 4
 VMEM_MOST = 67043328
 SUBS = [pl.ds(j * NB, NB) for j in range(DB)]
 ANY = pl.BlockSpec(memory_space=pl.ANY)
@@ -147,8 +148,10 @@
 def attention_fwd(qkv, pt, mixed):
     mask = lane_mask()
 
-    def one(rows):
-        for h in range(PAIRS):
+    def one(block):
+        for u in range(GROUP * PAIRS):
+            h = u // GROUP
+            rows = pl.ds(pl.multiple_of(block.start + (u % GROUP) * SEQ, SEQ), SEQ)
             q, k, v = (qkv[rows, pl.ds(n * D + h * SEQ, SEQ)] for n in range(3))
             st = nn(k, split_heads_t(q)) * 0.125
             e = jnp.exp(st - jnp.max(st, axis=0, keepdims=True))
@@ -156,7 +159,7 @@
             pt[rows, pl.ds(h * NB, NB)] = p
             o = tn(p, v)
             mixed[rows, pl.ds(h * SEQ, SEQ)] = jnp.where(mask, o[:SEQ], o[SEQ:]).astype(BF16)
-    by_rows(one, SEQ)
+    by_rows(one, GROUP * SEQ)
 
 
 def attention_bwd(s, duo, qkv, pt, dmixed):

time: 892 us -> 889 us (level)
  no operation moved by 1% of the time
where the time goes in v6:
time: 889 us; the launch traced here: 878 us
  Pallas kernels  844 us (95%)
  waiting for transfers between devices  19.7 us (2%)
  between operations  14.2 us (2%)
    pallas_call x5, Pallas kernels, scatter_sum(): pl.pallas_call(functools.partial(scatter_kernel, groups, n_tiles, len(src...  632 us
    pallas_call x1, Pallas kernels, front(): pl.pallas_call(front_kernel, out_shape=[jax.ShapeDtypeStruct(s, BF16) for...  136 us
    pallas_call x2, Pallas kernels, place_attention(): pl.pallas_call(kernel, grid=(D // rows,), out_shape=[jax.ShapeDtypeStruct...  38.5 us
    pallas_call x3, Pallas kernels, place_blocks(): pl.pallas_call(kernel, out_shape=jax.ShapeDtypeStruct(shape, F32), in_spe...  37.9 us
    all_gather x4, waiting for transfers between devices, gather(): return lax.all_gather(shard, 'data', axis=0, tiled=True)  19.6 us
  transfers between devices with their start and end apart: 4, of which 1 were waited for; matrix products, arithmetic and copies ran while one was open for 0% of the time, Pallas kernels for 66%

profile of v6, /device:TPU:0, one launch (start us, length us, event | category | flops | bytes accessed | tf_op | source)
XLA Modules:
  0.0 878.4 jit_solution(9043544945200226920)
XLA Ops:
  7.2 0.0 all-gather.7.cloned.1.call-start
  7.2 135.6 %front.1 = (bf16[2,1024,1280]{2,1,0:T(8,128)(2,1)}, bf16[2,1024,3840]{2,1,0:T(8,128)(2,1)}, bf16[2,1024,2560]{2,1,0:T(8,128)(2,1)}, bf16[2,1024,1280]{2,1,0:T(8,...) custom-call(bf16[1024,1280]{1,0:T(8,128)(2,1)} %bitcast.5, ...), custom_call_target="tpu_custom_call" | custom-call | tf_op jit(solution)/shard_map/front/pallas_call | solution.py:301
  142.9 111.5 %scatter_sum_1.1 = (f32[80,5120]{1,0:T(8,128)}, bf16[1024,1280]{1,0:T(8,128)(2,1)}) custom-call(bf16[2,1024,1280]{2,1,0:T(8,128)(2,1)} %get-tuple-element.36.refs_0_, bf16[1024,1280]{1,0:T(8,128)(2,1)} %get-tuple-element.38.refs_1_.refs_7_, bf16[2,1024,1280]{2,1,0:T(8,128)(2,1)} %get-tuple-element.39.refs_2_, bf16[1024,1280]{1,0:T(8,128)(2,1)} %get-tuple-element.40.refs_3_, ...), custom_call_target="tpu_custom_call" | custom-call | flops 104857600000 | bytes 52428800 | tf_op jit(solution)/shard_map/scatter_sum_1/pallas_call | solution.py:700
  254.3 0.0 all-gather.7.cloned.1.call-update
  254.3 0.0 all-gather.9.cloned.1.call-start
  254.4 132.4 %scatter_sum_2.1 = (f32[80,3840]{1,0:T(8,128)}, bf16[1024,5120]{1,0:T(8,128)(2,1)}, bf16[1024,1280]{1,0:T(8,128)(2,1)}, bf16[1024,1280]{1,0:T(8,128)(2,1)}) custom-call(bf16[2,1024,5120]{2,1,0:T(8,128)(2,1)} %get-tuple-element.37.refs_0_, bf16[1024,1280]{1,0:T(8,128)(2,1)} %get-tuple-element.44.refs_1_.refs_5_, bf16[1024,1280]{1,0:T(8,128)(2,1)} %bitcast.8, ...), custom_call_target="tpu_custom_call" | custom-call | flops 78643200000 | bytes 39321600 | tf_op jit(solution)/shard_map/scatter_sum_2/pallas_call | solution.py:700
  386.8 0.0 all-gather.9.cloned.1.call-update
  386.8 0.0 all-gather.5.cloned.1.call-start
  386.8 158.2 %scatter_sum_3.1 = (f32[80,5120]{1,0:T(8,128)}, bf16[1024,1280]{1,0:T(8,128)(2,1)}) custom-call(bf16[2,1024,1280]{2,1,0:T(8,128)(2,1)} %get-tuple-element.36.refs_0_, bf16[1024,1280]{1,0:T(8,128)(2,1)} %get-tuple-element.48.refs_1_.refs_7_, bf16[2,1024,1280]{2,1,0:T(8,128)(2,1)} %get-tuple-element.39.refs_2_, bf16[1024,1280]{1,0:T(8,128)(2,1)} %get-tuple-element.49.refs_3_, ...), custom_call_target="tpu_custom_call" | custom-call | flops 104857600000 | bytes 52428800 | tf_op jit(solution)/shard_map/scatter_sum_3/pallas_call | solution.py:700
  545.0 0.0 all-gather.5.cloned.1.call-update
  545.1 0.0 all-gather.11.cloned.1.call-start
  545.1 152.3 %scatter_sum_4.1.refs_3_ = f32[80,5120]{1,0:T(8,128)} custom-call(bf16[2,1024,1280]{2,1,0:T(8,128)(2,1)} %get-tuple-element.53.refs_0_, bf16[1024,5120]{1,0:T(8,128)(2,1)} %get-tuple-element.54.refs_1_, bf16[1024,5120]{1,0:T(8,128)(2,1)} %get-tuple-element.55.refs_2_, f32[80,5120]{1,0:T(8,128)} %get-tuple-element.51.refs_3_), custom_call_target="tpu_custom_call" | custom-call | flops 104857600000 | bytes 52428800 | tf_op jit(solution)/shard_map/scatter_sum_4/pallas_call | solution.py:700
  697.4 0.0 all-gather.11.cloned.1.call-update
  697.4 78.0 %scatter_sum_5.1.refs_0_ = f32[2,2,2,2,80,1280]{5,4,3,2,1,0:T(8,128)} custom-call(bf16[2,1024,5120]{2,1,0:T(8,128)(2,1)} %get-tuple-element.37.refs_0_, bf16[1024,1280]{1,0:T(8,128)(2,1)} %get-tuple-element.44.refs_1_.refs_5_, bf16[1024,1280]{1,0:T(8,128)(2,1)} %bitcast.9, f32[80,5120]{1,0:T(8,128)} %scatter_sum_4.1.refs_3_), custom_call_target="tpu_custom_call" | custom-call | flops 26214400000 | bytes 13107200 | tf_op jit(solution)/shard_map/scatter_sum_5/pallas_call | solution.py:700
  775.4 0.0 all-gather.7.cloned.1.call-done.src
  775.4 18.8 %place_attention_1.1 = (f32[2,1280,1280]{2,1,0:T(8,128)}, f32[2,1280,1280]{2,1,0:T(8,128)}, f32[2,1280,1280]{2,1,0:T(8,128)}, f32[2,1280,1280]{2,1,0:T(8,128)}) custom-call(f32[1280,5120]{1,0:T(8,128)} %all-gather.7.cloned.1.call-done.src, f32[2,2,2,2,80,1280]{5,4,3,2,1,0:T(8,128)} %scatter_sum_5.1.refs_0_), custom_call_target="tpu_custom_call" | custom-call | flops 1638400 | bytes 52428800 | tf_op jit(solution)/shard_map/place_attention_1/pallas_call | solution.py:727
  794.2 0.0 all-gather.9.cloned.1.call-done.src
  794.2 14.1 %place_down_0.1.refs_0_ = f32[5120,1280]{1,0:T(8,128)} custom-call(f32[1280,3840]{1,0:T(8,128)} %all-gather.9.cloned.1.call-done.src, f32[2,1280,1280]{2,1,0:T(8,128)} %get-tuple-element.56.refs_0_.refs_1_), custom_call_target="tpu_custom_call" | custom-call | flops 1638400 | bytes 39321600 | tf_op jit(solution)/shard_map/place_down_0/pallas_call | solution.py:760
  808.3 5.4 place_down_3.1.refs_5_
  813.7 0.0 all-gather.5.cloned.1.call-done.src
  813.7 19.7 %place_attention_0.1 = (f32[2,1280,1280]{2,1,0:T(8,128)}, f32[2,1280,1280]{2,1,0:T(8,128)}, f32[2,1280,1280]{2,1,0:T(8,128)}, f32[2,1280,1280]{2,1,0:T(8,128)}, bf16[1024,1280]{1,0:T(8,128)(2,1)}) custom-call(f32[1280,5120]{1,0:T(8,128)} %all-gather.5.cloned.1.call-done.src, ...), custom_call_target="tpu_custom_call", output_to_operand_aliasing={{0}: (2, {}), {1}: (3, {}), {2}: (4, {}), {3}: (5, {})} | custom-call | flops 1638400 | bytes 52428800 | tf_op jit(solution)/shard_map/place_attention_0/pallas_call | solution.py:727
  833.5 19.5 %all-gather.11.cloned.1.call-done.src = f32[1280,5120]{1,0:T(8,128)} async-done(((f32[80,5120]{1,0:T(8,128)}), f32[1280,5120]{1,0:T(8,128)}) %all-gather.11.cloned.1.call-update) | async-done | bytes 26214416 | tf_op jit(solution)/shard_map/all_gather | solution.py:713
  853.0 18.4 %place_up.1 = f32[1280,5120]{1,0:T(8,128)} custom-call(f32[1280,5120]{1,0:T(8,128)} %all-gather.11.cloned.1.call-done.src, f32[2,1280,1280]{2,1,0:T(8,128)} %get-tuple-element.29.refs_0_), custom_call_target="tpu_custom_call" | custom-call | flops 1638400 | bytes 52428800 | tf_op jit(solution)/shard_map/place_up/pallas_call | solution.py:760
Async XLA Ops:
  7.2 768.2 %all-gather.7.cloned.1.call-start = ((), (), s32[]{:S(2)}) async-start(), calls=%async_computation.1 | async-start | bytes 27852800 | tf_op jit(solution)/shard_map/all_gather | solution.py:713
  254.3 539.8 %all-gather.9.cloned.1.call-start = ((), (), s32[]{:S(2)}) async-start(), calls=%async_computation.2 | async-start | bytes 20889600 | tf_op jit(solution)/shard_map/all_gather | solution.py:713
  386.8 426.9 %all-gather.5.cloned.1.call-start = ((), (), s32[]{:S(2)}) async-start(), calls=%async_computation | async-start | bytes 27852800 | tf_op jit(solution)/shard_map/all_gather | solution.py:713
  545.1 308.0 %all-gather.11.cloned.1.call-start = ((), (), s32[]{:S(2)}) async-start(), calls=%async_computation.3 | async-start | bytes 27852800 | tf_op jit(solution)/shard_map/all_gather | solution.py:713
Sparse Core Ops, SparseCore 0:
  254.5 167.8 all-gather.6
  424.6 130.4 all-gather.8
  557.3 175.0 all-gather.4
  734.5 118.5 all-gather.10

commit v7 on v6

--- a/solution.py
+++ b/solution.py
@@ -13,7 +13,7 @@
 NB = 256
 DB, FB = D // NB, FF // NB
 PAIRS = 10
-GROUP = 4
+GROUP = 8
 VMEM_MOST = 67043328
 SUBS = [pl.ds(j * NB, NB) for j in range(DB)]
 ANY = pl.BlockSpec(memory_space=pl.ANY)

time: 889 us -> 889 us (level)
  no operation moved by 1% of the time
where the time goes in v7:
time: 889 us; the launch traced here: 878 us
  Pallas kernels  844 us (95%)
  waiting for transfers between devices  19.7 us (2%)
  between operations  14.2 us (2%)
    pallas_call x5, Pallas kernels, scatter_sum(): pl.pallas_call(functools.partial(scatter_kernel, groups, n_tiles, len(src...  632 us
    pallas_call x1, Pallas kernels, front(): pl.pallas_call(front_kernel, out_shape=[jax.ShapeDtypeStruct(s, BF16) for...  135 us
    pallas_call x2, Pallas kernels, place_attention(): pl.pallas_call(kernel, grid=(D // rows,), out_shape=[jax.ShapeDtypeStruct...  38.5 us
    pallas_call x3, Pallas kernels, place_blocks(): pl.pallas_call(kernel, out_shape=jax.ShapeDtypeStruct(shape, F32), in_spe...  37.9 us
    all_gather x4, waiting for transfers between devices, gather(): return lax.all_gather(shard, 'data', axis=0, tiled=True)  19.6 us
  transfers between devices with their start and end apart: 4, of which 1 were waited for; matrix products, arithmetic and copies ran while one was open for 0% of the time, Pallas kernels for 66%

profile of v7, /device:TPU:0, one launch (start us, length us, event | category | flops | bytes accessed | tf_op | source)
XLA Modules:
  0.0 877.6 jit_solution(4754077099029403215)
XLA Ops:
  7.2 0.0 all-gather.7.cloned.1.call-start
  7.2 134.9 %front.1 = (bf16[2,1024,1280]{2,1,0:T(8,128)(2,1)}, bf16[2,1024,3840]{2,1,0:T(8,128)(2,1)}, bf16[2,1024,2560]{2,1,0:T(8,128)(2,1)}, bf16[2,1024,1280]{2,1,0:T(8,...) custom-call(bf16[1024,1280]{1,0:T(8,128)(2,1)} %bitcast.5, ...), custom_call_target="tpu_custom_call" | custom-call | tf_op jit(solution)/shard_map/front/pallas_call | solution.py:301
  142.1 111.5 %scatter_sum_1.1 = (f32[80,5120]{1,0:T(8,128)}, bf16[1024,1280]{1,0:T(8,128)(2,1)}) custom-call(bf16[2,1024,1280]{2,1,0:T(8,128)(2,1)} %get-tuple-element.36.refs_0_, bf16[1024,1280]{1,0:T(8,128)(2,1)} %get-tuple-element.38.refs_1_.refs_7_, bf16[2,1024,1280]{2,1,0:T(8,128)(2,1)} %get-tuple-element.39.refs_2_, bf16[1024,1280]{1,0:T(8,128)(2,1)} %get-tuple-element.40.refs_3_, ...), custom_call_target="tpu_custom_call" | custom-call | flops 104857600000 | bytes 52428800 | tf_op jit(solution)/shard_map/scatter_sum_1/pallas_call | solution.py:700
  253.6 0.0 all-gather.7.cloned.1.call-update
  253.6 0.0 all-gather.9.cloned.1.call-start
  253.6 132.4 %scatter_sum_2.1 = (f32[80,3840]{1,0:T(8,128)}, bf16[1024,5120]{1,0:T(8,128)(2,1)}, bf16[1024,1280]{1,0:T(8,128)(2,1)}, bf16[1024,1280]{1,0:T(8,128)(2,1)}) custom-call(bf16[2,1024,5120]{2,1,0:T(8,128)(2,1)} %get-tuple-element.37.refs_0_, bf16[1024,1280]{1,0:T(8,128)(2,1)} %get-tuple-element.44.refs_1_.refs_5_, bf16[1024,1280]{1,0:T(8,128)(2,1)} %bitcast.8, ...), custom_call_target="tpu_custom_call" | custom-call | flops 78643200000 | bytes 39321600 | tf_op jit(solution)/shard_map/scatter_sum_2/pallas_call | solution.py:700
  386.0 0.0 all-gather.9.cloned.1.call-update
  386.0 0.0 all-gather.5.cloned.1.call-start
  386.1 158.2 %scatter_sum_3.1 = (f32[80,5120]{1,0:T(8,128)}, bf16[1024,1280]{1,0:T(8,128)(2,1)}) custom-call(bf16[2,1024,1280]{2,1,0:T(8,128)(2,1)} %get-tuple-element.36.refs_0_, bf16[1024,1280]{1,0:T(8,128)(2,1)} %get-tuple-element.48.refs_1_.refs_7_, bf16[2,1024,1280]{2,1,0:T(8,128)(2,1)} %get-tuple-element.39.refs_2_, bf16[1024,1280]{1,0:T(8,128)(2,1)} %get-tuple-element.49.refs_3_, ...), custom_call_target="tpu_custom_call" | custom-call | flops 104857600000 | bytes 52428800 | tf_op jit(solution)/shard_map/scatter_sum_3/pallas_call | solution.py:700
  544.3 0.0 all-gather.5.cloned.1.call-update
  544.3 0.0 all-gather.11.cloned.1.call-start
  544.3 152.3 %scatter_sum_4.1.refs_3_ = f32[80,5120]{1,0:T(8,128)} custom-call(bf16[2,1024,1280]{2,1,0:T(8,128)(2,1)} %get-tuple-element.53.refs_0_, bf16[1024,5120]{1,0:T(8,128)(2,1)} %get-tuple-element.54.refs_1_, bf16[1024,5120]{1,0:T(8,128)(2,1)} %get-tuple-element.55.refs_2_, f32[80,5120]{1,0:T(8,128)} %get-tuple-element.51.refs_3_), custom_call_target="tpu_custom_call" | custom-call | flops 104857600000 | bytes 52428800 | tf_op jit(solution)/shard_map/scatter_sum_4/pallas_call | solution.py:700
  696.6 0.0 all-gather.11.cloned.1.call-update
  696.6 78.0 %scatter_sum_5.1.refs_0_ = f32[2,2,2,2,80,1280]{5,4,3,2,1,0:T(8,128)} custom-call(bf16[2,1024,5120]{2,1,0:T(8,128)(2,1)} %get-tuple-element.37.refs_0_, bf16[1024,1280]{1,0:T(8,128)(2,1)} %get-tuple-element.44.refs_1_.refs_5_, bf16[1024,1280]{1,0:T(8,128)(2,1)} %bitcast.9, f32[80,5120]{1,0:T(8,128)} %scatter_sum_4.1.refs_3_), custom_call_target="tpu_custom_call" | custom-call | flops 26214400000 | bytes 13107200 | tf_op jit(solution)/shard_map/scatter_sum_5/pallas_call | solution.py:700
  774.6 0.0 all-gather.7.cloned.1.call-done.src
  774.6 18.8 %place_attention_1.1 = (f32[2,1280,1280]{2,1,0:T(8,128)}, f32[2,1280,1280]{2,1,0:T(8,128)}, f32[2,1280,1280]{2,1,0:T(8,128)}, f32[2,1280,1280]{2,1,0:T(8,128)}) custom-call(f32[1280,5120]{1,0:T(8,128)} %all-gather.7.cloned.1.call-done.src, f32[2,2,2,2,80,1280]{5,4,3,2,1,0:T(8,128)} %scatter_sum_5.1.refs_0_), custom_call_target="tpu_custom_call" | custom-call | flops 1638400 | bytes 52428800 | tf_op jit(solution)/shard_map/place_attention_1/pallas_call | solution.py:727
  793.4 0.0 all-gather.9.cloned.1.call-done.src
  793.4 14.1 %place_down_0.1.refs_0_ = f32[5120,1280]{1,0:T(8,128)} custom-call(f32[1280,3840]{1,0:T(8,128)} %all-gather.9.cloned.1.call-done.src, f32[2,1280,1280]{2,1,0:T(8,128)} %get-tuple-element.56.refs_0_.refs_1_), custom_call_target="tpu_custom_call" | custom-call | flops 1638400 | bytes 39321600 | tf_op jit(solution)/shard_map/place_down_0/pallas_call | solution.py:760
  807.5 5.4 place_down_3.1.refs_5_
  812.9 0.0 all-gather.5.cloned.1.call-done.src
  813.0 19.7 %place_attention_0.1 = (f32[2,1280,1280]{2,1,0:T(8,128)}, f32[2,1280,1280]{2,1,0:T(8,128)}, f32[2,1280,1280]{2,1,0:T(8,128)}, f32[2,1280,1280]{2,1,0:T(8,128)}, bf16[1024,1280]{1,0:T(8,128)(2,1)}) custom-call(f32[1280,5120]{1,0:T(8,128)} %all-gather.5.cloned.1.call-done.src, ...), custom_call_target="tpu_custom_call", output_to_operand_aliasing={{0}: (2, {}), {1}: (3, {}), {2}: (4, {}), {3}: (5, {})} | custom-call | flops 1638400 | bytes 52428800 | tf_op jit(solution)/shard_map/place_attention_0/pallas_call | solution.py:727
  832.7 19.5 %all-gather.11.cloned.1.call-done.src = f32[1280,5120]{1,0:T(8,128)} async-done(((f32[80,5120]{1,0:T(8,128)}), f32[1280,5120]{1,0:T(8,128)}) %all-gather.11.cloned.1.call-update) | async-done | bytes 26214416 | tf_op jit(solution)/shard_map/all_gather | solution.py:713
  852.3 18.4 %place_up.1 = f32[1280,5120]{1,0:T(8,128)} custom-call(f32[1280,5120]{1,0:T(8,128)} %all-gather.11.cloned.1.call-done.src, f32[2,1280,1280]{2,1,0:T(8,128)} %get-tuple-element.29.refs_0_), custom_call_target="tpu_custom_call" | custom-call | flops 1638400 | bytes 52428800 | tf_op jit(solution)/shard_map/place_up/pallas_call | solution.py:760
Async XLA Ops:
  7.2 767.5 %all-gather.7.cloned.1.call-start = ((), (), s32[]{:S(2)}) async-start(), calls=%async_computation.1 | async-start | bytes 27852800 | tf_op jit(solution)/shard_map/all_gather | solution.py:713
  253.6 539.8 %all-gather.9.cloned.1.call-start = ((), (), s32[]{:S(2)}) async-start(), calls=%async_computation.2 | async-start | bytes 20889600 | tf_op jit(solution)/shard_map/all_gather | solution.py:713
  386.0 426.9 %all-gather.5.cloned.1.call-start = ((), (), s32[]{:S(2)}) async-start(), calls=%async_computation | async-start | bytes 27852800 | tf_op jit(solution)/shard_map/all_gather | solution.py:713
  544.3 308.0 %all-gather.11.cloned.1.call-start = ((), (), s32[]{:S(2)}) async-start(), calls=%async_computation.3 | async-start | bytes 27852800 | tf_op jit(solution)/shard_map/all_gather | solution.py:713
Sparse Core Ops, SparseCore 0:
  253.7 167.8 all-gather.6
  423.8 130.4 all-gather.8
  556.5 175.0 all-gather.4
  733.7 118.5 all-gather.10
